TPU v7x, 8 devices: a whole 2x2x1 slice. The times are simulated.
8 devices in a mesh: dp: 4 (over z, y, x), tp: 2 (over core).
Axes of the slice: x: 2, y: 2, z: 1, core: 2. Of those that a mesh axis runs over, the one named last changes fastest.
Arguments:
- block_in: bfloat16 [3, 8, 2048, 1408], P(None, 'dp')
- pre_act: bfloat16 [3, 8, 2048, 6144], P(None, 'dp', None, 'tp')
- w_in: bfloat16 [3, 1408, 6144], P(None, None, 'tp')
- w_out: bfloat16 [3, 6144, 1408], P(None, 'tp')
- d_out: bfloat16 [8, 2048, 1408], P('dp')
- noise_in: float32 [3, 1408, 6144], P(None, None, 'tp')
- noise_out: float32 [3, 6144, 1408], P(None, 'tp')
- clip_norm: float32 [], replicated
- noise_mult: float32 [], replicated
Outputs:
- output 1: float32 [3, 1408, 6144], P(None, None, 'tp')
- output 2: float32 [3, 6144, 1408], P(None, 'tp')
All inputs are finite; a program needn't handle non-finite values.
Results may differ from a plain program's by a relative error of at most 0.00950181.
Values are sent between devices in bfloat16 or wider.
A program may use at most 1.5 GiB of HBM per device.

v0:
```python
import jax
import jax.numpy as jnp
from jax import lax
from jax.sharding import PartitionSpec as P

INV_SQRT2 = 0.7071067811865476
INV_SQRT_2PI = 0.3989422804014327


def gelu_parts(u_vals):
    u_wide = u_vals.astype(jnp.float32)
    norm_cdf = 0.5 * (1.0 + lax.erf(u_wide * INV_SQRT2))
    hidden = (u_wide * norm_cdf).astype(jnp.bfloat16)
    gelu_slope = norm_cdf + u_wide * jnp.exp(-0.5 * u_wide * u_wide) * INV_SQRT_2PI
    return hidden, gelu_slope


def solution(mesh):
    data_size = mesh.shape['dp']

    def local_run(block_in, pre_act, w_in, w_out, d_out, noise_in, noise_out, clip_norm, noise_mult):
        n_layers = block_in.shape[0]
        local_batch = block_in.shape[1]
        batch_total = local_batch * data_size
        d_z = d_out
        saved = [None] * n_layers
        part_sq = jnp.zeros((local_batch,), jnp.float32)
        for layer_idx in range(n_layers - 1, -1, -1):
            hidden, gelu_slope = gelu_parts(pre_act[layer_idx])
            back_h = jnp.einsum('btd,fd->btf', d_z, w_out[layer_idx], preferred_element_type=jnp.float32)
            d_hid = (gelu_slope * back_h).astype(jnp.bfloat16)
            x_layer = block_in[layer_idx]
            gram_h = jnp.einsum('btf,bsf->bts', hidden, hidden, preferred_element_type=jnp.float32)
            gram_z = jnp.einsum('btd,bsd->bts', d_z, d_z, preferred_element_type=jnp.float32)
            gram_x = jnp.einsum('btd,bsd->bts', x_layer, x_layer, preferred_element_type=jnp.float32)
            gram_d = jnp.einsum('btf,bsf->bts', d_hid, d_hid, preferred_element_type=jnp.float32)
            part_sq = part_sq + jnp.sum(gram_h * gram_z + gram_x * gram_d, axis=(1, 2))
            saved[layer_idx] = (hidden, d_hid, d_z)
            if layer_idx > 0:
                part_dx = jnp.einsum('btf,df->btd', d_hid, w_in[layer_idx], preferred_element_type=jnp.float32).astype(jnp.bfloat16)
                summed_dx = lax.psum(part_dx, 'tp')
                d_z = (d_z.astype(jnp.float32) + summed_dx.astype(jnp.float32)).astype(jnp.bfloat16)
        sq_norm = lax.psum(part_sq, 'tp')
        clip_factor = jnp.minimum(1.0, clip_norm / jnp.sqrt(sq_norm))
        scale_rows = clip_factor[:, None, None]
        grads_in = []
        grads_out = []
        for layer_idx in range(n_layers):
            hidden, d_hid, d_z_layer = saved[layer_idx]
            d_hid_c = (d_hid * scale_rows).astype(jnp.bfloat16)
            d_z_c = (d_z_layer * scale_rows).astype(jnp.bfloat16)
            grads_in.append(jnp.einsum('btd,btf->df', block_in[layer_idx], d_hid_c, preferred_element_type=jnp.float32))
            grads_out.append(jnp.einsum('btf,btd->fd', hidden, d_z_c, preferred_element_type=jnp.float32))
        sum_in, sum_out = lax.psum((jnp.stack(grads_in), jnp.stack(grads_out)), 'dp')
        noise_coef = noise_mult * clip_norm
        grad_in = (sum_in + noise_coef * noise_in) / batch_total
        grad_out = (sum_out + noise_coef * noise_out) / batch_total
        return grad_in, grad_out

    return jax.shard_map(
        local_run,
        mesh=mesh,
        in_specs=(P(None, 'dp', None, None), P(None, 'dp', None, 'tp'), P(None, None, 'tp'), P(None, 'tp', None),
                  P('dp', None, None), P(None, None, 'tp'), P(None, 'tp', None), P(), P()),
        out_specs=(P(None, None, 'tp'), P(None, 'tp', None)),
        check_vma=False,
    )
```

profile of v0, /device:TPU:0, one launch (start us, length us, event | category | flops | bytes accessed | tf_op | source)
XLA Modules:
  0.0 3315.1 jit_solution(16626854565292011769)
XLA Ops:
  7.2 0.0 all-reduce.5.cloned.1.call-start
  7.2 72.1 %fusion.20 = (f32[2,2048,3072]{2,1,0:T(8,128)}, f32[2,2048,3072]{2,1,0:T(8,128)}, f32[2,2048,3072]{2,1,0:T(8,128)}) fusion(bf16[3,2,2048,3072]{3,2,1,0:T(8,128)(2,1)} %param.10), kind=kLoop, calls=%fused_computation.39 | loop fusion | flops 150994944 | bytes 226492416 | tf_op jit(solution)/shard_map/mul | solution.py:12
  79.3 64.4 %fusion.16 = bf16[2,2048,3072]{2,1,0:T(8,128)(2,1)} fusion(f32[2,2048,3072]{2,1,0:T(8,128)} %get-tuple-element.8, bf16[2,2048,1408]{2,1,0:T(8,128)(2,1)} %param.13, bf16[3,2,2048,3072]{3,2,1,0:T(8,128)(2,1)} %param.10, bf16[3,3072,1408]{2,1,0:T(8,128)(2,1)} %param.12), kind=kOutput, calls=%fused_computation.35 | convolution fusion | flops 35534143488 | bytes 120848384 | tf_op jit(solution)/shard_map/btd,fd->btf/dot_general | solution.py:30
  143.7 47.0 %convolution_convert_fusion.1 = bf16[2,2048,1408]{2,1,0:T(8,128)(2,1)} fusion(bf16[2,2048,3072]{2,1,0:T(8,128)(2,1)} %fusion.16, bf16[3,1408,3072]{2,1,0:T(8,128)(2,1)} %param.11), kind=kOutput, calls=%fused_computation.83 | convolution fusion | flops 35439247360 | bytes 45350912 | tf_op jit(solution)/shard_map/btf,df->btd/dot_general | solution.py:40
  190.6 0.0 all-reduce.5.cloned.1.call-update
  190.7 0.0 all-reduce.7.cloned.1.call-start
  190.7 89.1 %fusion.75 = f32[2,2048,2048]{2,1,0:T(8,128)} fusion(f32[2,2048,3072]{2,1,0:T(8,128)} %get-tuple-element.8, bf16[3,2,2048,3072]{3,2,1,0:T(8,128)(2,1)} %param.10), kind=kOutput, calls=%fused_computation.104 | convolution fusion | flops 51577356288 | bytes 109051904 | tf_op jit(solution)/shard_map/btf,bsf->bts/dot_general | solution.py:33
  279.8 88.8 %fusion.78 = f32[2,2048,2048]{2,1,0:T(8,128)} fusion(f32[2,2048,3072]{2,1,0:T(8,128)} %get-tuple-element.7, bf16[3,2,2048,3072]{3,2,1,0:T(8,128)(2,1)} %param.10), kind=kOutput, calls=%fused_computation.105 | convolution fusion | flops 51577356288 | bytes 109051904 | tf_op jit(solution)/shard_map/btf,bsf->bts/dot_general | solution.py:33
  368.6 88.7 %fusion.72 = f32[2,2048,2048]{2,1,0:T(8,128)} fusion(f32[2,2048,3072]{2,1,0:T(8,128)} %get-tuple-element.6, bf16[3,2,2048,3072]{3,2,1,0:T(8,128)(2,1)} %param.10), kind=kOutput, calls=%fused_computation.103 | convolution fusion | flops 51577356288 | bytes 109051904 | tf_op jit(solution)/shard_map/btf,bsf->bts/dot_general | solution.py:33
  457.3 62.5 %fusion.81 = f32[2,2048,2048]{2,1,0:T(8,128)} fusion(bf16[2,2048,3072]{2,1,0:T(8,128)(2,1)} %fusion.16), kind=kOutput, calls=%fused_computation.107 | convolution fusion | flops 51539607552 | bytes 58720256 | tf_op jit(solution)/shard_map/btf,bsf->bts/dot_general | solution.py:36
  519.8 34.6 %fusion.80 = f32[2,2048,2048]{2,1,0:T(8,128)} fusion(bf16[2,2048,1408]{2,1,0:T(8,128)(2,1)} %param.13), kind=kOutput, calls=%fused_computation.106 | convolution fusion | flops 23622320128 | bytes 45088768 | tf_op jit(solution)/shard_map/btd,bsd->bts/dot_general | solution.py:34
  554.4 46.1 %add_reduce_fusion.2 = f32[2]{0:T(128)} fusion(f32[2,2048,2048]{2,1,0:T(8,128)} %fusion.81, f32[2,2048,2048]{2,1,0:T(8,128)} %fusion.75, f32[2,2048,2048]{2,1,0:T(8,128)} %fusion.80, bf16[3,2,2048,1408]{3,2,1,0:T(8,128)(2,1)} %param.9), kind=kOutput, calls=%fused_computation.51 | convolution fusion | flops 23655874560 | bytes 112197640 | tf_op jit(solution)/shard_map/btd,bsd->bts/dot_general | solution.py:35
  600.5 0.0 all-reduce.5.cloned.1.call-done
  600.5 13.0 fusion.33
  613.5 64.8 %fusion.25 = bf16[2,2048,3072]{2,1,0:T(8,128)(2,1)} fusion(f32[2,2048,3072]{2,1,0:T(8,128)} %get-tuple-element.6, bf16[2,2048,1408]{2,1,0:T(8,128)(2,1)} %fusion.33, bf16[3,2,2048,3072]{3,2,1,0:T(8,128)(2,1)} %param.10, bf16[3,3072,1408]{2,1,0:T(8,128)(2,1)} %param.12), kind=kOutput, calls=%fused_computation.44 | convolution fusion | flops 35534143488 | bytes 120848384 | tf_op jit(solution)/shard_map/btd,fd->btf/dot_general | solution.py:30
  678.3 46.8 %convolution_convert_fusion = bf16[2,2048,1408]{2,1,0:T(8,128)(2,1)} fusion(bf16[2,2048,3072]{2,1,0:T(8,128)(2,1)} %fusion.25, bf16[3,1408,3072]{2,1,0:T(8,128)(2,1)} %param.11), kind=kOutput, calls=%fused_computation.82 | convolution fusion | flops 35439247360 | bytes 45350912 | tf_op jit(solution)/shard_map/btf,df->btd/dot_general | solution.py:40
  725.2 0.0 all-reduce.7.cloned.1.call-update
  725.2 0.0 all-reduce.9.cloned.1.call-start
  725.2 62.7 %fusion.83 = f32[2,2048,2048]{2,1,0:T(8,128)} fusion(bf16[2,2048,3072]{2,1,0:T(8,128)(2,1)} %fusion.25), kind=kOutput, calls=%fused_computation.109 | convolution fusion | flops 51539607552 | bytes 58720256 | tf_op jit(solution)/shard_map/btf,bsf->bts/dot_general | solution.py:36
  788.0 34.6 %fusion.82 = f32[2,2048,2048]{2,1,0:T(8,128)} fusion(bf16[2,2048,1408]{2,1,0:T(8,128)(2,1)} %fusion.33), kind=kOutput, calls=%fused_computation.108 | convolution fusion | flops 23622320128 | bytes 45088768 | tf_op jit(solution)/shard_map/btd,bsd->bts/dot_general | solution.py:34
  822.5 46.0 %add_reduce_fusion.1 = f32[2]{0:T(128)} fusion(f32[2,2048,2048]{2,1,0:T(8,128)} %fusion.83, f32[2,2048,2048]{2,1,0:T(8,128)} %fusion.72, f32[2,2048,2048]{2,1,0:T(8,128)} %fusion.82, bf16[3,2,2048,1408]{3,2,1,0:T(8,128)(2,1)} %param.9), kind=kOutput, calls=%fused_computation.50 | convolution fusion | flops 23655874560 | bytes 112197640 | tf_op jit(solution)/shard_map/btd,bsd->bts/dot_general | solution.py:35
  868.5 0.0 all-reduce.7.cloned.1.call-done
  868.5 54.8 %fusion.7 = bf16[2,2048,3072]{2,1,0:T(8,128)(2,1)} fusion(f32[2,2048,3072]{2,1,0:T(8,128)} %get-tuple-element.7, bf16[3,2,2048,3072]{3,2,1,0:T(8,128)(2,1)} %param.10, bf16[3,3072,1408]{2,1,0:T(8,128)(2,1)} %param.12, bf16[2,2048,1408]{2,1,0:T(8,128)(2,1)} %fusion.33, bf16[2,2048,1408]{2,1,0:T(8,128)(2,1)} %all-reduce.7.cloned.1.call-done), kind=kOutput, calls=%fused_computation.26 | convolution fusion | flops 35557212160 | bytes 132382720 | tf_op jit(solution)/shard_map/btd,fd->btf/dot_general | solution.py:30
  923.2 62.5 %fusion.84 = f32[2,2048,2048]{2,1,0:T(8,128)} fusion(bf16[2,2048,3072]{2,1,0:T(8,128)(2,1)} %fusion.7), kind=kOutput, calls=%fused_computation.110 | convolution fusion | flops 51539607552 | bytes 58720256 | tf_op jit(solution)/shard_map/btf,bsf->bts/dot_general | solution.py:36
  985.7 43.4 %fusion.68 = f32[2,2048,2048]{2,1,0:T(8,128)} fusion(bf16[2,2048,1408]{2,1,0:T(8,128)(2,1)} %fusion.33, bf16[2,2048,1408]{2,1,0:T(8,128)(2,1)} %all-reduce.7.cloned.1.call-done), kind=kOutput, calls=%fused_computation.102 | convolution fusion | flops 23645388800 | bytes 56623104 | tf_op jit(solution)/shard_map/btd,bsd->bts/dot_general | solution.py:34
  1029.1 0.0 copy-start
  1029.1 0.0 copy-start.1
  1029.1 45.5 %add_reduce_fusion = f32[2]{0:T(128)S(1)} fusion(f32[2,2048,2048]{2,1,0:T(8,128)} %fusion.84, f32[2,2048,2048]{2,1,0:T(8,128)} %fusion.78, f32[2,2048,2048]{2,1,0:T(8,128)} %fusion.68, bf16[3,2,2048,1408]{3,2,1,0:T(8,128)(2,1)} %param.9), kind=kOutput, calls=%fused_computation.49 | convolution fusion | flops 23655874560 | bytes 112197640 | tf_op jit(solution)/shard_map/btd,bsd->bts/dot_general | solution.py:35
  1074.6 0.0 copy-done
  1074.6 0.0 copy-done.1
  1075.2 3.0 psum.37
  1078.3 52.2 %convolution_bitcast_fusion.1 = f32[1,3072,1408]{2,1,0:T(8,128)} fusion(bf16[2,2048,1408]{2,1,0:T(8,128)(2,1)} %fusion.33, f32[2]{0:T(128)S(1)} %multiply_minimum_fusion, f32[2,2048,3072]{2,1,0:T(8,128)} %get-tuple-element.6, bf16[3,2,2048,3072]{3,2,1,0:T(8,128)(2,1)} %param.10), kind=kOutput, calls=%fused_computation.71 | convolution fusion | flops 35488530432 | bytes 104333320 | tf_op jit(solution)/shard_map/btf,btd->fd/dot_general | solution.py:53
  1130.5 52.3 %convolution_bitcast_fusion = f32[1,3072,1408]{2,1,0:T(8,128)} fusion(bf16[2,2048,1408]{2,1,0:T(8,128)(2,1)} %param.13, f32[2]{0:T(128)S(1)} %multiply_minimum_fusion, f32[2,2048,3072]{2,1,0:T(8,128)} %get-tuple-element.8, bf16[3,2,2048,3072]{3,2,1,0:T(8,128)(2,1)} %param.10), kind=kOutput, calls=%fused_computation.70 | convolution fusion | flops 35488530432 | bytes 104333320 | tf_op jit(solution)/shard_map/btf,btd->fd/dot_general | solution.py:53
  1182.8 48.9 %fusion.39 = f32[1,1408,3072]{1,2,0:T(8,128)} fusion(bf16[2,2048,3072]{2,1,0:T(8,128)(2,1)} %fusion.7, f32[2]{0:T(128)S(1)} %multiply_minimum_fusion, bf16[3,2,2048,1408]{3,2,1,0:T(8,128)(2,1)} %param.9), kind=kOutput, calls=%fused_computation.69 | convolution fusion | flops 35471228928 | bytes 54001672 | tf_op jit(solution)/shard_map/btd,btf->df/dot_general | solution.py:52
  1231.7 48.7 %fusion.38 = f32[1,1408,3072]{1,2,0:T(8,128)} fusion(bf16[2,2048,3072]{2,1,0:T(8,128)(2,1)} %fusion.25, f32[2]{0:T(128)S(1)} %multiply_minimum_fusion, bf16[3,2,2048,1408]{3,2,1,0:T(8,128)(2,1)} %param.9), kind=kOutput, calls=%fused_computation.68 | convolution fusion | flops 35471228928 | bytes 54001672 | tf_op jit(solution)/shard_map/btd,btf->df/dot_general | solution.py:52
  1280.4 48.7 %fusion.37 = f32[1,1408,3072]{1,2,0:T(8,128)} fusion(bf16[2,2048,3072]{2,1,0:T(8,128)(2,1)} %fusion.16, f32[2]{0:T(128)S(1)} %multiply_minimum_fusion, bf16[3,2,2048,1408]{3,2,1,0:T(8,128)(2,1)} %param.9), kind=kOutput, calls=%fused_computation.67 | convolution fusion | flops 35471228928 | bytes 54001672 | tf_op jit(solution)/shard_map/btd,btf->df/dot_general | solution.py:52
  1329.1 55.0 %convolution_bitcast_fusion.2 = f32[1,3072,1408]{2,1,0:T(8,128)} fusion(f32[2]{0:T(128)S(1)} %multiply_minimum_fusion, bf16[2,2048,1408]{2,1,0:T(8,128)(2,1)} %fusion.33, bf16[2,2048,1408]{2,1,0:T(8,128)(2,1)} %all-reduce.7.cloned.1.call-done, f32[2,2048,3072]{2,1,0:T(8,128)} %get-tuple-element.7, bf16[3,2,2048,3072]{3,2,1,0:T(8,128)(2,1)} %param.10), kind=kOutput, calls=%fused_computation.72 | convolution fusion | flops 35511599104 | bytes 115867656 | tf_op jit(solution)/shard_map/btf,btd->fd/dot_general | solution.py:53
  1384.1 33.4 %pad_maximum_fusion.1 = f32[3,3072,1408]{2,1,0:T(8,128)} fusion(f32[1,3072,1408]{2,1,0:T(8,128)} %convolution_bitcast_fusion, f32[1,3072,1408]{2,1,0:T(8,128)} %convolution_bitcast_fusion.1, f32[1,3072,1408]{2,1,0:T(8,128)} %convolution_bitcast_fusion.2), kind=kLoop, calls=%fused_computation.16 | loop fusion | flops 25952256 | bytes 103809024 | tf_op jit(solution)/shard_map/stack | solution.py:54
  1417.5 33.4 %pad_maximum_fusion = f32[3,1408,3072]{1,2,0:T(8,128)} fusion(f32[1,1408,3072]{1,2,0:T(8,128)} %fusion.37, f32[1,1408,3072]{1,2,0:T(8,128)} %fusion.38, f32[1,1408,3072]{1,2,0:T(8,128)} %fusion.39), kind=kLoop, calls=%fused_computation.15 | loop fusion | flops 25952256 | bytes 103809024 | tf_op jit(solution)/shard_map/stack | solution.py:54
  1451.0 0.0 all-reduce.9.cloned.1.call-update
  1451.7 51.5 %copy.14 = f32[3,1408,3072]{1,2,0:T(8,128)} copy(f32[3,1408,3072]{2,1,0:T(8,128)} %param.14) | data formatting | bytes 103809024 | tf_op args[5]
  1503.1 1652.9 %all-reduce.9.cloned.1.call-done = (f32[3,1408,3072]{1,2,0:T(8,128)}, f32[3,3072,1408]{2,1,0:T(8,128)}) async-done(((f32[3,1408,3072]{1,2,0:T(8,128)}, f32[3,3072,1408]{2,1,0:T(8,128)}), (f32[3,1408,3072]{1,2,0:T(8,128)}, f32[3,3072,1408]{2,1,0:T(8,128)})) %all-reduce.9.cloned.1.call-update) | async-done | bytes 103809040 | tf_op jit(solution)/shard_map/psum | solution.py:54
  3156.0 50.5 %add_multiply_fusion.1 = f32[3,1408,3072]{1,2,0:T(8,128)} fusion(f32[3,1408,3072]{1,2,0:T(8,128)} %get-tuple-element.4, f32[3,1408,3072]{1,2,0:T(8,128)} %copy.14, f32[]{:T(128)S(6)} %mul.179), kind=kLoop, calls=%fused_computation.18 | loop fusion | flops 38928384 | bytes 155713536 | tf_op jit(solution)/shard_map/div | solution.py:56
  3206.5 51.4 %copy.18 = f32[3,1408,3072]{2,1,0:T(8,128)} copy(f32[3,1408,3072]{1,2,0:T(8,128)} %add_multiply_fusion.1) | data formatting | bytes 103809024
  3257.8 50.5 %add_multiply_fusion = f32[3,3072,1408]{2,1,0:T(8,128)} fusion(f32[3,3072,1408]{2,1,0:T(8,128)} %get-tuple-element.5, f32[3,3072,1408]{2,1,0:T(8,128)} %param.15, f32[]{:T(128)S(6)} %mul.179), kind=kLoop, calls=%fused_computation.17 | loop fusion | flops 38928384 | bytes 155713536 | tf_op jit(solution)/shard_map/div | solution.py:57
  (2 shorter events, 0.0 us)
Async XLA Ops:
  7.2 593.3 %all-reduce.5.cloned.1.call-start = ((), (), s32[]{:S(2)}) async-start(), calls=%async_computation | async-start | bytes 23068672 | tf_op jit(solution)/shard_map/psum | solution.py:41
  190.7 677.8 %all-reduce.7.cloned.1.call-start = ((), (), s32[]{:S(2)}) async-start(), calls=%async_computation.1 | async-start | bytes 23068672 | tf_op jit(solution)/shard_map/psum | solution.py:41
  725.2 2430.8 %all-reduce.9.cloned.1.call-start = ((), (), s32[]{:S(2)}) async-start(), calls=%async_computation.2 | async-start | bytes 207618048 | tf_op jit(solution)/shard_map/psum | solution.py:54
  1029.1 45.5 %copy-start = (f32[2]{0:T(128)S(1)}, f32[2]{0:T(128)}, u32[]{:S(2)}) copy-start(f32[2]{0:T(128)} %add_reduce_fusion.2) | copy-start | bytes 28
  1029.1 45.5 %copy-start.1 = (f32[2]{0:T(128)S(1)}, f32[2]{0:T(128)}, u32[]{:S(2)}) copy-start(f32[2]{0:T(128)} %add_reduce_fusion.1) | copy-start | bytes 28
Sparse Core Ops, SparseCore 0:
  190.8 37.5 all-reduce.4
  725.3 37.5 all-reduce.6
  1451.1 1704.8 all-reduce.8
where the time goes:
time: 3320 us
  waiting for transfers between devices  1650 us (50%)
  matrix products  1290 us (39%)
  other arithmetic  253 us (8%)
  local copies, waits for them, and re-layouts  103 us (3%)
    psum x1, waiting for transfers between devices, local_run(): lax.psum((jnp.stack(grads_in), jnp.stack(grads_out)), 'dp')  1650 us
    dot_general x3, matrix products, local_run(): jnp.einsum('btf,bsf->bts', hidden, hidden, preferred_element_type=jnp.flo...  267 us
    dot_general x3, matrix products, local_run(): jnp.einsum('btf,bsf->bts', d_hid, d_hid, preferred_element_type=jnp.float32)  188 us
    dot_general x3, matrix products, local_run(): jnp.einsum('btd,fd->btf', d_z, w_out[layer_idx], preferred_element_type=j...  184 us
    dot_general x3, matrix products, local_run(): jnp.einsum('btf,btd->fd', hidden, d_z_c, preferred_element_type=jnp.float32)  160 us
    dot_general x3, matrix products, local_run(): jnp.einsum('btd,btf->df', block_in[layer_idx], d_hid_c, preferred_element...  146 us
    dot_general x3, matrix products, local_run(): jnp.einsum('btd,bsd->bts', x_layer, x_layer, preferred_element_type=jnp.f...  138 us
    dot_general x3, matrix products, local_run(): jnp.einsum('btd,bsd->bts', d_z, d_z, preferred_element_type=jnp.float32)  113 us
  transfers between devices with their start and end apart: 3, of which 1 were waited for; matrix products, arithmetic and copies ran while one was open for 18% of the time, Pallas kernels for 0%

commit v1 on v0

v1 whole, which is shorter than its diff:
```python
import functools

import jax
import jax.numpy as jnp
from jax import lax
from jax.experimental import pallas as pl
from jax.experimental.pallas import tpu as pltpu
from jax.sharding import PartitionSpec as P


INV_SQRT2 = 0.7071067811865476
INV_SQRT_2PI = 0.3989422804014327
F_BLOCK = 512
T_CHUNK = 512
IN_CHUNK = 128
IN_SLOTS = 4
ROW_STEPS = 2
VMEM_LIMIT = 66_500_000

F32 = jnp.float32
BF16 = jnp.bfloat16
ANY = pl.ANY


def dot_nn(a, b):
    return lax.dot_general(a, b, (((1,), (0,)), ((), ())), preferred_element_type=F32)


def dot_nt(a, b):
    return lax.dot_general(a, b, (((1,), (1,)), ((), ())), preferred_element_type=F32)


def layer_kernel(first, last, n_steps, sc_ref, u_ref, w1_ref, w2_ref, x_hbm, dz_hbm, *refs):
    refs = list(refs)
    p_hbm, q_hbm = (None, None) if first else (refs.pop(0), refs.pop(0))
    refs.pop(0)
    if last:
        g1_hbm, g2_hbm = refs.pop(0), refs.pop(0)
    else:
        g1k_hbm, g1s_hbm, g2k_hbm, g2s_hbm, dx_hbm = [refs.pop(0) for _ in range(5)]
    dzo_hbm = None if (first or last) else refs.pop(0)
    ss_ref = refs.pop(0)
    x_t, dz, dz_t, dh, h, bh, x_st = [refs.pop(0) for _ in range(7)]
    p_st, q_st = (None, None) if first else (refs.pop(0), refs.pop(0))
    if last:
        g1_st, g2_st = refs.pop(0), refs.pop(0)
    else:
        acc, g1k_st, g1s_st, g2k_st, g2s_st = [refs.pop(0) for _ in range(5)]
    in_sem, out_sem = refs.pop(0), refs.pop(0)

    step = pl.program_id(0)
    layer, example, x_pos, y_pos = sc_ref[0], sc_ref[1], sc_ref[2], sc_ref[3]
    n_tok, d_model = dz.shape
    half_d = d_model // 2
    n_t = n_tok // T_CHUNK
    n_in = n_tok // IN_CHUNK

    def in_copies(c):
        slot = lax.rem(c, IN_SLOTS)
        rows = pl.ds(pl.multiple_of(c * IN_CHUNK, IN_CHUNK), IN_CHUNK)
        dz_src = dz_hbm.at[rows, :] if last else dz_hbm.at[example, rows, :]
        pairs = [(x_hbm.at[layer, example, rows, :], x_st.at[slot]), (dz_src, dz.at[rows, :])]
        if not first:
            pairs += [(p_hbm.at[rows, :], p_st.at[slot]), (q_hbm.at[rows, :], q_st.at[slot])]
        return [pltpu.make_async_copy(a, b, in_sem.at[k, slot]) for k, (a, b) in enumerate(pairs)]

    @pl.when(step == 0)
    def _():
        for c in range(IN_SLOTS - 1):
            for cp in in_copies(c):
                cp.start()
        if not last:
            acc[...] = jnp.zeros_like(acc)
        ss_ref[...] = jnp.zeros_like(ss_ref)

        def load(c, carry):
            @pl.when(c + IN_SLOTS - 1 < n_in)
            def _():
                for cp in in_copies(c + IN_SLOTS - 1):
                    cp.start()

            for cp in in_copies(c):
                cp.wait()
            slot = lax.rem(c, IN_SLOTS)
            at = pl.ds(pl.multiple_of(c * IN_CHUNK, IN_CHUNK), IN_CHUNK)
            x_t[:, at] = x_st[slot].T
            if first:
                z = dz[at, :]
            else:
                z = (dz[at, :].astype(F32) + (p_st[slot].astype(F32) + q_st[slot].astype(F32))).astype(BF16)
                dz[at, :] = z
            dz_t[:, at] = z.T
            return carry

        lax.fori_loop(0, n_in, load, 0)
        if dzo_hbm is not None:
            pltpu.make_async_copy(dz, dzo_hbm, out_sem.at[4]).start()

    for s in range(n_t + (1 if last else 2)):
        if s < n_t:
            bh[s % 2] = dot_nt(dz[pl.ds(s * T_CHUNK, T_CHUNK), :], w2_ref[0])
        if 1 <= s <= n_t:
            rows = pl.ds((s - 1) * T_CHUNK, T_CHUNK)
            u = u_ref[0, 0, rows, :].astype(F32)
            cdf = 0.5 * (1.0 + lax.erf(u * INV_SQRT2))
            h[rows, :] = (u * cdf).astype(BF16)
            slope = cdf + u * jnp.exp(-0.5 * u * u) * INV_SQRT_2PI
            dh[rows, :] = (slope * bh[(s - 1) % 2]).astype(BF16)
        if s >= 2 and not last:
            rows = pl.ds((s - 2) * T_CHUNK, T_CHUNK)
            acc[rows, :] = acc[rows, :] + dot_nt(dh[rows, :], w1_ref[0])

    cols = lambda k: pl.ds(pl.multiple_of(k * F_BLOCK, F_BLOCK), F_BLOCK)

    if last:
        def out_copies(k):
            yield pltpu.make_async_copy(g1_st, g1_hbm.at[:, cols(k)], out_sem.at[0]), None
            yield pltpu.make_async_copy(g2_st, g2_hbm.at[:, cols(k)], out_sem.at[1]), None
    else:
        fb = lambda k: lax.rem(k + (n_steps // 2) * (1 - y_pos), n_steps)

        def out_copies(k):
            yield pltpu.make_async_copy(g1k_st, g1k_hbm.at[:, cols(fb(k))], out_sem.at[0]), None
            yield pltpu.make_async_copy(g1s_st, g1s_hbm.at[:, cols(fb(k))], out_sem.at[1]), None
            yield pltpu.make_async_copy(g2s_st, g2s_hbm.at[:, cols(k)], out_sem.at[2]), k < n_steps // 2
            yield pltpu.make_async_copy(g2k_st, g2k_hbm.at[:, cols(k - n_steps // 2)], out_sem.at[3]), k >= n_steps // 2

    def run(copies, act):
        for cp, cond in copies:
            if cond is None:
                getattr(cp, act)()
            else:
                pl.when(cond)(getattr(cp, act))

    @pl.when(step > 0)
    def _():
        run(out_copies(step - 1), 'wait')

    def square(g):
        return jnp.sum((g * g).reshape(g.shape[0] // 8, 8, g.shape[1]), axis=0)

    def weight_grads(r, carry):
        quarter = half_d // ROW_STEPS
        a = pl.multiple_of(r * quarter, quarter)
        b = pl.multiple_of(r * quarter + half_d, quarter)
        if last:
            total = ss_ref[...]
            for at in (a, b):
                rows = pl.ds(at, quarter)
                g = dot_nn(x_t[rows, :], dh[...])
                g1_st[rows, :] = g
                total = total + square(g)
                g = dot_nn(dz_t[rows, :], h[...])
                g2_st[rows, :] = g
                total = total + square(g)
        else:
            own = pl.multiple_of(r * quarter + x_pos * half_d, quarter)
            far = pl.multiple_of(r * quarter + (1 - x_pos) * half_d, quarter)
            rows = pl.ds(a, quarter)
            g = dot_nn(x_t[pl.ds(own, quarter), :], dh[...])
            g1k_st[rows, :] = g
            total = ss_ref[...] + square(g)
            g = dot_nn(x_t[pl.ds(far, quarter), :], dh[...])
            g1s_st[rows, :] = g.astype(BF16)
            total = total + square(g)
            for at in (a, b):
                rows = pl.ds(at, quarter)
                g = dot_nn(dz_t[rows, :], h[...])
                g2k_st[rows, :] = g
                g2s_st[rows, :] = g.astype(BF16)
                total = total + square(g)
        ss_ref[...] = total
        return carry

    lax.fori_loop(0, ROW_STEPS, weight_grads, 0)
    run(out_copies(step), 'start')

    @pl.when(step == n_steps - 1)
    def _():
        if not last:
            def dx_copy(c):
                rows = pl.ds(pl.multiple_of(c * IN_CHUNK, IN_CHUNK), IN_CHUNK)
                slot = lax.rem(c, IN_SLOTS)
                return pltpu.make_async_copy(x_st.at[slot], dx_hbm.at[rows, :], in_sem.at[0, slot])

            def put(c, carry):
                @pl.when(c >= IN_SLOTS)
                def _():
                    dx_copy(c - IN_SLOTS).wait()

                rows = pl.ds(pl.multiple_of(c * IN_CHUNK, IN_CHUNK), IN_CHUNK)
                x_st[lax.rem(c, IN_SLOTS)] = acc[rows, :].astype(BF16)
                dx_copy(c).start()
                return carry

            lax.fori_loop(0, n_in, put, 0)
            for c in range(n_in - IN_SLOTS, n_in):
                dx_copy(c).wait()
        run(out_copies(step), 'wait')
        if dzo_hbm is not None:
            pltpu.make_async_copy(dz, dzo_hbm, out_sem.at[4]).wait()


def run_layer(kind, place, layer, example, pre_act, w_in, w_out, block_in, dz, parts, token):
    first, last = kind == 'first', kind == 'last'
    n_tok, d_model, d_ff = block_in.shape[2], block_in.shape[3], pre_act.shape[3]
    n_steps = d_ff // F_BLOCK
    half_d, half_f = d_model // 2, d_ff // 2

    def f_at(j, sc):
        return j if last else lax.rem(j + (n_steps // 2) * (1 - sc[3]), n_steps)

    in_specs = [
        pl.BlockSpec((1, 1, n_tok, F_BLOCK), lambda j, sc: (sc[0], sc[1], 0, f_at(j, sc))),
        pl.BlockSpec((1, d_model, F_BLOCK), lambda j, sc: (sc[0], 0, f_at(j, sc))),
        pl.BlockSpec((1, F_BLOCK, d_model), lambda j, sc: (sc[0], f_at(j, sc), 0)),
    ]
    extra = [block_in, dz, *parts, token]
    in_specs += [pl.BlockSpec(memory_space=ANY)] * len(extra)
    sds = jax.ShapeDtypeStruct
    scratch = [
        pltpu.VMEM((d_model, n_tok), BF16),
        pltpu.VMEM((n_tok, d_model), BF16),
        pltpu.VMEM((d_model, n_tok), BF16),
        pltpu.VMEM((n_tok, F_BLOCK), BF16),
        pltpu.VMEM((n_tok, F_BLOCK), BF16),
        pltpu.VMEM((2, T_CHUNK, F_BLOCK), F32),
        pltpu.VMEM((IN_SLOTS, IN_CHUNK, d_model), BF16),
    ]
    if not first:
        scratch += [pltpu.VMEM((IN_SLOTS, IN_CHUNK, d_model), BF16)] * 2
    if last:
        outs = [sds((d_model, d_ff), F32), sds((d_model, d_ff), F32)]
        scratch += [pltpu.VMEM((d_model, F_BLOCK), F32)] * 2
    else:
        outs = [
            sds((half_d, d_ff), F32), sds((half_d, d_ff), BF16),
            sds((d_model, half_f), F32), sds((d_model, half_f), BF16),
            sds((n_tok, d_model), BF16),
        ]
        if not first:
            outs.append(sds((n_tok, d_model), BF16))
        scratch += [
            pltpu.VMEM((n_tok, d_model), F32),
            pltpu.VMEM((half_d, F_BLOCK), F32), pltpu.VMEM((half_d, F_BLOCK), BF16),
            pltpu.VMEM((d_model, F_BLOCK), F32), pltpu.VMEM((d_model, F_BLOCK), BF16),
        ]
    scratch += [pltpu.SemaphoreType.DMA((4, IN_SLOTS)), pltpu.SemaphoreType.DMA((5,))]
    out_specs = [pl.BlockSpec(memory_space=ANY)] * len(outs)
    outs.append(sds((8, F_BLOCK), F32))
    out_specs.append(pl.BlockSpec((8, F_BLOCK), lambda j, sc: (0, 0)))
    n_dots = 3 if last else 4
    return pl.pallas_call(
        functools.partial(layer_kernel, first, last, n_steps),
        out_shape=outs,
        grid_spec=pltpu.PrefetchScalarGridSpec(
            num_scalar_prefetch=1, grid=(n_steps,), in_specs=in_specs, out_specs=out_specs, scratch_shapes=scratch),
        compiler_params=pltpu.CompilerParams(dimension_semantics=('arbitrary',), vmem_limit_bytes=VMEM_LIMIT),
        cost_estimate=pl.CostEstimate(
            flops=2 * n_dots * n_tok * d_model * d_ff, bytes_accessed=80_000_000, transcendentals=2 * n_tok * d_ff),
    )(jnp.stack([jnp.int32(layer), jnp.int32(example), place[0], place[1]]), pre_act, w_in, w_out, *extra)


def put_in_kernel(sc_ref, coef_ref, piece_ref, noise_ref, *rest):
    out_ref = rest[-1]
    out_ref[0, 0] = (piece_ref[...].astype(F32) + coef_ref[0] * noise_ref[0, 0]) * coef_ref[1]


def put_out_kernel(sc_ref, coef_ref, piece_ref, noise_ref, *rest):
    out_ref = rest[-1]
    out_ref[0, 0] = (piece_ref[...].astype(F32).T + coef_ref[0] * noise_ref[0, 0]) * coef_ref[1]


def put_piece(transposed, total, layer, quarter, coef, piece, noise):
    if transposed:
        rows, width = piece.shape[1], piece.shape[0]
        block = 256
        piece_spec = pl.BlockSpec((width, block), lambda i, sc: (0, i))
    else:
        rows, width = piece.shape
        block = rows // 2
        piece_spec = pl.BlockSpec((block, width), lambda i, sc: (i, 0))
    big_spec = pl.BlockSpec((1, 1, block, width), lambda i, sc: (sc[0], sc[1], i, 0))
    args = [jnp.stack([jnp.int32(layer), quarter]), coef, piece, noise]
    in_specs = [pl.BlockSpec(memory_space=pltpu.SMEM), piece_spec, big_spec]
    aliases = {}
    if total is not None:
        args.append(total)
        in_specs.append(pl.BlockSpec(memory_space=ANY))
        aliases = {4: 0}
    return pl.pallas_call(
        put_out_kernel if transposed else put_in_kernel,
        out_shape=jax.ShapeDtypeStruct(noise.shape, F32),
        grid_spec=pltpu.PrefetchScalarGridSpec(
            num_scalar_prefetch=1, grid=(rows // block,), in_specs=in_specs, out_specs=big_spec),
        input_output_aliases=aliases,
        compiler_params=pltpu.CompilerParams(dimension_semantics=('arbitrary',), vmem_limit_bytes=40_000_000),
        cost_estimate=pl.CostEstimate(flops=4 * rows * width, bytes_accessed=10 * rows * width, transcendentals=0),
        name='put_out' if transposed else 'put_in',
    )(*args)


def solution(mesh):
    data_size = mesh.shape['dp']
    swap_x = [(i, i ^ 1) for i in range(data_size)]
    swap_y = [(i, i ^ 2) for i in range(data_size)]

    def local_step(block_in, pre_act, w_in, w_out, d_out, noise_in, noise_out, clip_norm, noise_mult):
        n_layers, local_batch, _, d_model = block_in.shape
        d_ff = pre_act.shape[3]
        batch_total = local_batch * data_size
        dp = lax.axis_index('dp')
        x_pos, y_pos = lax.rem(dp, 2), dp // 2
        place = (x_pos, y_pos)
        over_x = lambda v: lax.ppermute(v, 'dp', swap_x)
        over_y = lambda v: lax.ppermute(v, 'dp', swap_y)
        over_tp = lambda v: lax.ppermute(v, 'tp', [(0, 1), (1, 0)])

        token = jnp.zeros((8, F_BLOCK), F32)
        d_z = [d_out] * local_batch
        parts = [()] * local_batch
        grads = [[None] * local_batch for _ in range(n_layers)]
        far = [[None] * local_batch for _ in range(n_layers)]
        sums = [[] for _ in range(local_batch)]
        for layer in range(n_layers - 1, -1, -1):
            kind = 'first' if layer == n_layers - 1 else ('last' if layer == 0 else 'mid')
            for ex in range(local_batch):
                res = run_layer(kind, place, layer, ex, pre_act, w_in, w_out, block_in, d_z[ex], parts[ex], token)
                token = res[-1]
                sums[ex].append(jnp.sum(token))
                if kind == 'last':
                    grads[layer][ex] = res[:2]
                else:
                    g1k, g1s, g2k, g2s, dx_part = res[:5]
                    grads[layer][ex] = (g1k, g2k)
                    parts[ex] = (dx_part, over_tp(dx_part))
                    far_x = over_x(g1s)
                    far_y = over_y(g2s)
                    far[layer][ex] = (far_x, far_y)
                    if kind == 'mid':
                        d_z[ex] = res[5]

        part_sq = jnp.stack([sum(s) for s in sums])
        part_all = lax.dynamic_update_slice(jnp.zeros((batch_total,), F32), part_sq, (dp * local_batch,))
        sq_norm = lax.psum(part_all, ('dp', 'tp'))
        clip = jnp.minimum(1.0, clip_norm / jnp.sqrt(sq_norm))
        at = lambda d: [lax.dynamic_index_in_dim(clip, d * local_batch + k, keepdims=False) for k in range(local_batch)]
        c_own, c_x, c_y = at(dp), at(dp ^ 1), at(dp ^ 2)
        mix = lambda cs, vs: sum(c * v.astype(F32) for c, v in zip(cs, vs))
        coef = jnp.stack([noise_mult * clip_norm, jnp.float32(1.0 / batch_total)])

        cut = lambda v, axis, pos: lax.dynamic_slice_in_dim(v, pos * (v.shape[axis] // 2), v.shape[axis] // 2, axis)
        noise_in4 = noise_in.reshape(n_layers, 4, d_model // 4, d_ff)
        noise_out4 = noise_out.reshape(n_layers, 4, d_ff // 4, d_model)
        grad_in = grad_out = None

        def half(layer, which, axis, pos, c_far, far_parts, part_pos):
            own = [grads[layer][k][which] for k in range(local_batch)]
            if layer == 0:
                own = [cut(v, axis, pos) for v in own]
            vals = [cut(v, axis, part_pos) for v in own]
            res = mix(c_own, vals)
            fp = [cut(v, axis, part_pos) for v in far_parts]
            return res + (mix(c_far, fp) if layer else fp[0].astype(F32))

        order = [2, 1, 0]
        last_far = [
            (over_x(mix(c_own, [cut(grads[0][k][0], 0, 1 - x_pos) for k in range(local_batch)]).astype(BF16)),),
            (over_y(mix(c_own, [cut(grads[0][k][1], 1, 1 - y_pos) for k in range(local_batch)]).astype(BF16)),),
        ]
        for layer in order:
            far1 = [far[layer][k][0] for k in range(local_batch)] if layer else last_far[0]
            far2 = [far[layer][k][1] for k in range(local_batch)] if layer else last_far[1]
            send1 = half(layer, 0, 0, x_pos, c_x, far1, 1 - y_pos).astype(BF16)
            send2 = half(layer, 1, 1, y_pos, c_y, far2, 1 - x_pos).astype(BF16)
            got1, got2 = over_y(send1), over_x(send2)
            own1 = (half(layer, 0, 0, x_pos, c_x, far1, y_pos) + got1.astype(F32)).astype(BF16)
            own2 = (half(layer, 1, 1, y_pos, c_y, far2, x_pos) + got2.astype(F32)).astype(BF16)
            near1, near2 = over_y(own1), over_x(own2)
            side1, side2 = over_x(own1), over_y(own2)
            diag1, diag2 = over_x(near1), over_y(near2)
            q1 = lambda a, b: 2 * a + b
            for a, b, v in ((x_pos, y_pos, own1), (x_pos, 1 - y_pos, near1), (1 - x_pos, y_pos, side1), (1 - x_pos, 1 - y_pos, diag1)):
                grad_in = put_piece(False, grad_in, layer, q1(a, b), coef, v, noise_in4)
            for a, b, v in ((y_pos, x_pos, own2), (y_pos, 1 - x_pos, near2), (1 - y_pos, x_pos, side2), (1 - y_pos, 1 - x_pos, diag2)):
                grad_out = put_piece(True, grad_out, layer, q1(a, b), coef, v, noise_out4)
        return grad_in.reshape(n_layers, d_model, d_ff), grad_out.reshape(n_layers, d_ff, d_model)


    return jax.shard_map(
        local_step,
        mesh=mesh,
        in_specs=(P(None, 'dp', None, None), P(None, 'dp', None, 'tp'), P(None, None, 'tp'), P(None, 'tp', None),
                  P('dp', None, None), P(None, None, 'tp'), P(None, 'tp', None), P(), P()),
        out_specs=(P(None, None, 'tp'), P(None, 'tp', None)),
        check_vma=False,
    )
```

time: 3320 us -> 1560 us (0.47)
  matrix products: 1290 us -> 0 us
  waiting for transfers between devices: 1650 us -> 526 us
  Pallas kernels: 0 us -> 710 us
  blocking collectives: 3.05 us -> 117 us
  other arithmetic: 253 us -> 151 us
  local copies, waits for them, and re-layouts: 103 us -> 1.33 us
  starting transfers between devices: 0.12 us -> 41.6 us
    psum x3 -> x0, waiting for transfers between devices: 1650 us -> none  [the longest x1 1650 us: local_run(): lax.psum((jnp.stack(grads_in), jnp.stack(grads_out)), 'dp')]
    dot_general x23 -> x0, matrix products: 1290 us -> none  [the longest x3 267 us: local_run(): jnp.einsum('btf,bsf->bts', hidden, hidden, preferred_element_type=jnp.flo...]
    pallas_call x0 -> x30, Pallas kernels: none -> 710 us  [the longest x6 570 us: run_layer(): pl.pallas_call(functools.partial(layer_kernel, first, last, n_steps), out...]
    ppermute x0 -> x38, waiting for transfers between devices: none -> 526 us  [the longest x17 263 us: local_step(): over_x = lambda v: lax.ppermute(v, 'dp', swap_x)]
    convert_element_type x1 -> x14, other arithmetic: 13 us -> 140 us  [the longest x3 32 us: local_step(): (half(layer, 1, 1, y_pos, c_y, far2, x_pos) + got2.astype(F32)).astype(BF16)]
    psum x1, blocking collectives: 3.05 us -> 117 us  [local_step(): sq_norm = lax.psum(part_all, ('dp', 'tp'))]
    unnamed x6 -> x20, local copies, waits for them, and re-layouts: 103 us -> 0.04 us
    div x2 -> x0, other arithmetic: 101 us -> none  [the longest x1 50.5 us: local_run(): grad_in = (sum_in + noise_coef * noise_in) / batch_total]
  transfers between devices with their start and end apart: 3 -> 38, of which waited for: 1 -> 15; matrix products, arithmetic and copies ran while one was open for 18% -> 10% of each run, Pallas kernels for 0% -> 39%
where the time goes in v1:
time: 1560 us; the launch traced here: 1550 us
  Pallas kernels  710 us (46%)
  waiting for transfers between devices  526 us (34%)
  other arithmetic  151 us (10%)
  blocking collectives  117 us (8%)
  starting transfers between devices  41.6 us (3%)
    pallas_call x6, Pallas kernels, run_layer(): pl.pallas_call(functools.partial(layer_kernel, first, last, n_steps), out...  570 us
    ppermute x17, waiting for transfers between devices, local_step(): over_x = lambda v: lax.ppermute(v, 'dp', swap_x)  263 us
    ppermute x17, waiting for transfers between devices, local_step(): over_y = lambda v: lax.ppermute(v, 'dp', swap_y)  263 us
    pallas_call x24, Pallas kernels, put_piece(): pl.pallas_call(put_out_kernel if transposed else put_in_kernel, out_shape...  140 us
    psum x1, blocking collectives, local_step(): sq_norm = lax.psum(part_all, ('dp', 'tp'))  117 us
    convert_element_type x3, other arithmetic, local_step(): (half(layer, 1, 1, y_pos, c_y, far2, x_pos) + got2.astype(F32)).astype(BF16)  32 us
  transfers between devices with their start and end apart: 38, of which 15 were waited for; matrix products, arithmetic and copies ran while one was open for 10% of the time, Pallas kernels for 39%

profile of v1, /device:TPU:0, one launch (start us, length us, event | category | flops | bytes accessed | tf_op | source)
XLA Modules:
  0.0 1551.7 jit_solution(13338803621262209814)
XLA Ops:
  1.9 101.1 %shard_map.104 = (f32[704,3072]{1,0:T(8,128)}, bf16[704,3072]{1,0:T(8,128)(2,1)}, f32[1408,1536]{1,0:T(8,128)}, bf16[1408,1536]{1,0:T(8,128)(2,1)}, bf16[2048,1408]{1,0:T(8,128)(2,1)}, /*index=5*/f32[8,512]{1,0:T(8,128)}) custom-call(s32[4]{0:T(128)} %get-tuple-element.72.sc_ref, bf16[3,2,2048,3072]{3,2,1,0:T(8,128)(2,1)} %u_ref.11, ...), custom_call_target="tpu_custom_call" | custom-call | flops 70866960384 | bytes 80000000 | tf_op jit(solution)/shard_map/pallas_call | solution.py:253
  103.8 101.3 %shard_map.105 = (f32[704,3072]{1,0:T(8,128)}, bf16[704,3072]{1,0:T(8,128)(2,1)}, f32[1408,1536]{1,0:T(8,128)}, bf16[1408,1536]{1,0:T(8,128)(2,1)}, bf16[2048,1408]{1,0:T(8,128)(2,1)}, /*index=5*/f32[8,512]{1,0:T(8,128)}) custom-call(s32[4]{0:T(128)} %get-tuple-element.73.sc_ref, bf16[3,2,2048,3072]{3,2,1,0:T(8,128)(2,1)} %u_ref.11, ...), custom_call_target="tpu_custom_call" | custom-call | flops 70866960384 | bytes 80000000 | tf_op jit(solution)/shard_map/pallas_call | solution.py:253
  206.5 103.3 %shard_map.106 = (f32[704,3072]{1,0:T(8,128)}, bf16[704,3072]{1,0:T(8,128)(2,1)}, f32[1408,1536]{1,0:T(8,128)}, bf16[1408,1536]{1,0:T(8,128)(2,1)}, bf16[2048,14...) custom-call(s32[4]{0:T(128)} %fusion.7.sc_ref, bf16[3,2,2048,3072]{3,2,1,0:T(8,128)(2,1)} %u_ref.11, ...), custom_call_target="tpu_custom_call" | custom-call | flops 70866960384 | bytes 80000000 | tf_op jit(solution)/shard_map/pallas_call | solution.py:253
  310.3 103.5 %shard_map.107 = (f32[704,3072]{1,0:T(8,128)}, bf16[704,3072]{1,0:T(8,128)(2,1)}, f32[1408,1536]{1,0:T(8,128)}, bf16[1408,1536]{1,0:T(8,128)(2,1)}, bf16[2048,14...) custom-call(s32[4]{0:T(128)} %add_add_fusion.1.sc_ref, bf16[3,2,2048,3072]{3,2,1,0:T(8,128)(2,1)} %u_ref.11, ...), custom_call_target="tpu_custom_call" | custom-call | flops 70866960384 | bytes 80000000 | tf_op jit(solution)/shard_map/pallas_call | solution.py:253
  426.5 80.4 %shard_map.108 = (f32[1408,3072]{1,0:T(8,128)}, f32[1408,3072]{1,0:T(8,128)}, f32[8,512]{1,0:T(8,128)}) custom-call(s32[4]{0:T(128)} %add_add_fusion.sc_ref, bf16[3,2,2048,3072]{3,2,1,0:T(8,128)(2,1)} %u_ref.11, bf16[3,1408,3072]{2,1,0:T(8,128)(2,1)} %w1_ref.11, bf16[3,3072,1408]{2,1,0:T(8,128)(2,1)} %w2_ref.11, bf16[3,2,2048,1408]{3,2,1,0:T(8,128)(2,1)} %x_hbm.11, ...), custom_call_target="tpu_custom_call" | custom-call | flops 53150220288 | bytes 80000000 | tf_op jit(solution)/shard_map/pallas_call | solution.py:253
  514.9 89.1 %collective-permute-done.16 = bf16[704,3072]{1,0:T(8,128)(2,1)} collective-permute-done((bf16[704,3072]{1,0:T(8,128)(2,1)}, bf16[704,3072]{1,0:T(8,128)(2,1)}, u32[]{:S(2)}, u32[]{:S(2)}) %collective-permute-start.16) | collective-permute-done | bytes 4325408 | tf_op jit(solution)/shard_map/ppermute | solution.py:315
  607.6 80.3 %shard_map.109 = (f32[1408,3072]{1,0:T(8,128)}, f32[1408,3072]{1,0:T(8,128)}, f32[8,512]{1,0:T(8,128)}) custom-call(s32[4]{0:T(128)} %fusion.5.sc_ref, bf16[3,2,2048,3072]{3,2,1,0:T(8,128)(2,1)} %u_ref.11, bf16[3,1408,3072]{2,1,0:T(8,128)(2,1)} %w1_ref.11, bf16[3,3072,1408]{2,1,0:T(8,128)(2,1)} %w2_ref.11, bf16[3,2,2048,1408]{3,2,1,0:T(8,128)(2,1)} %x_hbm.11, ...), custom_call_target="tpu_custom_call" | custom-call | flops 53150220288 | bytes 80000000 | tf_op jit(solution)/shard_map/pallas_call | solution.py:253
  691.3 116.9 %psum.7 = f32[8]{0:T(128)S(1)} all-reduce(f32[8]{0:T(128)S(1)} %maximum_dynamic-update-slice_fusion), channel_id=1, replica_groups=mesh['dp'=4,'tp'=2] {'dp','tp'}, use_global_device_ids=true, to_apply=%region_6.7 | all-reduce | flops 8 | bytes 64 | tf_op jit(solution)/shard_map/psum | solution.py:345
  808.9 11.4 add_convert_fusion.1
  822.6 12.0 add_convert_fusion
  835.0 10.4 add_convert_fusion.9
  847.1 8.9 add_convert_fusion.11
  856.4 9.7 add_convert_fusion.3
  867.7 8.5 add_convert_fusion.5
  876.3 101.3 %collective-permute-done.17 = bf16[352,3072]{1,0:T(8,128)(2,1)} collective-permute-done((bf16[352,3072]{1,0:T(8,128)(2,1)}, bf16[352,3072]{1,0:T(8,128)(2,1)}, u32[]{:S(2)}, u32[]{:S(2)}) %collective-permute-start.17) | collective-permute-done | bytes 2162720 | tf_op jit(solution)/shard_map/ppermute | solution.py:316
  977.6 9.0 add_convert_fusion.8.piece_ref
  986.6 34.1 %collective-permute-done.11 = bf16[352,3072]{1,0:T(8,128)(2,1)} collective-permute-done((bf16[352,3072]{1,0:T(8,128)(2,1)}, bf16[352,3072]{1,0:T(8,128)(2,1)}, u32[]{:S(2)}, u32[]{:S(2)}) %collective-permute-start.11) | collective-permute-done | bytes 2162720 | tf_op jit(solution)/shard_map/ppermute | solution.py:316
  1021.4 11.1 add_convert_fusion.10.piece_ref
  1033.7 8.1 add_convert_fusion.13
  1043.3 9.9 add_convert_fusion.7
  1054.5 10.8 add_convert_fusion.2.piece_ref
  1065.4 10.7 add_convert_fusion.4.piece_ref
  1077.3 5.2 collective-permute-done.18.piece_ref
  1083.8 33.2 %collective-permute-done.14.piece_ref = bf16[352,3072]{1,0:T(8,128)(2,1)} collective-permute-done((bf16[352,3072]{1,0:T(8,128)(2,1)}, bf16[352,3072]{1,0:T(8,128)(2,1)}, u32[]{:S(2)}, u32[]{:S(2)}) %collective-permute-start.14) | collective-permute-done | bytes 2162720 | tf_op jit(solution)/shard_map/ppermute | solution.py:315
  1117.8 11.1 collective-permute-done.5
  1130.1 33.3 %collective-permute-done.22 = bf16[1408,768]{1,0:T(8,128)(2,1)} collective-permute-done((bf16[1408,768]{1,0:T(8,128)(2,1)}, bf16[1408,768]{1,0:T(8,128)(2,1)}, u32[]{:S(2)}, u32[]{:S(2)}) %collective-permute-start.22) | collective-permute-done | bytes 2162720 | tf_op jit(solution)/shard_map/ppermute | solution.py:315
  1164.8 10.5 add_convert_fusion.6.piece_ref
  1175.3 9.1 add_convert_fusion.12.piece_ref
  1184.9 24.8 %collective-permute-done.35.piece_ref = bf16[1408,768]{1,0:T(8,128)(2,1)} collective-permute-done((bf16[1408,768]{1,0:T(8,128)(2,1)}, bf16[1408,768]{1,0:T(8,128)(2,1)}, u32[]{:S(2)}, u32[]{:S(2)}) %collective-permute-start.35) | collective-permute-done | bytes 2162720 | tf_op jit(solution)/shard_map/ppermute | solution.py:315
  1211.2 44.9 %collective-permute-done.29.piece_ref = bf16[1408,768]{1,0:T(8,128)(2,1)} collective-permute-done((bf16[1408,768]{1,0:T(8,128)(2,1)}, bf16[1408,768]{1,0:T(8,128)(2,1)}, u32[]{:S(2)}, u32[]{:S(2)}) %collective-permute-start.29) | collective-permute-done | bytes 2162720 | tf_op jit(solution)/shard_map/ppermute | solution.py:315
  1258.1 9.8 collective-permute-done.31.piece_ref
  1269.6 32.8 %collective-permute-done.19.piece_ref = bf16[352,3072]{1,0:T(8,128)(2,1)} collective-permute-done((bf16[352,3072]{1,0:T(8,128)(2,1)}, bf16[352,3072]{1,0:T(8,128)(2,1)}, u32[]{:S(2)}, u32[]{:S(2)}) %collective-permute-start.19) | collective-permute-done | bytes 2162720 | tf_op jit(solution)/shard_map/ppermute | solution.py:315
  1303.1 11.1 collective-permute-done.36.piece_ref
  1315.6 45.0 %collective-permute-done.30.piece_ref = bf16[1408,768]{1,0:T(8,128)(2,1)} collective-permute-done((bf16[1408,768]{1,0:T(8,128)(2,1)}, bf16[1408,768]{1,0:T(8,128)(2,1)}, u32[]{:S(2)}, u32[]{:S(2)}) %collective-permute-start.30) | collective-permute-done | bytes 2162720 | tf_op jit(solution)/shard_map/ppermute | solution.py:316
  1361.8 45.2 %collective-permute-done.6.piece_ref = bf16[352,3072]{1,0:T(8,128)(2,1)} collective-permute-done((bf16[352,3072]{1,0:T(8,128)(2,1)}, bf16[352,3072]{1,0:T(8,128)(2,1)}, u32[]{:S(2)}, u32[]{:S(2)}) %collective-permute-start.6) | collective-permute-done | bytes 2162720 | tf_op jit(solution)/shard_map/ppermute | solution.py:316
  1411.8 6.6 put_out.12.rest_0_
  1422.9 6.6 put_out.13.rest_0_
  1434.6 6.6 put_out.14.rest_0_
  1446.3 6.6 put_out.15.rest_0_
  1452.9 6.6 put_out.16.rest_0_
  1459.4 6.6 put_out.17.rest_0_
  1466.0 6.6 put_out.18.rest_0_
  1472.5 6.6 put_out.19.rest_0_
  1479.1 6.6 put_out.20.rest_0_
  1506.2 5.1 put_in.19.rest_0_
  1516.5 6.6 put_out.21.rest_0_
  1528.2 6.6 put_out.22.rest_0_
  1539.9 6.6 put_out.23
  (138 shorter events, 113.6 us)
Async XLA Ops:
  103.0 103.5 %collective-permute-start = (bf16[2048,1408]{1,0:T(8,128)(2,1)}, bf16[2048,1408]{1,0:T(8,128)(2,1)}, u32[]{:S(2)}, u32[]{:S(2)}) collective-permute-start(bf16[2048,1408]{1,0:T(8,128)(2,1)} %get-tuple-element.35.refs_0_), channel_id=1, source_target_pairs={{0,1},{1,0},{2,3},{3,2},{4,5},{5,4},{6,7},{7,6}} | collective-permute-start | bytes 17301512 | tf_op jit(solution)/shard_map/ppermute | solution.py:317
  205.2 105.1 %collective-permute-start.2 = (bf16[2048,1408]{1,0:T(8,128)(2,1)}, bf16[2048,1408]{1,0:T(8,128)(2,1)}, u32[]{:S(2)}, u32[]{:S(2)}) collective-permute-start(bf16[2048,1408]{1,0:T(8,128)(2,1)} %get-tuple-element.40.refs_0_), channel_id=1, source_target_pairs={{0,1},{1,0},{2,3},{3,2},{4,5},{5,4},{6,7},{7,6}} | collective-permute-start | bytes 17301512 | tf_op jit(solution)/shard_map/ppermute | solution.py:317
  309.8 116.6 %collective-permute-start.1 = (bf16[2048,1408]{1,0:T(8,128)(2,1)}, bf16[2048,1408]{1,0:T(8,128)(2,1)}, u32[]{:S(2)}, u32[]{:S(2)}) collective-permute-start(bf16[2048,1408]{1,0:T(8,128)(2,1)} %get-tuple-element.39.refs_0_), channel_id=1, source_target_pairs={{0,1},{1,0},{2,3},{3,2},{4,5},{5,4},{6,7},{7,6}} | collective-permute-start | bytes 17301512 | tf_op jit(solution)/shard_map/ppermute | solution.py:317
  310.3 108.6 %copy-start.1 = (f32[8,512]{1,0:T(8,128)S(1)}, f32[8,512]{1,0:T(8,128)}, u32[]{:S(2)}) copy-start(f32[8,512]{1,0:T(8,128)} %get-tuple-element.34.refs_0_) | copy-start | bytes 49156
  310.3 109.2 %copy-start.2 = (f32[8,512]{1,0:T(8,128)S(1)}, f32[8,512]{1,0:T(8,128)}, u32[]{:S(2)}) copy-start(f32[8,512]{1,0:T(8,128)} %get-tuple-element.36.refs_2_) | copy-start | bytes 49156
  310.3 111.7 %copy-start = (f32[8,512]{1,0:T(8,128)S(1)}, f32[8,512]{1,0:T(8,128)}, u32[]{:S(2)}) copy-start(f32[8,512]{1,0:T(8,128)} %get-tuple-element.37.refs_2_) | copy-start | bytes 49156
  413.8 192.3 %collective-permute-start.3 = (bf16[2048,1408]{1,0:T(8,128)(2,1)}, bf16[2048,1408]{1,0:T(8,128)(2,1)}, u32[]{:S(2)}, u32[]{:S(2)}) collective-permute-start(bf16[2048,1408]{1,0:T(8,128)(2,1)} %get-tuple-element.44.refs_0_), channel_id=1, source_target_pairs={{0,1},{1,0},{2,3},{3,2},{4,5},{5,4},{6,7},{7,6}} | collective-permute-start | bytes 17301512 | tf_op jit(solution)/shard_map/ppermute | solution.py:317
  413.9 97.5 %collective-permute-start.15 = (bf16[704,3072]{1,0:T(8,128)(2,1)}, bf16[704,3072]{1,0:T(8,128)(2,1)}, u32[]{:S(2)}, u32[]{:S(2)}) collective-permute-start(bf16[704,3072]{1,0:T(8,128)(2,1)} %get-tuple-element.54), channel_id=1, source_target_pairs={{0,2},{2,0},{4,6},{6,4},{1,3},{3,1},{5,7},{7,5}} | collective-permute-start | bytes 12976136 | tf_op jit(solution)/shard_map/ppermute | solution.py:315
  416.8 96.6 %collective-permute-start.32 = (bf16[1408,1536]{1,0:T(8,128)(2,1)}, bf16[1408,1536]{1,0:T(8,128)(2,1)}, u32[]{:S(2)}, u32[]{:S(2)}) collective-permute-start(bf16[1408,1536]{1,0:T(8,128)(2,1)} %get-tuple-element.64), channel_id=1, source_target_pairs={{0,4},{2,6},{4,0},{6,2},{1,5},{3,7},{5,1},{7,3}} | collective-permute-start | bytes 12976136 | tf_op jit(solution)/shard_map/ppermute | solution.py:316
  418.3 185.7 %collective-permute-start.16 = (bf16[704,3072]{1,0:T(8,128)(2,1)}, bf16[704,3072]{1,0:T(8,128)(2,1)}, u32[]{:S(2)}, u32[]{:S(2)}) collective-permute-start(bf16[704,3072]{1,0:T(8,128)(2,1)} %get-tuple-element.55), channel_id=1, source_target_pairs={{0,2},{2,0},{4,6},{6,4},{1,3},{3,1},{5,7},{7,5}} | collective-permute-start | bytes 12976136 | tf_op jit(solution)/shard_map/ppermute | solution.py:315
  426.4 393.9 %collective-permute-start.33 = (bf16[1408,1536]{1,0:T(8,128)(2,1)}, bf16[1408,1536]{1,0:T(8,128)(2,1)}, u32[]{:S(2)}, u32[]{:S(2)}) collective-permute-start(bf16[1408,1536]{1,0:T(8,128)(2,1)} %get-tuple-element.65), channel_id=1, source_target_pairs={{0,4},{2,6},{4,0},{6,2},{1,5},{3,7},{5,1},{7,3}} | collective-permute-start | bytes 12976136 | tf_op jit(solution)/shard_map/ppermute | solution.py:316
  511.3 323.3 %collective-permute-start.9 = (bf16[704,3072]{1,0:T(8,128)(2,1)}, bf16[704,3072]{1,0:T(8,128)(2,1)}, u32[]{:S(2)}, u32[]{:S(2)}) collective-permute-start(bf16[704,3072]{1,0:T(8,128)(2,1)} %get-tuple-element.50), channel_id=1, source_target_pairs={{0,2},{2,0},{4,6},{6,4},{1,3},{3,1},{5,7},{7,5}} | collective-permute-start | bytes 12976136 | tf_op jit(solution)/shard_map/ppermute | solution.py:315
  513.4 342.6 %collective-permute-start.26 = (bf16[1408,1536]{1,0:T(8,128)(2,1)}, bf16[1408,1536]{1,0:T(8,128)(2,1)}, u32[]{:S(2)}, u32[]{:S(2)}) collective-permute-start(bf16[1408,1536]{1,0:T(8,128)(2,1)} %get-tuple-element.60), channel_id=1, source_target_pairs={{0,4},{2,6},{4,0},{6,2},{1,5},{3,7},{5,1},{7,3}} | collective-permute-start | bytes 12976136 | tf_op jit(solution)/shard_map/ppermute | solution.py:316
  604.0 241.4 %collective-permute-start.10 = (bf16[704,3072]{1,0:T(8,128)(2,1)}, bf16[704,3072]{1,0:T(8,128)(2,1)}, u32[]{:S(2)}, u32[]{:S(2)}) collective-permute-start(bf16[704,3072]{1,0:T(8,128)(2,1)} %get-tuple-element.51), channel_id=1, source_target_pairs={{0,2},{2,0},{4,6},{6,4},{1,3},{3,1},{5,7},{7,5}} | collective-permute-start | bytes 12976136 | tf_op jit(solution)/shard_map/ppermute | solution.py:315
  606.1 260.0 %collective-permute-start.27 = (bf16[1408,1536]{1,0:T(8,128)(2,1)}, bf16[1408,1536]{1,0:T(8,128)(2,1)}, u32[]{:S(2)}, u32[]{:S(2)}) collective-permute-start(bf16[1408,1536]{1,0:T(8,128)(2,1)} %get-tuple-element.61), channel_id=1, source_target_pairs={{0,4},{2,6},{4,0},{6,2},{1,5},{3,7},{5,1},{7,3}} | collective-permute-start | bytes 12976136 | tf_op jit(solution)/shard_map/ppermute | solution.py:316
  607.6 80.3 %copy-start.3 = (f32[8,512]{1,0:T(8,128)S(1)}, f32[8,512]{1,0:T(8,128)}, u32[]{:S(2)}) copy-start(f32[8,512]{1,0:T(8,128)} %get-tuple-element.42.refs_2_) | copy-start | bytes 49156
  820.3 212.2 %collective-permute-start.4 = (bf16[704,3072]{1,0:T(8,128)(2,1)}, bf16[704,3072]{1,0:T(8,128)(2,1)}, u32[]{:S(2)}, u32[]{:S(2)}) collective-permute-start(bf16[704,3072]{1,0:T(8,128)(2,1)} %add_convert_fusion.1), channel_id=1, source_target_pairs={{0,2},{2,0},{4,6},{6,4},{1,3},{3,1},{5,7},{7,5}} | collective-permute-start | bytes 12976136 | tf_op jit(solution)/shard_map/ppermute | solution.py:315
  822.6 24.5 %slice-start.3 = ((s8[8650752]{0:T(1024)(128)(4,1)}), s8[262144]{0:T(1024)(128)(4,1)S(1)}, s32[]{:S(2)}) async-start(s8[8650752]{0:T(1024)(128)(4,1)} %bitcast.51), calls=%async_computation.3 | async-start | bytes 524288
  822.6 24.5 %slice-start.4 = ((s8[8650752]{0:T(1024)(128)(4,1)}), s8[4194304]{0:T(1024)(128)(4,1)S(1)}, s32[]{:S(2)}) async-start(s8[8650752]{0:T(1024)(128)(4,1)} %bitcast.51), calls=%async_computation.4 | async-start | bytes 8388608
  834.6 207.2 %collective-permute-start.21 = (bf16[1408,1536]{1,0:T(8,128)(2,1)}, bf16[1408,1536]{1,0:T(8,128)(2,1)}, u32[]{:S(2)}, u32[]{:S(2)}) collective-permute-start(bf16[1408,1536]{1,0:T(8,128)(2,1)} %add_convert_fusion), channel_id=1, source_target_pairs={{0,4},{2,6},{4,0},{6,2},{1,5},{3,7},{5,1},{7,3}} | collective-permute-start | bytes 12976136 | tf_op jit(solution)/shard_map/ppermute | solution.py:316
  835.0 12.1 slice-start.5
  845.4 132.1 %collective-permute-start.17 = (bf16[352,3072]{1,0:T(8,128)(2,1)}, bf16[352,3072]{1,0:T(8,128)(2,1)}, u32[]{:S(2)}, u32[]{:S(2)}) collective-permute-start(bf16[352,3072]{1,0:T(8,128)(2,1)} %add_convert_fusion.9), channel_id=1, source_target_pairs={{0,4},{2,6},{4,0},{6,2},{1,5},{3,7},{5,1},{7,3}} | collective-permute-start | bytes 6488072 | tf_op jit(solution)/shard_map/ppermute | solution.py:316
  856.0 164.7 %collective-permute-start.11 = (bf16[352,3072]{1,0:T(8,128)(2,1)}, bf16[352,3072]{1,0:T(8,128)(2,1)}, u32[]{:S(2)}, u32[]{:S(2)}) collective-permute-start(bf16[352,3072]{1,0:T(8,128)(2,1)} %add_convert_fusion.11), channel_id=1, source_target_pairs={{0,4},{2,6},{4,0},{6,2},{1,5},{3,7},{5,1},{7,3}} | collective-permute-start | bytes 6488072 | tf_op jit(solution)/shard_map/ppermute | solution.py:316
  856.3 121.2 %slice-start = ((s8[8650752]{0:T(1024)(128)(4,1)}), s8[4194304]{0:T(1024)(128)(4,1)S(1)}, s32[]{:S(2)}) async-start(s8[8650752]{0:T(1024)(128)(4,1)} %bitcast.49), calls=%async_computation | async-start | bytes 8388608
  856.3 121.2 %slice-start.1 = ((s8[8650752]{0:T(1024)(128)(4,1)}), s8[4194304]{0:T(1024)(128)(4,1)S(1)}, s32[]{:S(2)}) async-start(s8[8650752]{0:T(1024)(128)(4,1)} %bitcast.49), calls=%async_computation.1 | async-start | bytes 8388608
  866.1 187.1 %collective-permute-start.34 = (bf16[1408,768]{1,0:T(8,128)(2,1)S(1)}, bf16[1408,768]{1,0:T(8,128)(2,1)}, u32[]{:S(2)}, u32[]{:S(2)}) collective-permute-start(bf16[1408,768]{1,0:T(8,128)(2,1)S(1)} %add_convert_fusion.3), channel_id=1, source_target_pairs={{0,2},{2,0},{4,6},{6,4},{1,3},{3,1},{5,7},{7,5}} | collective-permute-start | bytes 6488072 | tf_op jit(solution)/shard_map/ppermute | solution.py:315
  867.7 109.9 %slice-start.2 = ((s8[8650752]{0:T(1024)(128)(4,1)}), s8[262144]{0:T(1024)(128)(4,1)S(1)}, s32[]{:S(2)}) async-start(s8[8650752]{0:T(1024)(128)(4,1)} %bitcast.49), calls=%async_computation.2 | async-start | bytes 524288
  977.5 75.9 %collective-permute-start.28 = (bf16[1408,768]{1,0:T(8,128)(2,1)S(1)}, bf16[1408,768]{1,0:T(8,128)(2,1)}, u32[]{:S(2)}, u32[]{:S(2)}) collective-permute-start(bf16[1408,768]{1,0:T(8,128)(2,1)S(1)} %add_convert_fusion.5), channel_id=1, source_target_pairs={{0,2},{2,0},{4,6},{6,4},{1,3},{3,1},{5,7},{7,5}} | collective-permute-start | bytes 6488072 | tf_op jit(solution)/shard_map/ppermute | solution.py:315
  1020.7 55.4 %collective-permute-start.20 = (bf16[352,3072]{1,0:T(8,128)(2,1)S(1)}, bf16[352,3072]{1,0:T(8,128)(2,1)}, u32[]{:S(2)}, u32[]{:S(2)}) collective-permute-start(bf16[352,3072]{1,0:T(8,128)(2,1)S(1)} %add_convert_fusion.8.piece_ref), channel_id=1, source_target_pairs={{0,2},{2,0},{4,6},{6,4},{1,3},{3,1},{5,7},{7,5}} | collective-permute-start | bytes 6488072 | tf_op jit(solution)/shard_map/ppermute | solution.py:315
  1032.5 50.0 %collective-permute-start.18 = (bf16[352,3072]{1,0:T(8,128)(2,1)S(1)}, bf16[352,3072]{1,0:T(8,128)(2,1)}, u32[]{:S(2)}, u32[]{:S(2)}) collective-permute-start(bf16[352,3072]{1,0:T(8,128)(2,1)S(1)} %add_convert_fusion.8.piece_ref), channel_id=1, source_target_pairs={{0,4},{2,6},{4,0},{6,2},{1,5},{3,7},{5,1},{7,3}} | collective-permute-start | bytes 6488072 | tf_op jit(solution)/shard_map/ppermute | solution.py:316
  1041.8 75.2 %collective-permute-start.14 = (bf16[352,3072]{1,0:T(8,128)(2,1)}, bf16[352,3072]{1,0:T(8,128)(2,1)}, u32[]{:S(2)}, u32[]{:S(2)}) collective-permute-start(bf16[352,3072]{1,0:T(8,128)(2,1)} %add_convert_fusion.10.piece_ref), channel_id=1, source_target_pairs={{0,2},{2,0},{4,6},{6,4},{1,3},{3,1},{5,7},{7,5}} | collective-permute-start | bytes 6488072 | tf_op jit(solution)/shard_map/ppermute | solution.py:315
  1053.2 75.7 %collective-permute-start.5 = (bf16[352,3072]{1,0:T(8,128)(2,1)}, bf16[352,3072]{1,0:T(8,128)(2,1)}, u32[]{:S(2)}, u32[]{:S(2)}) collective-permute-start(bf16[352,3072]{1,0:T(8,128)(2,1)} %add_convert_fusion.13), channel_id=1, source_target_pairs={{0,4},{2,6},{4,0},{6,2},{1,5},{3,7},{5,1},{7,3}} | collective-permute-start | bytes 6488072 | tf_op jit(solution)/shard_map/ppermute | solution.py:316
  1053.4 110.0 %collective-permute-start.22 = (bf16[1408,768]{1,0:T(8,128)(2,1)}, bf16[1408,768]{1,0:T(8,128)(2,1)}, u32[]{:S(2)}, u32[]{:S(2)}) collective-permute-start(bf16[1408,768]{1,0:T(8,128)(2,1)} %add_convert_fusion.7), channel_id=1, source_target_pairs={{0,2},{2,0},{4,6},{6,4},{1,3},{3,1},{5,7},{7,5}} | collective-permute-start | bytes 6488072 | tf_op jit(solution)/shard_map/ppermute | solution.py:315
  1076.1 108.3 %collective-permute-start.12 = (bf16[352,3072]{1,0:T(8,128)(2,1)}, bf16[352,3072]{1,0:T(8,128)(2,1)}, u32[]{:S(2)}, u32[]{:S(2)}) collective-permute-start(bf16[352,3072]{1,0:T(8,128)(2,1)} %add_convert_fusion.10.piece_ref), channel_id=1, source_target_pairs={{0,4},{2,6},{4,0},{6,2},{1,5},{3,7},{5,1},{7,3}} | collective-permute-start | bytes 6488072 | tf_op jit(solution)/shard_map/ppermute | solution.py:316
  1082.5 127.2 %collective-permute-start.35 = (bf16[1408,768]{1,0:T(8,128)(2,1)}, bf16[1408,768]{1,0:T(8,128)(2,1)}, u32[]{:S(2)}, u32[]{:S(2)}) collective-permute-start(bf16[1408,768]{1,0:T(8,128)(2,1)} %add_convert_fusion.2.piece_ref), channel_id=1, source_target_pairs={{0,2},{2,0},{4,6},{6,4},{1,3},{3,1},{5,7},{7,5}} | collective-permute-start | bytes 6488072 | tf_op jit(solution)/shard_map/ppermute | solution.py:315
  1117.0 139.0 %collective-permute-start.29 = (bf16[1408,768]{1,0:T(8,128)(2,1)}, bf16[1408,768]{1,0:T(8,128)(2,1)}, u32[]{:S(2)}, u32[]{:S(2)}) collective-permute-start(bf16[1408,768]{1,0:T(8,128)(2,1)} %add_convert_fusion.4.piece_ref), channel_id=1, source_target_pairs={{0,2},{2,0},{4,6},{6,4},{1,3},{3,1},{5,7},{7,5}} | collective-permute-start | bytes 6488072 | tf_op jit(solution)/shard_map/ppermute | solution.py:315
  1128.9 128.6 %collective-permute-start.37 = (bf16[1408,768]{1,0:T(8,128)(2,1)}, bf16[1408,768]{1,0:T(8,128)(2,1)}, u32[]{:S(2)}, u32[]{:S(2)}) collective-permute-start(bf16[1408,768]{1,0:T(8,128)(2,1)} %add_convert_fusion.2.piece_ref), channel_id=1, source_target_pairs={{0,4},{2,6},{4,0},{6,2},{1,5},{3,7},{5,1},{7,3}} | collective-permute-start | bytes 6488072 | tf_op jit(solution)/shard_map/ppermute | solution.py:316
  1163.4 104.5 %collective-permute-start.31 = (bf16[1408,768]{1,0:T(8,128)(2,1)}, bf16[1408,768]{1,0:T(8,128)(2,1)}, u32[]{:S(2)}, u32[]{:S(2)}) collective-permute-start(bf16[1408,768]{1,0:T(8,128)(2,1)} %add_convert_fusion.4.piece_ref), channel_id=1, source_target_pairs={{0,4},{2,6},{4,0},{6,2},{1,5},{3,7},{5,1},{7,3}} | collective-permute-start | bytes 6488072 | tf_op jit(solution)/shard_map/ppermute | solution.py:316
  1184.4 118.0 %collective-permute-start.19 = (bf16[352,3072]{1,0:T(8,128)(2,1)}, bf16[352,3072]{1,0:T(8,128)(2,1)}, u32[]{:S(2)}, u32[]{:S(2)}) collective-permute-start(bf16[352,3072]{1,0:T(8,128)(2,1)} %collective-permute-done.18.piece_ref), channel_id=1, source_target_pairs={{0,2},{2,0},{4,6},{6,4},{1,3},{3,1},{5,7},{7,5}} | collective-permute-start | bytes 6488072 | tf_op jit(solution)/shard_map/ppermute | solution.py:315
  1209.7 104.5 %collective-permute-start.36 = (bf16[1408,768]{1,0:T(8,128)(2,1)}, bf16[1408,768]{1,0:T(8,128)(2,1)}, u32[]{:S(2)}, u32[]{:S(2)}) collective-permute-start(bf16[1408,768]{1,0:T(8,128)(2,1)} %collective-permute-done.35.piece_ref), channel_id=1, source_target_pairs={{0,4},{2,6},{4,0},{6,2},{1,5},{3,7},{5,1},{7,3}} | collective-permute-start | bytes 6488072 | tf_op jit(solution)/shard_map/ppermute | solution.py:316
  1256.1 104.5 %collective-permute-start.30 = (bf16[1408,768]{1,0:T(8,128)(2,1)}, bf16[1408,768]{1,0:T(8,128)(2,1)}, u32[]{:S(2)}, u32[]{:S(2)}) collective-permute-start(bf16[1408,768]{1,0:T(8,128)(2,1)} %collective-permute-done.29.piece_ref), channel_id=1, source_target_pairs={{0,4},{2,6},{4,0},{6,2},{1,5},{3,7},{5,1},{7,3}} | collective-permute-start | bytes 6488072 | tf_op jit(solution)/shard_map/ppermute | solution.py:316
  1257.5 149.4 %collective-permute-start.6 = (bf16[352,3072]{1,0:T(8,128)(2,1)}, bf16[352,3072]{1,0:T(8,128)(2,1)}, u32[]{:S(2)}, u32[]{:S(2)}) collective-permute-start(bf16[352,3072]{1,0:T(8,128)(2,1)} %add_convert_fusion.12.piece_ref), channel_id=1, source_target_pairs={{0,4},{2,6},{4,0},{6,2},{1,5},{3,7},{5,1},{7,3}} | collective-permute-start | bytes 6488072 | tf_op jit(solution)/shard_map/ppermute | solution.py:316
  1267.9 140.3 %collective-permute-start.23 = (bf16[1408,768]{1,0:T(8,128)(2,1)}, bf16[1408,768]{1,0:T(8,128)(2,1)}, u32[]{:S(2)}, u32[]{:S(2)}) collective-permute-start(bf16[1408,768]{1,0:T(8,128)(2,1)} %add_convert_fusion.6.piece_ref), channel_id=1, source_target_pairs={{0,2},{2,0},{4,6},{6,4},{1,3},{3,1},{5,7},{7,5}} | collective-permute-start | bytes 6488072 | tf_op jit(solution)/shard_map/ppermute | solution.py:315
  1302.4 203.8 %collective-permute-start.13 = (bf16[352,3072]{1,0:T(8,128)(2,1)}, bf16[352,3072]{1,0:T(8,128)(2,1)}, u32[]{:S(2)}, u32[]{:S(2)}) collective-permute-start(bf16[352,3072]{1,0:T(8,128)(2,1)} %collective-permute-done.12.piece_ref), channel_id=1, source_target_pairs={{0,2},{2,0},{4,6},{6,4},{1,3},{3,1},{5,7},{7,5}} | collective-permute-start | bytes 6488072 | tf_op jit(solution)/shard_map/ppermute | solution.py:315
  1314.2 220.5 %collective-permute-start.8 = (bf16[352,3072]{1,0:T(8,128)(2,1)}, bf16[352,3072]{1,0:T(8,128)(2,1)}, u32[]{:S(2)}, u32[]{:S(2)}) collective-permute-start(bf16[352,3072]{1,0:T(8,128)(2,1)} %add_convert_fusion.12.piece_ref), channel_id=1, source_target_pairs={{0,2},{2,0},{4,6},{6,4},{1,3},{3,1},{5,7},{7,5}} | collective-permute-start | bytes 6488072 | tf_op jit(solution)/shard_map/ppermute | solution.py:315
  1360.6 167.6 %collective-permute-start.25 = (bf16[1408,768]{1,0:T(8,128)(2,1)}, bf16[1408,768]{1,0:T(8,128)(2,1)}, u32[]{:S(2)}, u32[]{:S(2)}) collective-permute-start(bf16[1408,768]{1,0:T(8,128)(2,1)} %add_convert_fusion.6.piece_ref), channel_id=1, source_target_pairs={{0,4},{2,6},{4,0},{6,2},{1,5},{3,7},{5,1},{7,3}} | collective-permute-start | bytes 6488072 | tf_op jit(solution)/shard_map/ppermute | solution.py:316
  1406.9 139.5 %collective-permute-start.7 = (bf16[352,3072]{1,0:T(8,128)(2,1)}, bf16[352,3072]{1,0:T(8,128)(2,1)}, u32[]{:S(2)}, u32[]{:S(2)}) collective-permute-start(bf16[352,3072]{1,0:T(8,128)(2,1)} %collective-permute-done.6.piece_ref), channel_id=1, source_target_pairs={{0,2},{2,0},{4,6},{6,4},{1,3},{3,1},{5,7},{7,5}} | collective-permute-start | bytes 6488072 | tf_op jit(solution)/shard_map/ppermute | solution.py:315
  1408.3 131.6 %collective-permute-start.24 = (bf16[1408,768]{1,0:T(8,128)(2,1)}, bf16[1408,768]{1,0:T(8,128)(2,1)}, u32[]{:S(2)}, u32[]{:S(2)}) collective-permute-start(bf16[1408,768]{1,0:T(8,128)(2,1)} %collective-permute-done.23.piece_ref), channel_id=1, source_target_pairs={{0,4},{2,6},{4,0},{6,2},{1,5},{3,7},{5,1},{7,3}} | collective-permute-start | bytes 6488072 | tf_op jit(solution)/shard_map/ppermute | solution.py:316

commit v2 on v1

--- a/solution.py
+++ b/solution.py
@@ -10,9 +10,9 @@
 
 INV_SQRT2 = 0.7071067811865476
 INV_SQRT_2PI = 0.3989422804014327
+LOG2_E = 1.4426950408889634
 F_BLOCK = 512
-T_CHUNK = 512
-IN_CHUNK = 128
+T_CHUNK = 256
 IN_SLOTS = 4
 ROW_STEPS = 2
 VMEM_LIMIT = 66_500_000
@@ -40,90 +40,106 @@
         g1k_hbm, g1s_hbm, g2k_hbm, g2s_hbm, dx_hbm = [refs.pop(0) for _ in range(5)]
     dzo_hbm = None if (first or last) else refs.pop(0)
     ss_ref = refs.pop(0)
-    x_t, dz, dz_t, dh, h, bh, x_st = [refs.pop(0) for _ in range(7)]
+    x_t, dz, dz_t, dh, h, x_st = [refs.pop(0) for _ in range(6)]
     p_st, q_st = (None, None) if first else (refs.pop(0), refs.pop(0))
     if last:
         g1_st, g2_st = refs.pop(0), refs.pop(0)
     else:
         acc, g1k_st, g1s_st, g2k_st, g2s_st = [refs.pop(0) for _ in range(5)]
-    in_sem, out_sem = refs.pop(0), refs.pop(0)
+    in_sem, out_sem, io_sem = refs.pop(0), refs.pop(0), refs.pop(0)
 
     step = pl.program_id(0)
     layer, example, x_pos, y_pos = sc_ref[0], sc_ref[1], sc_ref[2], sc_ref[3]
     n_tok, d_model = dz.shape
     half_d = d_model // 2
     n_t = n_tok // T_CHUNK
-    n_in = n_tok // IN_CHUNK
 
     def in_copies(c):
-        slot = lax.rem(c, IN_SLOTS)
-        rows = pl.ds(pl.multiple_of(c * IN_CHUNK, IN_CHUNK), IN_CHUNK)
+        slot = c % IN_SLOTS
+        rows = pl.ds(c * T_CHUNK, T_CHUNK)
         dz_src = dz_hbm.at[rows, :] if last else dz_hbm.at[example, rows, :]
-        pairs = [(x_hbm.at[layer, example, rows, :], x_st.at[slot]), (dz_src, dz.at[rows, :])]
+        pairs = [(dz_src, dz.at[rows, :])]
         if not first:
             pairs += [(p_hbm.at[rows, :], p_st.at[slot]), (q_hbm.at[rows, :], q_st.at[slot])]
+        pairs += [(x_hbm.at[layer, example, rows, :], x_st.at[slot])]
         return [pltpu.make_async_copy(a, b, in_sem.at[k, slot]) for k, (a, b) in enumerate(pairs)]
+
+    def front(load):
+        for s in range(n_t + (0 if last else 1)):
+            rows = pl.ds(s * T_CHUNK, T_CHUNK)
+            if load and s < n_t:
+                if s + IN_SLOTS - 1 < n_t:
+                    for cp in in_copies(s + IN_SLOTS - 1):
+                        cp.start()
+                for cp in in_copies(s):
+                    cp.wait()
+                slot = s % IN_SLOTS
+                z = dz[rows, :]
+                if not first:
+                    z = (z.astype(F32) + (p_st[slot].astype(F32) + q_st[slot].astype(F32))).astype(BF16)
+                    dz[rows, :] = z
+                dz_t[:, rows] = z.T
+                x_t[:, rows] = x_st[slot].T
+            if s < n_t:
+                u = u_ref[0, 0, rows, :].astype(F32)
+                t = u * INV_SQRT2
+                cdf = 0.5 * lax.erf(t) + 0.5
+                h[rows, :] = (u * cdf).astype(BF16)
+                slope = cdf + (t * (INV_SQRT_2PI / INV_SQRT2)) * jnp.exp2((t * t) * -LOG2_E)
+                dh[rows, :] = (slope * dot_nt(dz[rows, :], w2_ref[0])).astype(BF16)
+            if s >= 1 and not last:
+                rows = pl.ds((s - 1) * T_CHUNK, T_CHUNK)
+                part = dot_nt(dh[rows, :], w1_ref[0])
+                acc[rows, :] = part if load else acc[rows, :] + part
 
     @pl.when(step == 0)
     def _():
         for c in range(IN_SLOTS - 1):
             for cp in in_copies(c):
                 cp.start()
-        if not last:
-            acc[...] = jnp.zeros_like(acc)
         ss_ref[...] = jnp.zeros_like(ss_ref)
-
-        def load(c, carry):
-            @pl.when(c + IN_SLOTS - 1 < n_in)
-            def _():
-                for cp in in_copies(c + IN_SLOTS - 1):
-                    cp.start()
-
-            for cp in in_copies(c):
-                cp.wait()
-            slot = lax.rem(c, IN_SLOTS)
-            at = pl.ds(pl.multiple_of(c * IN_CHUNK, IN_CHUNK), IN_CHUNK)
-            x_t[:, at] = x_st[slot].T
-            if first:
-                z = dz[at, :]
-            else:
-                z = (dz[at, :].astype(F32) + (p_st[slot].astype(F32) + q_st[slot].astype(F32))).astype(BF16)
-                dz[at, :] = z
-            dz_t[:, at] = z.T
-            return carry
-
-        lax.fori_loop(0, n_in, load, 0)
+        front(True)
         if dzo_hbm is not None:
-            pltpu.make_async_copy(dz, dzo_hbm, out_sem.at[4]).start()
-
-    for s in range(n_t + (1 if last else 2)):
-        if s < n_t:
-            bh[s % 2] = dot_nt(dz[pl.ds(s * T_CHUNK, T_CHUNK), :], w2_ref[0])
-        if 1 <= s <= n_t:
-            rows = pl.ds((s - 1) * T_CHUNK, T_CHUNK)
-            u = u_ref[0, 0, rows, :].astype(F32)
-            cdf = 0.5 * (1.0 + lax.erf(u * INV_SQRT2))
-            h[rows, :] = (u * cdf).astype(BF16)
-            slope = cdf + u * jnp.exp(-0.5 * u * u) * INV_SQRT_2PI
-            dh[rows, :] = (slope * bh[(s - 1) % 2]).astype(BF16)
-        if s >= 2 and not last:
-            rows = pl.ds((s - 2) * T_CHUNK, T_CHUNK)
-            acc[rows, :] = acc[rows, :] + dot_nt(dh[rows, :], w1_ref[0])
+            pltpu.make_async_copy(dz, dzo_hbm, io_sem.at[0]).start()
+
+    @pl.when(step > 0)
+    def _():
+        front(False)
+
+    if not last:
+        @pl.when(step == n_steps - 1)
+        def _():
+            if dzo_hbm is not None:
+                pltpu.make_async_copy(dz, dzo_hbm, io_sem.at[0]).wait()
+
+            def put(c, carry):
+                rows = pl.ds(pl.multiple_of(c * T_CHUNK, T_CHUNK), T_CHUNK)
+                dz[rows, :] = acc[rows, :].astype(BF16)
+                return carry
+
+            lax.fori_loop(0, n_t, put, 0)
+            pltpu.make_async_copy(dz, dx_hbm, io_sem.at[1]).start()
 
     cols = lambda k: pl.ds(pl.multiple_of(k * F_BLOCK, F_BLOCK), F_BLOCK)
-
-    if last:
-        def out_copies(k):
-            yield pltpu.make_async_copy(g1_st, g1_hbm.at[:, cols(k)], out_sem.at[0]), None
-            yield pltpu.make_async_copy(g2_st, g2_hbm.at[:, cols(k)], out_sem.at[1]), None
-    else:
-        fb = lambda k: lax.rem(k + (n_steps // 2) * (1 - y_pos), n_steps)
-
-        def out_copies(k):
-            yield pltpu.make_async_copy(g1k_st, g1k_hbm.at[:, cols(fb(k))], out_sem.at[0]), None
-            yield pltpu.make_async_copy(g1s_st, g1s_hbm.at[:, cols(fb(k))], out_sem.at[1]), None
-            yield pltpu.make_async_copy(g2s_st, g2s_hbm.at[:, cols(k)], out_sem.at[2]), k < n_steps // 2
-            yield pltpu.make_async_copy(g2k_st, g2k_hbm.at[:, cols(k - n_steps // 2)], out_sem.at[3]), k >= n_steps // 2
+    n_half = n_steps // 2
+
+    def out_copies(k, r):
+        def at(size):
+            return pl.ds(pl.multiple_of(r * size, 16), size)
+
+        half_rows, part_rows = at(half_d), at(half_d // ROW_STEPS)
+        if last:
+            return [
+                (pltpu.make_async_copy(g1_st.at[half_rows, :], g1_hbm.at[half_rows, cols(k)], out_sem.at[0, r]), None),
+                (pltpu.make_async_copy(g2_st.at[half_rows, :], g2_hbm.at[half_rows, cols(k)], out_sem.at[1, r]), None),
+            ]
+        fb = lax.rem(k + n_half * (1 - y_pos), n_steps)
+        return [
+            (pltpu.make_async_copy(g1k_st.at[part_rows, :], g1k_hbm.at[part_rows, cols(fb)], out_sem.at[0, r]), None),
+            (pltpu.make_async_copy(g1s_st.at[part_rows, :], g1s_hbm.at[part_rows, cols(fb)], out_sem.at[1, r]), None),
+            (pltpu.make_async_copy(g2s_st.at[half_rows, :], g2s_hbm.at[half_rows, cols(k)], out_sem.at[2, r]), k < n_half),
+            (pltpu.make_async_copy(g2k_st.at[half_rows, :], g2k_hbm.at[half_rows, cols(k - n_half)], out_sem.at[3, r]), k >= n_half),
+        ]
 
     def run(copies, act):
         for cp, cond in copies:
@@ -134,19 +150,18 @@
 
     @pl.when(step > 0)
     def _():
-        run(out_copies(step - 1), 'wait')
+        for r in range(ROW_STEPS):
+            run(out_copies(step - 1, r), 'wait')
 
     def square(g):
         return jnp.sum((g * g).reshape(g.shape[0] // 8, 8, g.shape[1]), axis=0)
 
     def weight_grads(r, carry):
-        quarter = half_d // ROW_STEPS
-        a = pl.multiple_of(r * quarter, quarter)
-        b = pl.multiple_of(r * quarter + half_d, quarter)
+        part = half_d // ROW_STEPS
+        total = ss_ref[...]
         if last:
-            total = ss_ref[...]
-            for at in (a, b):
-                rows = pl.ds(at, quarter)
+            for at in range(ROW_STEPS):
+                rows = pl.ds(pl.multiple_of(r * half_d + at * part, part), part)
                 g = dot_nn(x_t[rows, :], dh[...])
                 g1_st[rows, :] = g
                 total = total + square(g)
@@ -154,51 +169,33 @@
                 g2_st[rows, :] = g
                 total = total + square(g)
         else:
-            own = pl.multiple_of(r * quarter + x_pos * half_d, quarter)
-            far = pl.multiple_of(r * quarter + (1 - x_pos) * half_d, quarter)
-            rows = pl.ds(a, quarter)
-            g = dot_nn(x_t[pl.ds(own, quarter), :], dh[...])
+            own = pl.multiple_of(r * part + x_pos * half_d, part)
+            far = pl.multiple_of(r * part + (1 - x_pos) * half_d, part)
+            rows = pl.ds(pl.multiple_of(r * part, part), part)
+            g = dot_nn(x_t[pl.ds(own, part), :], dh[...])
             g1k_st[rows, :] = g
-            total = ss_ref[...] + square(g)
-            g = dot_nn(x_t[pl.ds(far, quarter), :], dh[...])
+            total = total + square(g)
+            g = dot_nn(x_t[pl.ds(far, part), :], dh[...])
             g1s_st[rows, :] = g.astype(BF16)
             total = total + square(g)
-            for at in (a, b):
-                rows = pl.ds(at, quarter)
+            for at in range(ROW_STEPS):
+                rows = pl.ds(pl.multiple_of(r * half_d + at * part, part), part)
                 g = dot_nn(dz_t[rows, :], h[...])
                 g2k_st[rows, :] = g
                 g2s_st[rows, :] = g.astype(BF16)
                 total = total + square(g)
         ss_ref[...] = total
+        run(out_copies(step, r), 'start')
         return carry
 
     lax.fori_loop(0, ROW_STEPS, weight_grads, 0)
-    run(out_copies(step), 'start')
 
     @pl.when(step == n_steps - 1)
     def _():
+        for r in range(ROW_STEPS):
+            run(out_copies(step, r), 'wait')
         if not last:
-            def dx_copy(c):
-                rows = pl.ds(pl.multiple_of(c * IN_CHUNK, IN_CHUNK), IN_CHUNK)
-                slot = lax.rem(c, IN_SLOTS)
-                return pltpu.make_async_copy(x_st.at[slot], dx_hbm.at[rows, :], in_sem.at[0, slot])
-
-            def put(c, carry):
-                @pl.when(c >= IN_SLOTS)
-                def _():
-                    dx_copy(c - IN_SLOTS).wait()
-
-                rows = pl.ds(pl.multiple_of(c * IN_CHUNK, IN_CHUNK), IN_CHUNK)
-                x_st[lax.rem(c, IN_SLOTS)] = acc[rows, :].astype(BF16)
-                dx_copy(c).start()
-                return carry
-
-            lax.fori_loop(0, n_in, put, 0)
-            for c in range(n_in - IN_SLOTS, n_in):
-                dx_copy(c).wait()
-        run(out_copies(step), 'wait')
-        if dzo_hbm is not None:
-            pltpu.make_async_copy(dz, dzo_hbm, out_sem.at[4]).wait()
+            pltpu.make_async_copy(dz, dx_hbm, io_sem.at[1]).wait()
 
 
 def run_layer(kind, place, layer, example, pre_act, w_in, w_out, block_in, dz, parts, token):
@@ -224,11 +221,10 @@
         pltpu.VMEM((d_model, n_tok), BF16),
         pltpu.VMEM((n_tok, F_BLOCK), BF16),
         pltpu.VMEM((n_tok, F_BLOCK), BF16),
-        pltpu.VMEM((2, T_CHUNK, F_BLOCK), F32),
-        pltpu.VMEM((IN_SLOTS, IN_CHUNK, d_model), BF16),
+        pltpu.VMEM((IN_SLOTS, T_CHUNK, d_model), BF16),
     ]
     if not first:
-        scratch += [pltpu.VMEM((IN_SLOTS, IN_CHUNK, d_model), BF16)] * 2
+        scratch += [pltpu.VMEM((IN_SLOTS, T_CHUNK, d_model), BF16)] * 2
     if last:
         outs = [sds((d_model, d_ff), F32), sds((d_model, d_ff), F32)]
         scratch += [pltpu.VMEM((d_model, F_BLOCK), F32)] * 2
@@ -245,7 +241,9 @@
             pltpu.VMEM((half_d, F_BLOCK), F32), pltpu.VMEM((half_d, F_BLOCK), BF16),
             pltpu.VMEM((d_model, F_BLOCK), F32), pltpu.VMEM((d_model, F_BLOCK), BF16),
         ]
-    scratch += [pltpu.SemaphoreType.DMA((4, IN_SLOTS)), pltpu.SemaphoreType.DMA((5,))]
+    scratch += [
+        pltpu.SemaphoreType.DMA((4, IN_SLOTS)), pltpu.SemaphoreType.DMA((4, ROW_STEPS)), pltpu.SemaphoreType.DMA((2,)),
+    ]
     out_specs = [pl.BlockSpec(memory_space=ANY)] * len(outs)
     outs.append(sds((8, F_BLOCK), F32))
     out_specs.append(pl.BlockSpec((8, F_BLOCK), lambda j, sc: (0, 0)))
@@ -341,11 +339,9 @@
                         d_z[ex] = res[5]
 
         part_sq = jnp.stack([sum(s) for s in sums])
-        part_all = lax.dynamic_update_slice(jnp.zeros((batch_total,), F32), part_sq, (dp * local_batch,))
-        sq_norm = lax.psum(part_all, ('dp', 'tp'))
-        clip = jnp.minimum(1.0, clip_norm / jnp.sqrt(sq_norm))
-        at = lambda d: [lax.dynamic_index_in_dim(clip, d * local_batch + k, keepdims=False) for k in range(local_batch)]
-        c_own, c_x, c_y = at(dp), at(dp ^ 1), at(dp ^ 2)
+        clip = jnp.minimum(1.0, clip_norm / jnp.sqrt(lax.psum(part_sq, 'tp')))
+        clip_x, clip_y = over_x(clip), over_y(clip)
+        c_own, c_x, c_y = [[v[k] for k in range(local_batch)] for v in (clip, clip_x, clip_y)]
         mix = lambda cs, vs: sum(c * v.astype(F32) for c, v in zip(cs, vs))
         coef = jnp.stack([noise_mult * clip_norm, jnp.float32(1.0 / batch_total)])
 
@@ -354,28 +350,30 @@
         noise_out4 = noise_out.reshape(n_layers, 4, d_ff // 4, d_model)
         grad_in = grad_out = None
 
-        def half(layer, which, axis, pos, c_far, far_parts, part_pos):
-            own = [grads[layer][k][which] for k in range(local_batch)]
+        def quarter(layer, which, half_pos, pos):
+            vals = [grads[layer][k][which] for k in range(local_batch)]
             if layer == 0:
-                own = [cut(v, axis, pos) for v in own]
-            vals = [cut(v, axis, part_pos) for v in own]
-            res = mix(c_own, vals)
-            fp = [cut(v, axis, part_pos) for v in far_parts]
-            return res + (mix(c_far, fp) if layer else fp[0].astype(F32))
-
-        order = [2, 1, 0]
-        last_far = [
-            (over_x(mix(c_own, [cut(grads[0][k][0], 0, 1 - x_pos) for k in range(local_batch)]).astype(BF16)),),
-            (over_y(mix(c_own, [cut(grads[0][k][1], 1, 1 - y_pos) for k in range(local_batch)]).astype(BF16)),),
-        ]
-        for layer in order:
-            far1 = [far[layer][k][0] for k in range(local_batch)] if layer else last_far[0]
-            far2 = [far[layer][k][1] for k in range(local_batch)] if layer else last_far[1]
-            send1 = half(layer, 0, 0, x_pos, c_x, far1, 1 - y_pos).astype(BF16)
-            send2 = half(layer, 1, 1, y_pos, c_y, far2, 1 - x_pos).astype(BF16)
-            got1, got2 = over_y(send1), over_x(send2)
-            own1 = (half(layer, 0, 0, x_pos, c_x, far1, y_pos) + got1.astype(F32)).astype(BF16)
-            own2 = (half(layer, 1, 1, y_pos, c_y, far2, x_pos) + got2.astype(F32)).astype(BF16)
+                vals = [cut(v, which, half_pos) for v in vals]
+            return mix(c_own, [cut(v, which, pos) for v in vals])
+
+        far_last = {}
+        for first_send in (True, False):
+            for which, over, half_pos, pos in ((0, over_x, 1 - x_pos, y_pos), (1, over_y, 1 - y_pos, x_pos)):
+                at = 1 - pos if first_send else pos
+                far_last[which, first_send] = over(quarter(0, which, half_pos, at).astype(BF16))
+
+        def pair_sum(layer, which, half_pos, pos, to_send):
+            at = 1 - pos if to_send else pos
+            res = quarter(layer, which, half_pos, at)
+            if layer == 0:
+                return res + far_last[which, to_send].astype(F32)
+            return res + mix(c_y if which else c_x, [cut(far[layer][k][which], which, at) for k in range(local_batch)])
+
+        for layer in range(n_layers - 1, -1, -1):
+            got1 = over_y(pair_sum(layer, 0, x_pos, y_pos, True).astype(BF16))
+            got2 = over_x(pair_sum(layer, 1, y_pos, x_pos, True).astype(BF16))
+            own1 = (pair_sum(layer, 0, x_pos, y_pos, False) + got1.astype(F32)).astype(BF16)
+            own2 = (pair_sum(layer, 1, y_pos, x_pos, False) + got2.astype(F32)).astype(BF16)
             near1, near2 = over_y(own1), over_x(own2)
             side1, side2 = over_x(own1), over_y(own2)
             diag1, diag2 = over_x(near1), over_y(near2)

time: 1560 us -> 1520 us (0.974)
  blocking collectives: 117 us -> 2.68 us
  waiting for transfers between devices: 526 us -> 628 us
  Pallas kernels: 710 us -> 667 us
    psum x1, blocking collectives: 117 us -> 2.68 us  [local_step(): clip = jnp.minimum(1.0, clip_norm / jnp.sqrt(lax.psum(part_sq, 'tp')))]
    ppermute x17 -> x19, waiting for transfers between devices: 263 us -> 340 us  [local_step(): over_x = lambda v: lax.ppermute(v, 'dp', swap_x)]
    pallas_call x6, Pallas kernels: 570 us -> 528 us  [run_layer(): pl.pallas_call(functools.partial(layer_kernel, first, last, n_steps), out...]
    ppermute x17 -> x19, waiting for transfers between devices: 263 us -> 288 us  [local_step(): over_y = lambda v: lax.ppermute(v, 'dp', swap_y)]
  transfers between devices with their start and end apart: 38 -> 42, of which waited for: 15 -> 20; matrix products, arithmetic and copies ran while one was open for 10% -> 10% of each run, Pallas kernels for 39% -> 38%
where the time goes in v2:
time: 1520 us; the launch traced here: 1510 us
  Pallas kernels  667 us (44%)
  waiting for transfers between devices  628 us (41%)
  other arithmetic  154 us (10%)
  starting transfers between devices  45.7 us (3%)
    pallas_call x6, Pallas kernels, run_layer(): pl.pallas_call(functools.partial(layer_kernel, first, last, n_steps), out...  528 us
    ppermute x19, waiting for transfers between devices, local_step(): over_x = lambda v: lax.ppermute(v, 'dp', swap_x)  340 us
    ppermute x19, waiting for transfers between devices, local_step(): over_y = lambda v: lax.ppermute(v, 'dp', swap_y)  288 us
    pallas_call x24, Pallas kernels, put_piece(): pl.pallas_call(put_out_kernel if transposed else put_in_kernel, out_shape...  139 us
    convert_element_type x3, other arithmetic, local_step(): (pair_sum(layer, 1, y_pos, x_pos, False) + got2.astype(F32)).astype(BF16)  31.1 us
  transfers between devices with their start and end apart: 42, of which 20 were waited for; matrix products, arithmetic and copies ran while one was open for 10% of the time, Pallas kernels for 38%

profile of v2, /device:TPU:0, one launch (start us, length us, event | category | flops | bytes accessed | tf_op | source)
XLA Modules:
  0.0 1509.3 jit_solution(13062235968675333197)
XLA Ops:
  1.9 92.6 %shard_map.104 = (f32[704,3072]{1,0:T(8,128)}, bf16[704,3072]{1,0:T(8,128)(2,1)}, f32[1408,1536]{1,0:T(8,128)}, bf16[1408,1536]{1,0:T(8,128)(2,1)}, bf16[2048,1408]{1,0:T(8,128)(2,1)}, /*index=5*/f32[8,512]{1,0:T(8,128)}) custom-call(s32[4]{0:T(128)} %get-tuple-element.76.sc_ref, bf16[3,2,2048,3072]{3,2,1,0:T(8,128)(2,1)} %u_ref.11, ...), custom_call_target="tpu_custom_call" | custom-call | flops 70866960384 | bytes 80000000 | tf_op jit(solution)/shard_map/pallas_call | solution.py:251
  95.4 103.8 %shard_map.105 = (f32[704,3072]{1,0:T(8,128)}, bf16[704,3072]{1,0:T(8,128)(2,1)}, f32[1408,1536]{1,0:T(8,128)}, bf16[1408,1536]{1,0:T(8,128)(2,1)}, bf16[2048,1408]{1,0:T(8,128)(2,1)}, /*index=5*/f32[8,512]{1,0:T(8,128)}) custom-call(s32[4]{0:T(128)} %get-tuple-element.77.sc_ref, bf16[3,2,2048,3072]{3,2,1,0:T(8,128)(2,1)} %u_ref.11, ...), custom_call_target="tpu_custom_call" | custom-call | flops 70866960384 | bytes 80000000 | tf_op jit(solution)/shard_map/pallas_call | solution.py:251
  200.6 93.3 %shard_map.106 = (f32[704,3072]{1,0:T(8,128)}, bf16[704,3072]{1,0:T(8,128)(2,1)}, f32[1408,1536]{1,0:T(8,128)}, bf16[1408,1536]{1,0:T(8,128)(2,1)}, bf16[2048,14...) custom-call(s32[4]{0:T(128)} %fusion.7.sc_ref, bf16[3,2,2048,3072]{3,2,1,0:T(8,128)(2,1)} %u_ref.11, ...), custom_call_target="tpu_custom_call" | custom-call | flops 70866960384 | bytes 80000000 | tf_op jit(solution)/shard_map/pallas_call | solution.py:251
  294.3 93.5 %shard_map.107 = (f32[704,3072]{1,0:T(8,128)}, bf16[704,3072]{1,0:T(8,128)(2,1)}, f32[1408,1536]{1,0:T(8,128)}, bf16[1408,1536]{1,0:T(8,128)(2,1)}, bf16[2048,14...) custom-call(s32[4]{0:T(128)} %add_add_fusion.1.sc_ref, bf16[3,2,2048,3072]{3,2,1,0:T(8,128)(2,1)} %u_ref.11, ...), custom_call_target="tpu_custom_call" | custom-call | flops 70866960384 | bytes 80000000 | tf_op jit(solution)/shard_map/pallas_call | solution.py:251
  401.4 72.3 %shard_map.108 = (f32[1408,3072]{1,0:T(8,128)}, f32[1408,3072]{1,0:T(8,128)}, f32[8,512]{1,0:T(8,128)}) custom-call(s32[4]{0:T(128)} %add_add_fusion.sc_ref, bf16[3,2,2048,3072]{3,2,1,0:T(8,128)(2,1)} %u_ref.11, bf16[3,1408,3072]{2,1,0:T(8,128)(2,1)} %w1_ref.11, bf16[3,3072,1408]{2,1,0:T(8,128)(2,1)} %w2_ref.11, bf16[3,2,2048,1408]{3,2,1,0:T(8,128)(2,1)} %x_hbm.11, ...), custom_call_target="tpu_custom_call" | custom-call | flops 53150220288 | bytes 80000000 | tf_op jit(solution)/shard_map/pallas_call | solution.py:251
  473.6 11.8 collective-permute-done.17
  487.3 90.8 %collective-permute-done.18 = bf16[704,3072]{1,0:T(8,128)(2,1)} collective-permute-done((bf16[704,3072]{1,0:T(8,128)(2,1)}, bf16[704,3072]{1,0:T(8,128)(2,1)}, u32[]{:S(2)}, u32[]{:S(2)}) %collective-permute-start.18) | collective-permute-done | bytes 4325408 | tf_op jit(solution)/shard_map/ppermute | solution.py:313
  580.0 90.2 %collective-permute-done.11 = bf16[704,3072]{1,0:T(8,128)(2,1)} collective-permute-done((bf16[704,3072]{1,0:T(8,128)(2,1)}, bf16[704,3072]{1,0:T(8,128)(2,1)}, u32[]{:S(2)}, u32[]{:S(2)}) %collective-permute-start.11) | collective-permute-done | bytes 4325408 | tf_op jit(solution)/shard_map/ppermute | solution.py:313
  673.3 72.6 %shard_map.109 = (f32[1408,3072]{1,0:T(8,128)}, f32[1408,3072]{1,0:T(8,128)}, f32[8,512]{1,0:T(8,128)}) custom-call(s32[4]{0:T(128)} %fusion.5.sc_ref, bf16[3,2,2048,3072]{3,2,1,0:T(8,128)(2,1)} %u_ref.11, bf16[3,1408,3072]{2,1,0:T(8,128)(2,1)} %w1_ref.11, bf16[3,3072,1408]{2,1,0:T(8,128)(2,1)} %w2_ref.11, bf16[3,2,2048,1408]{3,2,1,0:T(8,128)(2,1)} %x_hbm.11, ...), custom_call_target="tpu_custom_call" | custom-call | flops 53150220288 | bytes 80000000 | tf_op jit(solution)/shard_map/pallas_call | solution.py:251
  753.3 11.6 add_convert_fusion.15
  769.1 14.7 add_convert_fusion.7
  784.4 8.8 add_convert_fusion.9
  798.3 11.3 add_convert_fusion.11
  809.6 11.4 add_convert_fusion.3
  823.6 7.8 add_convert_fusion.1
  832.4 8.2 add_convert_fusion.13
  846.0 44.7 %collective-permute-done.19 = bf16[352,3072]{1,0:T(8,128)(2,1)} collective-permute-done((bf16[352,3072]{1,0:T(8,128)(2,1)S(1)}, bf16[352,3072]{1,0:T(8,128)(2,1)}, u32[]{:S(2)}, u32[]{:S(2)}) %collective-permute-start.19) | collective-permute-done | bytes 2162720 | tf_op jit(solution)/shard_map/ppermute | solution.py:314
  892.4 9.6 add_convert_fusion.5
  902.0 9.7 add_convert_fusion.8.piece_ref
  911.7 69.0 %collective-permute-done.13 = bf16[352,3072]{1,0:T(8,128)(2,1)S(1)} collective-permute-done((bf16[352,3072]{1,0:T(8,128)(2,1)}, bf16[352,3072]{1,0:T(8,128)(2,1)S(1)}, u32[]{:S(2)}, u32[]{:S(2)}) %collective-permute-start.13) | collective-permute-done | bytes 2162720 | tf_op jit(solution)/shard_map/ppermute | solution.py:314
  982.4 10.7 add_convert_fusion.10.piece_ref
  997.2 9.8 add_convert_fusion.piece_ref
  1007.0 11.1 add_convert_fusion.2.piece_ref
  1018.1 12.9 collective-permute-done.25
  1032.2 11.2 collective-permute-done.6
  1044.1 33.1 %collective-permute-done.22.piece_ref = bf16[352,3072]{1,0:T(8,128)(2,1)S(1)} collective-permute-done((bf16[352,3072]{1,0:T(8,128)(2,1)S(1)}, bf16[352,3072]{1,0:T(8,128)(2,1)S(1)}, u32[]{:S(2)}, u32[]{:S(2)}) %collective-permute-start.22) | collective-permute-done | bytes 2162720 | tf_op jit(solution)/shard_map/ppermute | solution.py:313
  1080.3 9.3 collective-permute-done.20.piece_ref
  1090.5 33.1 %collective-permute-done.16.piece_ref = bf16[352,3072]{1,0:T(8,128)(2,1)S(1)} collective-permute-done((bf16[352,3072]{1,0:T(8,128)(2,1)}, bf16[352,3072]{1,0:T(8,128)(2,1)S(1)}, u32[]{:S(2)}, u32[]{:S(2)}) %collective-permute-start.16) | collective-permute-done | bytes 2162720 | tf_op jit(solution)/shard_map/ppermute | solution.py:313
  1126.6 10.2 add_convert_fusion.4.piece_ref
  1136.8 9.1 add_convert_fusion.12.piece_ref
  1146.3 36.0 %collective-permute-done.41.piece_ref = bf16[1408,768]{1,0:T(8,128)(2,1)} collective-permute-done((bf16[1408,768]{1,0:T(8,128)(2,1)}, bf16[1408,768]{1,0:T(8,128)(2,1)}, u32[]{:S(2)}, u32[]{:S(2)}) %collective-permute-start.41) | collective-permute-done | bytes 2162720 | tf_op jit(solution)/shard_map/ppermute | solution.py:314
  1183.8 44.9 %collective-permute-done.35.piece_ref = bf16[1408,768]{1,0:T(8,128)(2,1)} collective-permute-done((bf16[1408,768]{1,0:T(8,128)(2,1)}, bf16[1408,768]{1,0:T(8,128)(2,1)}, u32[]{:S(2)}, u32[]{:S(2)}) %collective-permute-start.35) | collective-permute-done | bytes 2162720 | tf_op jit(solution)/shard_map/ppermute | solution.py:314
  1231.1 31.6 %collective-permute-done.26.piece_ref = bf16[1408,768]{1,0:T(8,128)(2,1)} collective-permute-done((bf16[1408,768]{1,0:T(8,128)(2,1)}, bf16[1408,768]{1,0:T(8,128)(2,1)}, u32[]{:S(2)}, u32[]{:S(2)}) %collective-permute-start.26) | collective-permute-done | bytes 2162720 | tf_op jit(solution)/shard_map/ppermute | solution.py:313
  1263.9 11.2 collective-permute-done.7.piece_ref
  1275.4 33.6 %collective-permute-done.21.piece_ref = bf16[352,3072]{1,0:T(8,128)(2,1)} collective-permute-done((bf16[352,3072]{1,0:T(8,128)(2,1)}, bf16[352,3072]{1,0:T(8,128)(2,1)}, u32[]{:S(2)}, u32[]{:S(2)}) %collective-permute-start.21) | collective-permute-done | bytes 2162720 | tf_op jit(solution)/shard_map/ppermute | solution.py:313
  1310.7 10.7 collective-permute-done.40.piece_ref
  1322.2 45.5 %collective-permute-done.34.piece_ref = bf16[1408,768]{1,0:T(8,128)(2,1)} collective-permute-done((bf16[1408,768]{1,0:T(8,128)(2,1)}, bf16[1408,768]{1,0:T(8,128)(2,1)}, u32[]{:S(2)}, u32[]{:S(2)}) %collective-permute-start.34) | collective-permute-done | bytes 2162720 | tf_op jit(solution)/shard_map/ppermute | solution.py:314
  1370.3 6.8 put_out.12.rest_0_
  1381.5 6.6 put_out.13.rest_0_
  1393.2 6.6 put_out.14.rest_0_
  1404.4 6.6 put_out.15.rest_0_
  1411.0 6.6 put_out.16.rest_0_
  1417.5 6.6 put_out.17.rest_0_
  1424.1 6.6 put_out.18.rest_0_
  1430.6 6.6 put_out.19.rest_0_
  1437.2 6.6 put_out.20.rest_0_
  1485.7 6.6 put_out.22.rest_0_
  1497.4 6.6 put_out.23
  (152 shorter events, 138.8 us)
Async XLA Ops:
  94.6 106.0 %collective-permute-start = (bf16[2048,1408]{1,0:T(8,128)(2,1)}, bf16[2048,1408]{1,0:T(8,128)(2,1)}, u32[]{:S(2)}, u32[]{:S(2)}) collective-permute-start(bf16[2048,1408]{1,0:T(8,128)(2,1)} %get-tuple-element.35.refs_0_), channel_id=1, source_target_pairs={{0,1},{1,0},{2,3},{3,2},{4,5},{5,4},{6,7},{7,6}} | collective-permute-start | bytes 17301512 | tf_op jit(solution)/shard_map/ppermute | solution.py:315
  199.2 95.1 %collective-permute-start.2 = (bf16[2048,1408]{1,0:T(8,128)(2,1)}, bf16[2048,1408]{1,0:T(8,128)(2,1)}, u32[]{:S(2)}, u32[]{:S(2)}) collective-permute-start(bf16[2048,1408]{1,0:T(8,128)(2,1)} %get-tuple-element.40.refs_0_), channel_id=1, source_target_pairs={{0,1},{1,0},{2,3},{3,2},{4,5},{5,4},{6,7},{7,6}} | collective-permute-start | bytes 17301512 | tf_op jit(solution)/shard_map/ppermute | solution.py:315
  293.8 106.0 %collective-permute-start.1 = (bf16[2048,1408]{1,0:T(8,128)(2,1)}, bf16[2048,1408]{1,0:T(8,128)(2,1)}, u32[]{:S(2)}, u32[]{:S(2)}) collective-permute-start(bf16[2048,1408]{1,0:T(8,128)(2,1)} %get-tuple-element.39.refs_0_), channel_id=1, source_target_pairs={{0,1},{1,0},{2,3},{3,2},{4,5},{5,4},{6,7},{7,6}} | collective-permute-start | bytes 17301512 | tf_op jit(solution)/shard_map/ppermute | solution.py:315
  294.3 98.5 %copy-start.7 = (f32[8,512]{1,0:T(8,128)S(1)}, f32[8,512]{1,0:T(8,128)}, u32[]{:S(2)}) copy-start(f32[8,512]{1,0:T(8,128)} %get-tuple-element.34.refs_0_) | copy-start | bytes 49156
  294.3 99.1 %copy-start.8 = (f32[8,512]{1,0:T(8,128)S(1)}, f32[8,512]{1,0:T(8,128)}, u32[]{:S(2)}) copy-start(f32[8,512]{1,0:T(8,128)} %get-tuple-element.36.refs_2_) | copy-start | bytes 49156
  294.3 101.0 %copy-start.6 = (f32[8,512]{1,0:T(8,128)S(1)}, f32[8,512]{1,0:T(8,128)}, u32[]{:S(2)}) copy-start(f32[8,512]{1,0:T(8,128)} %get-tuple-element.37.refs_2_) | copy-start | bytes 49156
  387.8 284.1 %collective-permute-start.3 = (bf16[2048,1408]{1,0:T(8,128)(2,1)}, bf16[2048,1408]{1,0:T(8,128)(2,1)}, u32[]{:S(2)}, u32[]{:S(2)}) collective-permute-start(bf16[2048,1408]{1,0:T(8,128)(2,1)} %get-tuple-element.44.refs_0_), channel_id=1, source_target_pairs={{0,1},{1,0},{2,3},{3,2},{4,5},{5,4},{6,7},{7,6}} | collective-permute-start | bytes 17301512 | tf_op jit(solution)/shard_map/ppermute | solution.py:315
  387.9 97.5 %collective-permute-start.17 = (bf16[704,3072]{1,0:T(8,128)(2,1)}, bf16[704,3072]{1,0:T(8,128)(2,1)}, u32[]{:S(2)}, u32[]{:S(2)}) collective-permute-start(bf16[704,3072]{1,0:T(8,128)(2,1)} %get-tuple-element.54), channel_id=1, source_target_pairs={{0,2},{2,0},{4,6},{6,4},{1,3},{3,1},{5,7},{7,5}} | collective-permute-start | bytes 12976136 | tf_op jit(solution)/shard_map/ppermute | solution.py:313
  390.9 430.1 %collective-permute-start.36 = (bf16[1408,1536]{1,0:T(8,128)(2,1)}, bf16[1408,1536]{1,0:T(8,128)(2,1)}, u32[]{:S(2)}, u32[]{:S(2)}) collective-permute-start(bf16[1408,1536]{1,0:T(8,128)(2,1)} %get-tuple-element.64), channel_id=1, source_target_pairs={{0,4},{2,6},{4,0},{6,2},{1,5},{3,7},{5,1},{7,3}} | collective-permute-start | bytes 12976136 | tf_op jit(solution)/shard_map/ppermute | solution.py:314
  392.2 185.9 %collective-permute-start.18 = (bf16[704,3072]{1,0:T(8,128)(2,1)}, bf16[704,3072]{1,0:T(8,128)(2,1)}, u32[]{:S(2)}, u32[]{:S(2)}) collective-permute-start(bf16[704,3072]{1,0:T(8,128)(2,1)} %get-tuple-element.55), channel_id=1, source_target_pairs={{0,2},{2,0},{4,6},{6,4},{1,3},{3,1},{5,7},{7,5}} | collective-permute-start | bytes 12976136 | tf_op jit(solution)/shard_map/ppermute | solution.py:313
  399.8 270.3 %collective-permute-start.11 = (bf16[704,3072]{1,0:T(8,128)(2,1)}, bf16[704,3072]{1,0:T(8,128)(2,1)}, u32[]{:S(2)}, u32[]{:S(2)}) collective-permute-start(bf16[704,3072]{1,0:T(8,128)(2,1)} %get-tuple-element.50), channel_id=1, source_target_pairs={{0,2},{2,0},{4,6},{6,4},{1,3},{3,1},{5,7},{7,5}} | collective-permute-start | bytes 12976136 | tf_op jit(solution)/shard_map/ppermute | solution.py:313
  485.4 336.9 %collective-permute-start.37 = (bf16[1408,1536]{1,0:T(8,128)(2,1)}, bf16[1408,1536]{1,0:T(8,128)(2,1)}, u32[]{:S(2)}, u32[]{:S(2)}) collective-permute-start(bf16[1408,1536]{1,0:T(8,128)(2,1)} %get-tuple-element.65), channel_id=1, source_target_pairs={{0,4},{2,6},{4,0},{6,2},{1,5},{3,7},{5,1},{7,3}} | collective-permute-start | bytes 12976136 | tf_op jit(solution)/shard_map/ppermute | solution.py:314
  578.1 186.9 %collective-permute-start.30 = (bf16[1408,1536]{1,0:T(8,128)(2,1)}, bf16[1408,1536]{1,0:T(8,128)(2,1)}, u32[]{:S(2)}, u32[]{:S(2)}) collective-permute-start(bf16[1408,1536]{1,0:T(8,128)(2,1)} %get-tuple-element.60), channel_id=1, source_target_pairs={{0,4},{2,6},{4,0},{6,2},{1,5},{3,7},{5,1},{7,3}} | collective-permute-start | bytes 12976136 | tf_op jit(solution)/shard_map/ppermute | solution.py:314
  670.2 123.1 %collective-permute-start.12 = (bf16[704,3072]{1,0:T(8,128)(2,1)}, bf16[704,3072]{1,0:T(8,128)(2,1)}, u32[]{:S(2)}, u32[]{:S(2)}) collective-permute-start(bf16[704,3072]{1,0:T(8,128)(2,1)} %get-tuple-element.51), channel_id=1, source_target_pairs={{0,2},{2,0},{4,6},{6,4},{1,3},{3,1},{5,7},{7,5}} | collective-permute-start | bytes 12976136 | tf_op jit(solution)/shard_map/ppermute | solution.py:313
  671.9 122.2 %collective-permute-start.31 = (bf16[1408,1536]{1,0:T(8,128)(2,1)}, bf16[1408,1536]{1,0:T(8,128)(2,1)}, u32[]{:S(2)}, u32[]{:S(2)}) collective-permute-start(bf16[1408,1536]{1,0:T(8,128)(2,1)} %get-tuple-element.61), channel_id=1, source_target_pairs={{0,4},{2,6},{4,0},{6,2},{1,5},{3,7},{5,1},{7,3}} | collective-permute-start | bytes 12976136 | tf_op jit(solution)/shard_map/ppermute | solution.py:314
  673.2 72.6 %copy-start.9 = (f32[8,512]{1,0:T(8,128)S(1)}, f32[8,512]{1,0:T(8,128)}, u32[]{:S(2)}) copy-start(f32[8,512]{1,0:T(8,128)} %get-tuple-element.42.refs_2_) | copy-start | bytes 49156
  765.0 3.6 collective-permute-start.10
  768.5 62.9 %collective-permute-start.5 = (bf16[352,3072]{1,0:T(8,128)(2,1)}, bf16[352,3072]{1,0:T(8,128)(2,1)}, u32[]{:S(2)}, u32[]{:S(2)}) collective-permute-start(bf16[352,3072]{1,0:T(8,128)(2,1)} %get-tuple-element.69), channel_id=1, source_target_pairs={{0,2},{2,0},{4,6},{6,4},{1,3},{3,1},{5,7},{7,5}} | collective-permute-start | bytes 6488072 | tf_op jit(solution)/shard_map/ppermute | solution.py:313
  793.2 3.6 collective-permute-start.29
  794.1 50.2 %collective-permute-start.24 = (bf16[1408,768]{1,0:T(8,128)(2,1)}, bf16[1408,768]{1,0:T(8,128)(2,1)}, u32[]{:S(2)}, u32[]{:S(2)}) collective-permute-start(bf16[1408,768]{1,0:T(8,128)(2,1)} %get-tuple-element.67), channel_id=1, source_target_pairs={{0,4},{2,6},{4,0},{6,2},{1,5},{3,7},{5,1},{7,3}} | collective-permute-start | bytes 6488072 | tf_op jit(solution)/shard_map/ppermute | solution.py:314
  796.8 93.8 %collective-permute-start.19 = (bf16[352,3072]{1,0:T(8,128)(2,1)S(1)}, bf16[352,3072]{1,0:T(8,128)(2,1)}, u32[]{:S(2)}, u32[]{:S(2)}) collective-permute-start(bf16[352,3072]{1,0:T(8,128)(2,1)S(1)} %add_convert_fusion.9), channel_id=1, source_target_pairs={{0,4},{2,6},{4,0},{6,2},{1,5},{3,7},{5,1},{7,3}} | collective-permute-start | bytes 6488072 | tf_op jit(solution)/shard_map/ppermute | solution.py:314
  798.3 25.3 %slice-start.1 = ((s8[8650752]{0:T(1024)(128)(4,1)}), s8[4194304]{0:T(1024)(128)(4,1)S(1)}, s32[]{:S(2)}) async-start(s8[8650752]{0:T(1024)(128)(4,1)} %bitcast.49), calls=%async_computation.1 | async-start | bytes 8388608
  821.0 172.1 %collective-permute-start.23 = (bf16[1408,768]{1,0:T(8,128)(2,1)}, bf16[1408,768]{1,0:T(8,128)(2,1)}, u32[]{:S(2)}, u32[]{:S(2)}) collective-permute-start(bf16[1408,768]{1,0:T(8,128)(2,1)} %get-tuple-element.66), channel_id=1, source_target_pairs={{0,4},{2,6},{4,0},{6,2},{1,5},{3,7},{5,1},{7,3}} | collective-permute-start | bytes 6488072 | tf_op jit(solution)/shard_map/ppermute | solution.py:314
  822.3 171.6 %collective-permute-start.4 = (bf16[352,3072]{1,0:T(8,128)(2,1)}, bf16[352,3072]{1,0:T(8,128)(2,1)}, u32[]{:S(2)}, u32[]{:S(2)}) collective-permute-start(bf16[352,3072]{1,0:T(8,128)(2,1)} %get-tuple-element.68), channel_id=1, source_target_pairs={{0,2},{2,0},{4,6},{6,4},{1,3},{3,1},{5,7},{7,5}} | collective-permute-start | bytes 6488072 | tf_op jit(solution)/shard_map/ppermute | solution.py:313
  831.4 59.3 %copy-start.5 = (bf16[1408,768]{1,0:T(8,128)(2,1)S(1)}, bf16[1408,768]{1,0:T(8,128)(2,1)}, u32[]{:S(2)}) copy-start(bf16[1408,768]{1,0:T(8,128)(2,1)} %add_convert_fusion.3) | copy-start | bytes 6488068
  831.4 149.4 %collective-permute-start.13 = (bf16[352,3072]{1,0:T(8,128)(2,1)}, bf16[352,3072]{1,0:T(8,128)(2,1)S(1)}, u32[]{:S(2)}, u32[]{:S(2)}) collective-permute-start(bf16[352,3072]{1,0:T(8,128)(2,1)} %add_convert_fusion.11), channel_id=1, source_target_pairs={{0,4},{2,6},{4,0},{6,2},{1,5},{3,7},{5,1},{7,3}} | collective-permute-start | bytes 6488072 | tf_op jit(solution)/shard_map/ppermute | solution.py:314
  844.3 150.2 %collective-permute-start.38 = (bf16[1408,768]{1,0:T(8,128)(2,1)}, bf16[1408,768]{1,0:T(8,128)(2,1)}, u32[]{:S(2)}, u32[]{:S(2)}) collective-permute-start(bf16[1408,768]{1,0:T(8,128)(2,1)} %add_convert_fusion.1), channel_id=1, source_target_pairs={{0,2},{2,0},{4,6},{6,4},{1,3},{3,1},{5,7},{7,5}} | collective-permute-start | bytes 6488072 | tf_op jit(solution)/shard_map/ppermute | solution.py:313
  890.7 104.8 %collective-permute-start.32 = (bf16[1408,768]{1,0:T(8,128)(2,1)S(1)}, bf16[1408,768]{1,0:T(8,128)(2,1)}, u32[]{:S(2)}, u32[]{:S(2)}) collective-permute-start(bf16[1408,768]{1,0:T(8,128)(2,1)S(1)} %copy-done.5), channel_id=1, source_target_pairs={{0,2},{2,0},{4,6},{6,4},{1,3},{3,1},{5,7},{7,5}} | collective-permute-start | bytes 6488072 | tf_op jit(solution)/shard_map/ppermute | solution.py:313
  980.8 50.2 %collective-permute-start.25 = (bf16[1408,768]{1,0:T(8,128)(2,1)}, bf16[1408,768]{1,0:T(8,128)(2,1)}, u32[]{:S(2)}, u32[]{:S(2)}) collective-permute-start(bf16[1408,768]{1,0:T(8,128)(2,1)} %add_convert_fusion.5), channel_id=1, source_target_pairs={{0,2},{2,0},{4,6},{6,4},{1,3},{3,1},{5,7},{7,5}} | collective-permute-start | bytes 6488072 | tf_op jit(solution)/shard_map/ppermute | solution.py:313
  993.1 50.2 %collective-permute-start.6 = (bf16[352,3072]{1,0:T(8,128)(2,1)}, bf16[352,3072]{1,0:T(8,128)(2,1)}, u32[]{:S(2)}, u32[]{:S(2)}) collective-permute-start(bf16[352,3072]{1,0:T(8,128)(2,1)} %add_convert_fusion.13), channel_id=1, source_target_pairs={{0,4},{2,6},{4,0},{6,2},{1,5},{3,7},{5,1},{7,3}} | collective-permute-start | bytes 6488072 | tf_op jit(solution)/shard_map/ppermute | solution.py:314
  993.9 83.3 %collective-permute-start.22 = (bf16[352,3072]{1,0:T(8,128)(2,1)S(1)}, bf16[352,3072]{1,0:T(8,128)(2,1)S(1)}, u32[]{:S(2)}, u32[]{:S(2)}) collective-permute-start(bf16[352,3072]{1,0:T(8,128)(2,1)S(1)} %add_convert_fusion.8.piece_ref), channel_id=1, source_target_pairs={{0,2},{2,0},{4,6},{6,4},{1,3},{3,1},{5,7},{7,5}} | collective-permute-start | bytes 6488072 | tf_op jit(solution)/shard_map/ppermute | solution.py:313
  994.5 95.2 %collective-permute-start.20 = (bf16[352,3072]{1,0:T(8,128)(2,1)S(1)}, bf16[352,3072]{1,0:T(8,128)(2,1)}, u32[]{:S(2)}, u32[]{:S(2)}) collective-permute-start(bf16[352,3072]{1,0:T(8,128)(2,1)S(1)} %add_convert_fusion.8.piece_ref), channel_id=1, source_target_pairs={{0,4},{2,6},{4,0},{6,2},{1,5},{3,7},{5,1},{7,3}} | collective-permute-start | bytes 6488072 | tf_op jit(solution)/shard_map/ppermute | solution.py:314
  995.5 128.1 %collective-permute-start.16 = (bf16[352,3072]{1,0:T(8,128)(2,1)}, bf16[352,3072]{1,0:T(8,128)(2,1)S(1)}, u32[]{:S(2)}, u32[]{:S(2)}) collective-permute-start(bf16[352,3072]{1,0:T(8,128)(2,1)} %add_convert_fusion.10.piece_ref), channel_id=1, source_target_pairs={{0,2},{2,0},{4,6},{6,4},{1,3},{3,1},{5,7},{7,5}} | collective-permute-start | bytes 6488072 | tf_op jit(solution)/shard_map/ppermute | solution.py:313
  1031.0 115.0 %collective-permute-start.14 = (bf16[352,3072]{1,0:T(8,128)(2,1)}, bf16[352,3072]{1,0:T(8,128)(2,1)}, u32[]{:S(2)}, u32[]{:S(2)}) collective-permute-start(bf16[352,3072]{1,0:T(8,128)(2,1)} %add_convert_fusion.10.piece_ref), channel_id=1, source_target_pairs={{0,4},{2,6},{4,0},{6,2},{1,5},{3,7},{5,1},{7,3}} | collective-permute-start | bytes 6488072 | tf_op jit(solution)/shard_map/ppermute | solution.py:314
  1043.3 139.0 %collective-permute-start.41 = (bf16[1408,768]{1,0:T(8,128)(2,1)}, bf16[1408,768]{1,0:T(8,128)(2,1)}, u32[]{:S(2)}, u32[]{:S(2)}) collective-permute-start(bf16[1408,768]{1,0:T(8,128)(2,1)} %add_convert_fusion.piece_ref), channel_id=1, source_target_pairs={{0,4},{2,6},{4,0},{6,2},{1,5},{3,7},{5,1},{7,3}} | collective-permute-start | bytes 6488072 | tf_op jit(solution)/shard_map/ppermute | solution.py:314
  1078.7 104.5 %collective-permute-start.39 = (bf16[1408,768]{1,0:T(8,128)(2,1)}, bf16[1408,768]{1,0:T(8,128)(2,1)}, u32[]{:S(2)}, u32[]{:S(2)}) collective-permute-start(bf16[1408,768]{1,0:T(8,128)(2,1)} %add_convert_fusion.piece_ref), channel_id=1, source_target_pairs={{0,2},{2,0},{4,6},{6,4},{1,3},{3,1},{5,7},{7,5}} | collective-permute-start | bytes 6488072 | tf_op jit(solution)/shard_map/ppermute | solution.py:313
  1089.7 139.0 %collective-permute-start.35 = (bf16[1408,768]{1,0:T(8,128)(2,1)}, bf16[1408,768]{1,0:T(8,128)(2,1)}, u32[]{:S(2)}, u32[]{:S(2)}) collective-permute-start(bf16[1408,768]{1,0:T(8,128)(2,1)} %add_convert_fusion.2.piece_ref), channel_id=1, source_target_pairs={{0,4},{2,6},{4,0},{6,2},{1,5},{3,7},{5,1},{7,3}} | collective-permute-start | bytes 6488072 | tf_op jit(solution)/shard_map/ppermute | solution.py:314
  1124.9 104.6 %collective-permute-start.33 = (bf16[1408,768]{1,0:T(8,128)(2,1)}, bf16[1408,768]{1,0:T(8,128)(2,1)}, u32[]{:S(2)}, u32[]{:S(2)}) collective-permute-start(bf16[1408,768]{1,0:T(8,128)(2,1)} %add_convert_fusion.2.piece_ref), channel_id=1, source_target_pairs={{0,2},{2,0},{4,6},{6,4},{1,3},{3,1},{5,7},{7,5}} | collective-permute-start | bytes 6488072 | tf_op jit(solution)/shard_map/ppermute | solution.py:313
  1146.0 116.7 %collective-permute-start.26 = (bf16[1408,768]{1,0:T(8,128)(2,1)}, bf16[1408,768]{1,0:T(8,128)(2,1)}, u32[]{:S(2)}, u32[]{:S(2)}) collective-permute-start(bf16[1408,768]{1,0:T(8,128)(2,1)} %add_convert_fusion.4.piece_ref), channel_id=1, source_target_pairs={{0,2},{2,0},{4,6},{6,4},{1,3},{3,1},{5,7},{7,5}} | collective-permute-start | bytes 6488072 | tf_op jit(solution)/shard_map/ppermute | solution.py:313
  1182.4 92.7 %collective-permute-start.7 = (bf16[352,3072]{1,0:T(8,128)(2,1)}, bf16[352,3072]{1,0:T(8,128)(2,1)}, u32[]{:S(2)}, u32[]{:S(2)}) collective-permute-start(bf16[352,3072]{1,0:T(8,128)(2,1)} %add_convert_fusion.12.piece_ref), channel_id=1, source_target_pairs={{0,4},{2,6},{4,0},{6,2},{1,5},{3,7},{5,1},{7,3}} | collective-permute-start | bytes 6488072 | tf_op jit(solution)/shard_map/ppermute | solution.py:314
  1183.2 125.9 %collective-permute-start.21 = (bf16[352,3072]{1,0:T(8,128)(2,1)}, bf16[352,3072]{1,0:T(8,128)(2,1)}, u32[]{:S(2)}, u32[]{:S(2)}) collective-permute-start(bf16[352,3072]{1,0:T(8,128)(2,1)} %collective-permute-done.20.piece_ref), channel_id=1, source_target_pairs={{0,2},{2,0},{4,6},{6,4},{1,3},{3,1},{5,7},{7,5}} | collective-permute-start | bytes 6488072 | tf_op jit(solution)/shard_map/ppermute | solution.py:313
  1228.7 92.7 %collective-permute-start.40 = (bf16[1408,768]{1,0:T(8,128)(2,1)}, bf16[1408,768]{1,0:T(8,128)(2,1)}, u32[]{:S(2)}, u32[]{:S(2)}) collective-permute-start(bf16[1408,768]{1,0:T(8,128)(2,1)} %collective-permute-done.39.piece_ref), channel_id=1, source_target_pairs={{0,4},{2,6},{4,0},{6,2},{1,5},{3,7},{5,1},{7,3}} | collective-permute-start | bytes 6488072 | tf_op jit(solution)/shard_map/ppermute | solution.py:314
  1229.5 138.2 %collective-permute-start.34 = (bf16[1408,768]{1,0:T(8,128)(2,1)}, bf16[1408,768]{1,0:T(8,128)(2,1)}, u32[]{:S(2)}, u32[]{:S(2)}) collective-permute-start(bf16[1408,768]{1,0:T(8,128)(2,1)} %collective-permute-done.33.piece_ref), channel_id=1, source_target_pairs={{0,4},{2,6},{4,0},{6,2},{1,5},{3,7},{5,1},{7,3}} | collective-permute-start | bytes 6488072 | tf_op jit(solution)/shard_map/ppermute | solution.py:314
  1262.7 223.0 %collective-permute-start.28 = (bf16[1408,768]{1,0:T(8,128)(2,1)}, bf16[1408,768]{1,0:T(8,128)(2,1)}, u32[]{:S(2)}, u32[]{:S(2)}) collective-permute-start(bf16[1408,768]{1,0:T(8,128)(2,1)} %add_convert_fusion.4.piece_ref), channel_id=1, source_target_pairs={{0,4},{2,6},{4,0},{6,2},{1,5},{3,7},{5,1},{7,3}} | collective-permute-start | bytes 6488072 | tf_op jit(solution)/shard_map/ppermute | solution.py:314
  1275.1 217.2 %collective-permute-start.9 = (bf16[352,3072]{1,0:T(8,128)(2,1)}, bf16[352,3072]{1,0:T(8,128)(2,1)}, u32[]{:S(2)}, u32[]{:S(2)}) collective-permute-start(bf16[352,3072]{1,0:T(8,128)(2,1)} %add_convert_fusion.12.piece_ref), channel_id=1, source_target_pairs={{0,2},{2,0},{4,6},{6,4},{1,3},{3,1},{5,7},{7,5}} | collective-permute-start | bytes 6488072 | tf_op jit(solution)/shard_map/ppermute | solution.py:313
  1309.1 154.7 %collective-permute-start.15 = (bf16[352,3072]{1,0:T(8,128)(2,1)}, bf16[352,3072]{1,0:T(8,128)(2,1)}, u32[]{:S(2)}, u32[]{:S(2)}) collective-permute-start(bf16[352,3072]{1,0:T(8,128)(2,1)} %collective-permute-done.14.piece_ref), channel_id=1, source_target_pairs={{0,2},{2,0},{4,6},{6,4},{1,3},{3,1},{5,7},{7,5}} | collective-permute-start | bytes 6488072 | tf_op jit(solution)/shard_map/ppermute | solution.py:313
  1321.4 176.0 %collective-permute-start.27 = (bf16[1408,768]{1,0:T(8,128)(2,1)}, bf16[1408,768]{1,0:T(8,128)(2,1)}, u32[]{:S(2)}, u32[]{:S(2)}) collective-permute-start(bf16[1408,768]{1,0:T(8,128)(2,1)} %collective-permute-done.26.piece_ref), channel_id=1, source_target_pairs={{0,4},{2,6},{4,0},{6,2},{1,5},{3,7},{5,1},{7,3}} | collective-permute-start | bytes 6488072 | tf_op jit(solution)/shard_map/ppermute | solution.py:314
  1367.8 136.2 %collective-permute-start.8 = (bf16[352,3072]{1,0:T(8,128)(2,1)}, bf16[352,3072]{1,0:T(8,128)(2,1)}, u32[]{:S(2)}, u32[]{:S(2)}) collective-permute-start(bf16[352,3072]{1,0:T(8,128)(2,1)} %collective-permute-done.7.piece_ref), channel_id=1, source_target_pairs={{0,2},{2,0},{4,6},{6,4},{1,3},{3,1},{5,7},{7,5}} | collective-permute-start | bytes 6488072 | tf_op jit(solution)/shard_map/ppermute | solution.py:313
  (7 other events, 68.0 us)

commit v3 on v0

v3 whole, which is shorter than its diff:
```python
import functools

import jax
import jax.numpy as jnp
from jax import lax
from jax.experimental import pallas as pl
from jax.experimental.pallas import tpu as pltpu
from jax.sharding import PartitionSpec as P

INV_SQRT2 = 0.7071067811865476
INV_SQRT_2PI = 0.3989422804014327
LOG2_E = 1.4426950408889634
F_BLOCK = 512
T_CHUNK = 256
IN_SLOTS = 3
ROW_STEPS = 2
VMEM_LIMIT = 66_500_000

F32 = jnp.float32
BF16 = jnp.bfloat16
ANY = pl.ANY
MESH = pl.DeviceIdType.MESH


def dot_nn(a, b):
    return lax.dot_general(a, b, (((1,), (0,)), ((), ())), preferred_element_type=F32)


def dot_nt(a, b):
    return lax.dot_general(a, b, (((1,), (1,)), ((), ())), preferred_element_type=F32)


def stack_kernel(n_layers, n_ex, n_steps, u_ref, w1_ref, w2_ref, x_hbm, dout_hbm,
                 p_hbm, q_hbm, dzo_hbm, g1k_hbm, g1s_hbm, g1r_hbm, g2k_hbm, g2s_hbm, g2r_hbm, g1l_hbm, g2l_hbm, ss_ref,
                 x_t, dz, dz_t, dh, h, acc, x_st, z_st, p_st, q_st, g1_st, g1s_st, g2_st, g2s_st,
                 in_sem, out_sem, io_sem, tp_send, tp_recv, far_send, far_recv):
    task, step = pl.program_id(0), pl.program_id(1)
    n_early = (n_layers - 1) * n_ex
    dp = lax.axis_index('dp')
    x_pos, y_pos = lax.rem(dp, 2), dp // 2
    x_far = {'dp': dp + 1 - 2 * x_pos}
    y_far = {'dp': dp + 2 - 4 * y_pos}
    tp_far = {'tp': 1 - lax.axis_index('tp')}
    n_tok, d_model = dz.shape
    half_d = d_model // 2
    n_half = n_steps // 2
    n_t = n_tok // T_CHUNK
    example = lax.rem(task, n_ex)
    cols = lambda k: pl.ds(pl.multiple_of(k * F_BLOCK, F_BLOCK), F_BLOCK)

    def in_start(t, c):
        slot, rows, ex = c % IN_SLOTS, pl.ds(c * T_CHUNK, T_CHUNK), lax.rem(t, n_ex)
        copy = lambda k, src, dst: pltpu.make_async_copy(src, dst.at[slot], in_sem.at[k, slot]).start()
        copy(0, x_hbm.at[n_layers - 1 - t // n_ex, ex, rows, :], x_st)

        @pl.when(t < n_early)
        def _():
            copy(1, dout_hbm.at[ex, rows, :], z_st)

        @pl.when(t >= n_early)
        def _():
            copy(1, dzo_hbm.at[ex, rows, :], z_st)

        @pl.when(t >= n_ex)
        def _():
            copy(2, p_hbm.at[t - n_ex, rows, :], p_st)
            copy(3, q_hbm.at[t - n_ex, rows, :], q_st)

    def in_wait(c):
        slot, rows = c % IN_SLOTS, pl.ds(c * T_CHUNK, T_CHUNK)
        wait = lambda k, dst: pltpu.make_async_copy(dout_hbm.at[0, rows, :], dst.at[slot], in_sem.at[k, slot]).wait()
        wait(0, x_st)
        wait(1, z_st)

        @pl.when(task >= n_ex)
        def _():
            wait(2, p_st)
            wait(3, q_st)

    def tp_copy(t):
        return pltpu.make_async_remote_copy(
            src_ref=p_hbm.at[t], dst_ref=q_hbm.at[t], send_sem=tp_send.at[t], recv_sem=tp_recv.at[t],
            device_id=tp_far, device_id_type=MESH)

    def front(load, to_dx):
        for s in range(n_t + (1 if to_dx else 0)):
            rows = pl.ds(s * T_CHUNK, T_CHUNK)
            if load and s < n_t:
                if s + IN_SLOTS - 1 < n_t:
                    in_start(task, s + IN_SLOTS - 1)
                in_wait(s)
                slot = s % IN_SLOTS
                z = z_st[slot]
                moved = (z.astype(F32) + (p_st[slot].astype(F32) + q_st[slot].astype(F32))).astype(BF16)
                z = jnp.where(task >= n_ex, moved, z) if to_dx else moved
                dz[rows, :] = z
                dz_t[:, rows] = z.T
                x_t[:, rows] = x_st[slot].T
            if s < n_t:
                u = u_ref[0, 0, rows, :].astype(F32)
                t = u * INV_SQRT2
                cdf = 0.5 * lax.erf(t) + 0.5
                h[rows, :] = (u * cdf).astype(BF16)
                slope = cdf + (t * (INV_SQRT_2PI / INV_SQRT2)) * jnp.exp2((t * t) * -LOG2_E)
                dh[rows, :] = (slope * dot_nt(dz[rows, :], w2_ref[0])).astype(BF16)
            if s >= 1 and to_dx:
                rows = pl.ds((s - 1) * T_CHUNK, T_CHUNK)
                part = dot_nt(dh[rows, :], w1_ref[0])
                acc[rows, :] = part if load else acc[rows, :] + part

    @pl.when((task == 0) & (step == 0))
    def _():
        ss_ref[...] = jnp.zeros_like(ss_ref)
        for c in range(IN_SLOTS - 1):
            in_start(task, c)

    for load in (True, False):
        for to_dx in (True, False):
            @pl.when(((step == 0) if load else (step > 0)) & ((task < n_early) if to_dx else (task >= n_early)))
            def _():
                front(load, to_dx)

    dz_keep = pltpu.make_async_copy(dz, dzo_hbm.at[example], io_sem.at[0])
    is_mid = (task >= n_ex) & (task < n_early)
    pl.when(is_mid & (step == 0))(dz_keep.start)
    ends_early = (step == n_steps - 1) & (task < n_early)
    dx_out = pltpu.make_async_copy(dz, p_hbm.at[task], io_sem.at[1])

    @pl.when(ends_early)
    def _():
        pl.when(is_mid)(dz_keep.wait)

        def put(c, carry):
            rows = pl.ds(pl.multiple_of(c * T_CHUNK, T_CHUNK), T_CHUNK)
            dz[rows, :] = acc[rows, :].astype(BF16)
            return carry

        lax.fori_loop(0, n_t, put, 0)
        dx_out.start()

    def out_copies(t, k, r):
        half_rows = pl.ds(pl.multiple_of(r * half_d, 16), half_d)
        part_rows = pl.ds(pl.multiple_of(r * (half_d // ROW_STEPS), 16), half_d // ROW_STEPS)
        early, k_half, k_col = t < n_early, k // n_half, lax.rem(k, n_half)
        copy = lambda n, src, dst: pltpu.make_async_copy(src, dst, out_sem.at[n, r])
        t_e, t_l = jnp.minimum(t, n_early - 1), jnp.maximum(t - n_early, 0)
        return [
            (early, copy(0, g1_st.at[part_rows, :], g1k_hbm.at[t_e, part_rows, cols(k)])),
            (early, copy(1, g1s_st.at[part_rows, :], g1s_hbm.at[t_e, part_rows, cols(k)])),
            (early & (k_half != y_pos), copy(2, g2s_st.at[half_rows, :], g2s_hbm.at[t_e, half_rows, cols(k_col)])),
            (early & (k_half == y_pos), copy(3, g2_st.at[half_rows, :], g2k_hbm.at[t_e, half_rows, cols(k_col)])),
            (~early, copy(0, g1_st.at[half_rows, :], g1l_hbm.at[t_l, half_rows, cols(k)])),
            (~early, copy(3, g2_st.at[half_rows, :], g2l_hbm.at[t_l, half_rows, cols(k)])),
        ]

    def far_x(src, dst):
        return pltpu.make_async_remote_copy(
            src_ref=src, dst_ref=dst, send_sem=far_send.at[0], recv_sem=far_recv.at[0], device_id=x_far, device_id_type=MESH)

    def far_y(src, dst):
        return pltpu.make_async_remote_copy(
            src_ref=src, dst_ref=dst, send_sem=far_send.at[1], recv_sem=far_recv.at[1], device_id=y_far, device_id_type=MESH)

    @pl.when((task > 0) | (step > 0))
    def _():
        t = jnp.where(step > 0, task, task - 1)
        k = jnp.where(step > 0, step - 1, n_steps - 1)
        for r in range(ROW_STEPS):
            for cond, cp in out_copies(t, k, r):
                pl.when(cond)(cp.wait)

        @pl.when(t < n_early)
        def _():
            far_x(g1s_hbm.at[t, :, cols(k)], g1r_hbm.at[t, :, cols(k)]).start()

        @pl.when((t < n_early) & (k // n_half != y_pos))
        def _():
            k_col = cols(lax.rem(k, n_half))
            far_y(g2s_hbm.at[t, :, k_col], g2r_hbm.at[t, :, k_col]).start()

    def square(g):
        return jnp.sum((g * g).reshape(g.shape[0] // 8, 8, g.shape[1]), axis=0)

    def weight_grads(early, r, carry):
        part = half_d // ROW_STEPS
        total = ss_ref[example]
        if early:
            own = pl.multiple_of(r * part + x_pos * half_d, part)
            far = pl.multiple_of(r * part + (1 - x_pos) * half_d, part)
            rows = pl.ds(pl.multiple_of(r * part, part), part)
            g = dot_nn(x_t[pl.ds(own, part), :], dh[...])
            g1_st[rows, :] = g
            total = total + square(g)
            g = dot_nn(x_t[pl.ds(far, part), :], dh[...])
            g1s_st[rows, :] = g.astype(BF16)
            total = total + square(g)
        for at in range(ROW_STEPS):
            rows = pl.ds(pl.multiple_of(r * half_d + at * part, part), part)
            if not early:
                g = dot_nn(x_t[rows, :], dh[...])
                g1_st[rows, :] = g
                total = total + square(g)
            g = dot_nn(dz_t[rows, :], h[...])
            g2_st[rows, :] = g
            if early:
                g2s_st[rows, :] = g.astype(BF16)
            total = total + square(g)
        ss_ref[example] = total
        for cond, cp in out_copies(task, step, r):
            pl.when(cond)(cp.start)
        return carry

    @pl.when(task < n_early)
    def _():
        lax.fori_loop(0, ROW_STEPS, functools.partial(weight_grads, True), 0)

    @pl.when(task >= n_early)
    def _():
        lax.fori_loop(0, ROW_STEPS, functools.partial(weight_grads, False), 0)

    @pl.when(ends_early)
    def _():
        dx_out.wait()
        tp_copy(task).start()

    @pl.when((step == n_steps - 1) & (task < n_early + n_ex - 1))
    def _():
        nxt = task + 1

        @pl.when(nxt >= n_ex)
        def _():
            tp_copy(nxt - n_ex).wait()

        for c in range(IN_SLOTS - 1):
            in_start(nxt, c)

    @pl.when((step == n_steps - 1) & (task == n_early + n_ex - 1))
    def _():
        for r in range(ROW_STEPS):
            for cond, cp in out_copies(task, step, r):
                pl.when(cond)(cp.wait)
        far_x(g1s_hbm, g1r_hbm).wait()
        far_y(g2s_hbm, g2r_hbm).wait()


def run_stack(pre_act, w_in, w_out, block_in, d_out):
    n_layers, n_ex, n_tok, d_model = block_in.shape
    d_ff = pre_act.shape[3]
    n_steps = d_ff // F_BLOCK
    half_d, half_f = d_model // 2, d_ff // 2
    n_early = (n_layers - 1) * n_ex
    top = n_layers - 1
    in_specs = [
        pl.BlockSpec((1, 1, n_tok, F_BLOCK), lambda t, j: (top - t // n_ex, lax.rem(t, n_ex), 0, j)),
        pl.BlockSpec((1, d_model, F_BLOCK),
                     lambda t, j: (jnp.maximum(top - t // n_ex, 1), 0, jnp.minimum(j + n_steps * (t // n_early), n_steps - 1))),
        pl.BlockSpec((1, F_BLOCK, d_model), lambda t, j: (top - t // n_ex, j, 0)),
        pl.BlockSpec(memory_space=ANY),
        pl.BlockSpec(memory_space=ANY),
    ]
    sds = jax.ShapeDtypeStruct
    outs = [
        sds((n_early, n_tok, d_model), BF16), sds((n_early, n_tok, d_model), BF16), sds((n_ex, n_tok, d_model), BF16),
        sds((n_early, half_d, d_ff), F32), sds((n_early, half_d, d_ff), BF16), sds((n_early, half_d, d_ff), BF16),
        sds((n_early, d_model, half_f), F32), sds((n_early, d_model, half_f), BF16), sds((n_early, d_model, half_f), BF16),
        sds((n_ex, d_model, d_ff), F32), sds((n_ex, d_model, d_ff), F32),
        sds((n_ex, 8, F_BLOCK), F32),
    ]
    out_specs = [pl.BlockSpec(memory_space=ANY)] * (len(outs) - 1) + [pl.BlockSpec((n_ex, 8, F_BLOCK), lambda t, j: (0, 0, 0))]
    vm = pltpu.VMEM
    scratch = [
        vm((d_model, n_tok), BF16), vm((n_tok, d_model), BF16), vm((d_model, n_tok), BF16),
        vm((n_tok, F_BLOCK), BF16), vm((n_tok, F_BLOCK), BF16), vm((n_tok, d_model), F32),
        *[vm((IN_SLOTS, T_CHUNK, d_model), BF16)] * 4,
        vm((d_model, F_BLOCK), F32), vm((half_d, F_BLOCK), BF16), vm((d_model, F_BLOCK), F32), vm((d_model, F_BLOCK), BF16),
        pltpu.SemaphoreType.DMA((4, IN_SLOTS)), pltpu.SemaphoreType.DMA((4, ROW_STEPS)), pltpu.SemaphoreType.DMA((2,)),
        pltpu.SemaphoreType.DMA((n_early,)), pltpu.SemaphoreType.DMA((n_early,)),
        pltpu.SemaphoreType.DMA((2,)), pltpu.SemaphoreType.DMA((2,)),
    ]
    n_dots = 4 * n_early + 3 * n_ex
    return pl.pallas_call(
        functools.partial(stack_kernel, n_layers, n_ex, n_steps),
        out_shape=outs,
        grid_spec=pltpu.PrefetchScalarGridSpec(
            num_scalar_prefetch=0, grid=(n_early + n_ex, n_steps), in_specs=in_specs, out_specs=out_specs, scratch_shapes=scratch),
        compiler_params=pltpu.CompilerParams(
            dimension_semantics=('arbitrary', 'arbitrary'), vmem_limit_bytes=VMEM_LIMIT, has_side_effects=True),
        cost_estimate=pl.CostEstimate(
            flops=2 * n_dots * n_tok * d_model * d_ff, bytes_accessed=500_000_000, transcendentals=2 * n_tok * d_ff),
        name='stack',
    )(pre_act, w_in, w_out, block_in, d_out)


def mix_kernel(sc_ref, coef_ref, *refs):
    total = refs[0][0].astype(F32) * coef_ref[0]
    for k, ref in enumerate(refs[1:-1]):
        total = total + ref[0].astype(F32) * coef_ref[k + 1]
    refs[-1][...] = total.astype(BF16)


def mix(which, shape, terms, coefs):
    rows, width = shape
    block = (rows // 2, width) if which == 0 else (rows // 4, width)

    def spec(k, lead):
        if which == 0:
            return pl.BlockSpec((1, *block), lambda i, sc: (lead, 2 * sc[k] + i, 0))
        return pl.BlockSpec((1, *block), lambda i, sc: (lead, i, sc[k]))

    out_map = lambda i, sc: (i, 0)
    places = jnp.stack([jnp.asarray(p, jnp.int32) for _, _, p in terms])
    return pl.pallas_call(
        mix_kernel,
        out_shape=jax.ShapeDtypeStruct((rows, width), BF16),
        grid_spec=pltpu.PrefetchScalarGridSpec(
            num_scalar_prefetch=1, grid=(rows // block[0],),
            in_specs=[pl.BlockSpec(memory_space=pltpu.SMEM)] + [spec(k, lead) for k, (_, lead, _) in enumerate(terms)],
            out_specs=pl.BlockSpec(block, out_map)),
        compiler_params=pltpu.CompilerParams(dimension_semantics=('arbitrary',), vmem_limit_bytes=40_000_000),
        cost_estimate=pl.CostEstimate(flops=2 * len(terms) * rows * width, bytes_accessed=14 * rows * width, transcendentals=0),
        name='mix',
    )(places, jnp.stack([jnp.asarray(c, F32) for c in coefs]), *[v for v, _, _ in terms])


def put_in_kernel(sc_ref, coef_ref, piece_ref, noise_ref, *rest):
    out_ref = rest[-1]
    out_ref[0, 0] = (piece_ref[...].astype(F32) + coef_ref[0] * noise_ref[0, 0]) * coef_ref[1]


def put_out_kernel(sc_ref, coef_ref, piece_ref, noise_ref, *rest):
    out_ref = rest[-1]
    out_ref[0, 0] = (piece_ref[...].astype(F32).T + coef_ref[0] * noise_ref[0, 0]) * coef_ref[1]


def put_piece(transposed, total, layer, quarter, coef, piece, noise):
    if transposed:
        rows, width = piece.shape[1], piece.shape[0]
        block = 256
        piece_spec = pl.BlockSpec((width, block), lambda i, sc: (0, i))
    else:
        rows, width = piece.shape
        block = rows // 2
        piece_spec = pl.BlockSpec((block, width), lambda i, sc: (i, 0))
    big_spec = pl.BlockSpec((1, 1, block, width), lambda i, sc: (sc[0], sc[1], i, 0))
    args = [jnp.stack([jnp.int32(layer), quarter]), coef, piece, noise]
    in_specs = [pl.BlockSpec(memory_space=pltpu.SMEM), piece_spec, big_spec]
    aliases = {}
    if total is not None:
        args.append(total)
        in_specs.append(pl.BlockSpec(memory_space=ANY))
        aliases = {4: 0}
    return pl.pallas_call(
        put_out_kernel if transposed else put_in_kernel,
        out_shape=jax.ShapeDtypeStruct(noise.shape, F32),
        grid_spec=pltpu.PrefetchScalarGridSpec(
            num_scalar_prefetch=1, grid=(rows // block,), in_specs=in_specs, out_specs=big_spec),
        input_output_aliases=aliases,
        compiler_params=pltpu.CompilerParams(dimension_semantics=('arbitrary',), vmem_limit_bytes=40_000_000),
        cost_estimate=pl.CostEstimate(flops=4 * rows * width, bytes_accessed=10 * rows * width, transcendentals=0),
        name='put_out' if transposed else 'put_in',
    )(*args)


def solution(mesh):
    data_size = mesh.shape['dp']
    swap_x = [(i, i ^ 1) for i in range(data_size)]
    swap_y = [(i, i ^ 2) for i in range(data_size)]

    def local_step(block_in, pre_act, w_in, w_out, d_out, noise_in, noise_out, clip_norm, noise_mult):
        n_layers, local_batch, _, d_model = block_in.shape
        d_ff = pre_act.shape[3]
        batch_total = local_batch * data_size
        dp = lax.axis_index('dp')
        x_pos, y_pos = lax.rem(dp, 2), dp // 2
        over_x = lambda v: lax.ppermute(v, 'dp', swap_x)
        over_y = lambda v: lax.ppermute(v, 'dp', swap_y)
        res = run_stack(pre_act, w_in, w_out, block_in, d_out)
        g1k, _, g1r, g2k, _, g2r, g1l, g2l, squares = res[3:]
        part_sq = jnp.sum(squares, axis=(1, 2))
        clip = jnp.minimum(1.0, clip_norm / jnp.sqrt(lax.psum(part_sq, 'tp')))
        clip_x, clip_y = over_x(clip), over_y(clip)
        c_own, c_x, c_y = [[v[k] for k in range(local_batch)] for v in (clip, clip_x, clip_y)]
        coef = jnp.stack([noise_mult * clip_norm, jnp.float32(1.0 / batch_total)])

        noise_in4 = noise_in.reshape(n_layers, 4, d_model // 4, d_ff)
        noise_out4 = noise_out.reshape(n_layers, 4, d_ff // 4, d_model)
        grad_in = grad_out = None

        shapes = ((d_model // 4, d_ff), (d_model, d_ff // 4))
        at_half, at_side = (x_pos, y_pos), (y_pos, x_pos)
        over_half, over_side = (over_x, over_y), (over_y, over_x)
        early, early_far, late = (g1k, g2k), (g1r, g2r), (g1l, g2l)

        def own_terms(layer, which, half_pos, pos):
            if layer == 0:
                return [(late[which], k, 2 * half_pos + pos) for k in range(local_batch)]
            first = (n_layers - 1 - layer) * local_batch
            return [(early[which], first + k, pos) for k in range(local_batch)]

        far_last = {}
        for to_send in (True, False):
            for which in (0, 1):
                pos = 1 - at_side[which] if to_send else at_side[which]
                piece = mix(which, shapes[which], own_terms(0, which, 1 - at_half[which], pos), c_own)
                far_last[which, to_send] = over_half[which](piece)

        def pair_sum(layer, which, to_send, *more):
            pos = 1 - at_side[which] if to_send else at_side[which]
            terms, coefs = own_terms(layer, which, at_half[which], pos), list(c_own)
            if layer == 0:
                more = (far_last[which, to_send], *more)
            else:
                first = (n_layers - 1 - layer) * local_batch
                terms += [(early_far[which], first + k, pos) for k in range(local_batch)]
                coefs += c_y if which else c_x
            terms += [(v[None], 0, 0) for v in more]
            return mix(which, shapes[which], terms, coefs + [1.0] * len(more))

        for layer in range(n_layers - 1, -1, -1):
            got = [over_side[which](pair_sum(layer, which, True)) for which in (0, 1)]
            own1, own2 = [pair_sum(layer, which, False, got[which]) for which in (0, 1)]
            near1, near2 = over_y(own1), over_x(own2)
            side1, side2 = over_x(own1), over_y(own2)
            diag1, diag2 = over_x(near1), over_y(near2)
            q1 = lambda a, b: 2 * a + b
            for a, b, v in ((x_pos, y_pos, own1), (x_pos, 1 - y_pos, near1), (1 - x_pos, y_pos, side1), (1 - x_pos, 1 - y_pos, diag1)):
                grad_in = put_piece(False, grad_in, layer, q1(a, b), coef, v, noise_in4)
            for a, b, v in ((y_pos, x_pos, own2), (y_pos, 1 - x_pos, near2), (1 - y_pos, x_pos, side2), (1 - y_pos, 1 - x_pos, diag2)):
                grad_out = put_piece(True, grad_out, layer, q1(a, b), coef, v, noise_out4)
        return grad_in.reshape(n_layers, d_model, d_ff), grad_out.reshape(n_layers, d_ff, d_model)

    return jax.shard_map(
        local_step,
        mesh=mesh,
        in_specs=(P(None, 'dp', None, None), P(None, 'dp', None, 'tp'), P(None, None, 'tp'), P(None, 'tp', None),
                  P('dp', None, None), P(None, None, 'tp'), P(None, 'tp', None), P(), P()),
        out_specs=(P(None, None, 'tp'), P(None, 'tp', None)),
        check_vma=False,
    )
```

time: 3320 us -> 1230 us (0.37)
  matrix products: 1290 us -> 0 us
  waiting for transfers between devices: 1650 us -> 430 us
  Pallas kernels: 0 us -> 760 us
  other arithmetic: 253 us -> 3.35 us
  local copies, waits for them, and re-layouts: 103 us -> 4.73 us
    psum x3 -> x0, waiting for transfers between devices: 1650 us -> none  [the longest x1 1650 us: local_run(): lax.psum((jnp.stack(grads_in), jnp.stack(grads_out)), 'dp')]
    dot_general x23 -> x0, matrix products: 1290 us -> none  [the longest x3 267 us: local_run(): jnp.einsum('btf,bsf->bts', hidden, hidden, preferred_element_type=jnp.flo...]
    pallas_call x0 -> x41, Pallas kernels: none -> 760 us  [the longest x1 514 us: run_stack(): pl.pallas_call(functools.partial(stack_kernel, n_layers, n_ex, n_steps),...]
    ppermute x0 -> x30, waiting for transfers between devices: none -> 430 us  [the longest x15 286 us: local_step(): over_y = lambda v: lax.ppermute(v, 'dp', swap_y)]
    div x2 -> x0, other arithmetic: 101 us -> none  [the longest x1 50.5 us: local_run(): grad_in = (sum_in + noise_coef * noise_in) / batch_total]
    unnamed x6 -> x20, local copies, waits for them, and re-layouts: 103 us -> 4.56 us
    mul x1 -> x0, other arithmetic: 72.1 us -> none  [gelu_parts(): norm_cdf = 0.5 * (1.0 + lax.erf(u_wide * INV_SQRT2))]
    another operation x2 -> x33, other arithmetic: 66.9 us -> 2.48 us  [the longest x24 1.8 us: put_piece(): args = [jnp.stack([jnp.int32(layer), quarter]), coef, piece, noise]]
  transfers between devices with their start and end apart: 3 -> 30, of which waited for: 1 -> 15; matrix products, arithmetic and copies ran while one was open for 18% -> 0% of each run, Pallas kernels for 0% -> 19%
where the time goes in v3:
time: 1230 us
  Pallas kernels  760 us (62%)
  waiting for transfers between devices  430 us (35%)
  starting transfers between devices  28.8 us (2%)
    pallas_call x1, Pallas kernels, run_stack(): pl.pallas_call(functools.partial(stack_kernel, n_layers, n_ex, n_steps),...  514 us
    ppermute x15, waiting for transfers between devices, local_step(): over_y = lambda v: lax.ppermute(v, 'dp', swap_y)  286 us
    ppermute x15, waiting for transfers between devices, local_step(): over_x = lambda v: lax.ppermute(v, 'dp', swap_x)  144 us
    pallas_call x24, Pallas kernels, put_piece(): pl.pallas_call(put_out_kernel if transposed else put_in_kernel, out_shape...  138 us
    pallas_call x16, Pallas kernels, mix(): pl.pallas_call(mix_kernel, out_shape=jax.ShapeDtypeStruct((rows, width),...  108 us
  transfers between devices with their start and end apart: 30, of which 15 were waited for; matrix products, arithmetic and copies ran while one was open for 0% of the time, Pallas kernels for 19%

profile of v3, /device:TPU:0, one launch (start us, length us, event | category | flops | bytes accessed | tf_op | source)
XLA Modules:
  0.0 1232.2 jit_solution(11246116807432224973)
XLA Ops:
  0.6 513.6 %stack.294 = (bf16[4,2048,1408]{2,1,0:T(8,128)(2,1)}, bf16[4,2048,1408]{2,1,0:T(8,128)(2,1)}, bf16[2,2048,1408]{2,1,0:T(8,128)(2,1)}, f32[4,704,3072]{2,1,0:T(8,...) custom-call(bf16[3,2,2048,3072]{3,2,1,0:T(8,128)(2,1)} %u_ref.1, ...), custom_call_target="tpu_custom_call" | custom-call | flops 389768282112 | bytes 500000000 | tf_op jit(solution)/shard_map/stack/pallas_call | solution.py:281
  522.8 5.3 mix.17
  528.8 5.9 mix.25
  535.2 6.0 mix.20
  543.3 5.5 mix.16
  550.1 5.9 mix.24
  556.0 7.4 mix.22
  563.5 7.3 mix.28
  570.8 7.3 mix.30
  586.4 44.8 %collective-permute-done.7 = bf16[352,3072]{1,0:T(8,128)(2,1)S(1)} collective-permute-done((bf16[352,3072]{1,0:T(8,128)(2,1)S(1)}, bf16[352,3072]{1,0:T(8,128)(2,1)S(1)}, u32[]{:S(2)}, u32[]{:S(2)}) %collective-permute-start.7) | collective-permute-done | bytes 2162720 | tf_op jit(solution)/shard_map/ppermute | solution.py:376
  633.0 6.5 mix.18
  639.5 6.6 mix.26
  646.0 7.2 mix.21.piece_ref
  653.2 24.4 %collective-permute-done.11 = bf16[352,3072]{1,0:T(8,128)(2,1)} collective-permute-done((bf16[352,3072]{1,0:T(8,128)(2,1)}, bf16[352,3072]{1,0:T(8,128)(2,1)}, u32[]{:S(2)}, u32[]{:S(2)}) %collective-permute-start.11) | collective-permute-done | bytes 2162720 | tf_op jit(solution)/shard_map/ppermute | solution.py:376
  677.6 6.8 mix.23.piece_ref
  686.1 37.9 %collective-permute-done.15 = bf16[1408,768]{1,0:T(8,128)(2,1)} collective-permute-done((bf16[1408,768]{1,0:T(8,128)(2,1)}, bf16[1408,768]{1,0:T(8,128)(2,1)}, u32[]{:S(2)}, u32[]{:S(2)}) %collective-permute-start.15) | collective-permute-done | bytes 2162720 | tf_op jit(solution)/shard_map/ppermute | solution.py:376
  727.5 8.1 mix.29.piece_ref
  735.6 8.0 mix.31.piece_ref
  743.6 26.7 %collective-permute-done.2 = bf16[352,3072]{1,0:T(8,128)(2,1)} collective-permute-done((bf16[352,3072]{1,0:T(8,128)(2,1)}, bf16[352,3072]{1,0:T(8,128)(2,1)}, u32[]{:S(2)}, u32[]{:S(2)}) %collective-permute-start.2) | collective-permute-done | bytes 2162720 | tf_op jit(solution)/shard_map/ppermute | solution.py:376
  772.3 44.3 %collective-permute-done.8.piece_ref = bf16[352,3072]{1,0:T(8,128)(2,1)} collective-permute-done((bf16[352,3072]{1,0:T(8,128)(2,1)}, bf16[352,3072]{1,0:T(8,128)(2,1)}, u32[]{:S(2)}, u32[]{:S(2)}) %collective-permute-start.8) | collective-permute-done | bytes 2162720 | tf_op jit(solution)/shard_map/ppermute | solution.py:376
  818.3 44.7 %collective-permute-done.12.piece_ref = bf16[352,3072]{1,0:T(8,128)(2,1)} collective-permute-done((bf16[352,3072]{1,0:T(8,128)(2,1)S(1)}, bf16[352,3072]{1,0:T(8,128)(2,1)}, u32[]{:S(2)}, u32[]{:S(2)}) %collective-permute-start.12) | collective-permute-done | bytes 2162720 | tf_op jit(solution)/shard_map/ppermute | solution.py:376
  863.1 7.3 mix.19.piece_ref
  870.4 7.4 mix.27.piece_ref
  879.8 23.0 %collective-permute-done.23.piece_ref = bf16[1408,768]{1,0:T(8,128)(2,1)} collective-permute-done((bf16[1408,768]{1,0:T(8,128)(2,1)}, bf16[1408,768]{1,0:T(8,128)(2,1)}, u32[]{:S(2)}, u32[]{:S(2)}) %collective-permute-start.23) | collective-permute-done | bytes 2162720 | tf_op jit(solution)/shard_map/ppermute | solution.py:375
  903.3 6.0 collective-permute-done.25.piece_ref
  910.8 38.3 %collective-permute-done.27.piece_ref = bf16[1408,768]{1,0:T(8,128)(2,1)} collective-permute-done((bf16[1408,768]{1,0:T(8,128)(2,1)}, bf16[1408,768]{1,0:T(8,128)(2,1)}, u32[]{:S(2)}, u32[]{:S(2)}) %collective-permute-start.27) | collective-permute-done | bytes 2162720 | tf_op jit(solution)/shard_map/ppermute | solution.py:375
  949.7 6.0 collective-permute-done.29.piece_ref
  956.1 46.0 %collective-permute-done.3.piece_ref = bf16[352,3072]{1,0:T(8,128)(2,1)} collective-permute-done((bf16[352,3072]{1,0:T(8,128)(2,1)}, bf16[352,3072]{1,0:T(8,128)(2,1)}, u32[]{:S(2)}, u32[]{:S(2)}) %collective-permute-start.3) | collective-permute-done | bytes 2162720 | tf_op jit(solution)/shard_map/ppermute | solution.py:376
  1003.6 38.1 %collective-permute-done.9.piece_ref = bf16[352,3072]{1,0:T(8,128)(2,1)S(1)} collective-permute-done((bf16[352,3072]{1,0:T(8,128)(2,1)}, bf16[352,3072]{1,0:T(8,128)(2,1)S(1)}, u32[]{:S(2)}, u32[]{:S(2)}) %collective-permute-start.9) | collective-permute-done | bytes 2162720 | tf_op jit(solution)/shard_map/ppermute | solution.py:375
  1043.2 44.8 %collective-permute-done.13.piece_ref = bf16[352,3072]{1,0:T(8,128)(2,1)S(1)} collective-permute-done((bf16[352,3072]{1,0:T(8,128)(2,1)}, bf16[352,3072]{1,0:T(8,128)(2,1)S(1)}, u32[]{:S(2)}, u32[]{:S(2)}) %collective-permute-start.13) | collective-permute-done | bytes 2162720 | tf_op jit(solution)/shard_map/ppermute | solution.py:375
  1098.1 6.6 put_out.12.rest_0_
  1104.6 5.1 put_in.13.rest_0_
  1109.8 6.6 put_out.13.rest_0_
  1116.3 5.1 put_in.14.rest_0_
  1121.5 6.8 put_out.14.rest_0_
  1143.0 5.2 put_in.18.rest_0_
  1152.7 5.2 put_in.20.rest_0_
  1157.9 6.1 put_out.15.rest_0_
  1164.0 6.6 put_out.16.rest_0_
  1170.6 6.6 put_out.17.rest_0_
  1177.1 6.6 put_out.18.rest_0_
  1183.7 6.6 put_out.19.rest_0_
  1190.3 6.6 put_out.20.rest_0_
  1202.0 6.6 put_out.21.rest_0_
  1208.5 5.1 put_in.22.rest_0_
  1213.7 6.6 put_out.22.rest_0_
  1220.2 5.1 put_in.23
  1225.4 6.6 put_out.23
  (114 shorter events, 73.5 us)
Async XLA Ops:
  518.4 16.4 %collective-permute-start.21 = (f32[2]{0:T(128)S(1)}, f32[2]{0:T(128)S(1)}, u32[]{:S(2)}, u32[]{:S(2)}) collective-permute-start(f32[2]{0:T(128)S(1)} %multiply_minimum_fusion.coef_ref), channel_id=1, source_target_pairs={{0,4},{2,6},{4,0},{6,2},{1,5},{3,7},{5,1},{7,3}} | collective-permute-start | bytes 32 | tf_op jit(solution)/shard_map/ppermute | solution.py:376
  521.3 13.5 %collective-permute-start.6 = (f32[2]{0:T(128)S(1)}, f32[2]{0:T(128)S(1)}, u32[]{:S(2)}, u32[]{:S(2)}) collective-permute-start(f32[2]{0:T(128)S(1)} %multiply_minimum_fusion.coef_ref), channel_id=1, source_target_pairs={{0,2},{2,0},{4,6},{6,4},{1,3},{3,1},{5,7},{7,5}} | collective-permute-start | bytes 32 | tf_op jit(solution)/shard_map/ppermute | solution.py:375
  528.1 50.2 %collective-permute-start.1 = (bf16[352,3072]{1,0:T(8,128)(2,1)}, bf16[352,3072]{1,0:T(8,128)(2,1)}, u32[]{:S(2)}, u32[]{:S(2)}) collective-permute-start(bf16[352,3072]{1,0:T(8,128)(2,1)} %mix.17), channel_id=1, source_target_pairs={{0,2},{2,0},{4,6},{6,4},{1,3},{3,1},{5,7},{7,5}} | collective-permute-start | bytes 6488072 | tf_op jit(solution)/shard_map/ppermute | solution.py:375
  534.7 50.2 %collective-permute-start.16 = (bf16[1408,768]{1,0:T(8,128)(2,1)}, bf16[1408,768]{1,0:T(8,128)(2,1)}, u32[]{:S(2)}, u32[]{:S(2)}) collective-permute-start(bf16[1408,768]{1,0:T(8,128)(2,1)} %mix.25), channel_id=1, source_target_pairs={{0,4},{2,6},{4,0},{6,2},{1,5},{3,7},{5,1},{7,3}} | collective-permute-start | bytes 6488072 | tf_op jit(solution)/shard_map/ppermute | solution.py:376
  534.7 0.5 copy-start.6
  534.7 0.5 copy-start.8
  541.2 89.9 %collective-permute-start.7 = (bf16[352,3072]{1,0:T(8,128)(2,1)S(1)}, bf16[352,3072]{1,0:T(8,128)(2,1)S(1)}, u32[]{:S(2)}, u32[]{:S(2)}) collective-permute-start(bf16[352,3072]{1,0:T(8,128)(2,1)S(1)} %mix.20), channel_id=1, source_target_pairs={{0,4},{2,6},{4,0},{6,2},{1,5},{3,7},{5,1},{7,3}} | collective-permute-start | bytes 6488072 | tf_op jit(solution)/shard_map/ppermute | solution.py:376
  548.7 135.7 %collective-permute-start = (bf16[352,3072]{1,0:T(8,128)(2,1)}, bf16[352,3072]{1,0:T(8,128)(2,1)}, u32[]{:S(2)}, u32[]{:S(2)}) collective-permute-start(bf16[352,3072]{1,0:T(8,128)(2,1)} %mix.16), channel_id=1, source_target_pairs={{0,2},{2,0},{4,6},{6,4},{1,3},{3,1},{5,7},{7,5}} | collective-permute-start | bytes 6488072 | tf_op jit(solution)/shard_map/ppermute | solution.py:375
  563.4 114.2 %collective-permute-start.11 = (bf16[352,3072]{1,0:T(8,128)(2,1)}, bf16[352,3072]{1,0:T(8,128)(2,1)}, u32[]{:S(2)}, u32[]{:S(2)}) collective-permute-start(bf16[352,3072]{1,0:T(8,128)(2,1)} %mix.22), channel_id=1, source_target_pairs={{0,4},{2,6},{4,0},{6,2},{1,5},{3,7},{5,1},{7,3}} | collective-permute-start | bytes 6488072 | tf_op jit(solution)/shard_map/ppermute | solution.py:376
  570.8 62.1 %copy-start.7 = (f32[2]{0:T(128)S(1)}, f32[2]{0:T(128)}, u32[]{:S(2)}) copy-start(f32[2]{0:T(128)} %copy-done.6) | copy-start | bytes 28
  570.8 62.1 %copy-start.9 = (f32[2]{0:T(128)S(1)}, f32[2]{0:T(128)}, u32[]{:S(2)}) copy-start(f32[2]{0:T(128)} %copy-done.8) | copy-start | bytes 28
  578.4 145.6 %collective-permute-start.15 = (bf16[1408,768]{1,0:T(8,128)(2,1)}, bf16[1408,768]{1,0:T(8,128)(2,1)}, u32[]{:S(2)}, u32[]{:S(2)}) collective-permute-start(bf16[1408,768]{1,0:T(8,128)(2,1)} %mix.24), channel_id=1, source_target_pairs={{0,4},{2,6},{4,0},{6,2},{1,5},{3,7},{5,1},{7,3}} | collective-permute-start | bytes 6488072 | tf_op jit(solution)/shard_map/ppermute | solution.py:376
  584.9 139.1 %collective-permute-start.22 = (bf16[1408,768]{1,0:T(8,128)(2,1)}, bf16[1408,768]{1,0:T(8,128)(2,1)}, u32[]{:S(2)}, u32[]{:S(2)}) collective-permute-start(bf16[1408,768]{1,0:T(8,128)(2,1)} %mix.28), channel_id=1, source_target_pairs={{0,2},{2,0},{4,6},{6,4},{1,3},{3,1},{5,7},{7,5}} | collective-permute-start | bytes 6488072 | tf_op jit(solution)/shard_map/ppermute | solution.py:375
  631.2 94.4 %collective-permute-start.26 = (bf16[1408,768]{1,0:T(8,128)(2,1)}, bf16[1408,768]{1,0:T(8,128)(2,1)}, u32[]{:S(2)}, u32[]{:S(2)}) collective-permute-start(bf16[1408,768]{1,0:T(8,128)(2,1)} %mix.30), channel_id=1, source_target_pairs={{0,2},{2,0},{4,6},{6,4},{1,3},{3,1},{5,7},{7,5}} | collective-permute-start | bytes 6488072 | tf_op jit(solution)/shard_map/ppermute | solution.py:375
  677.6 92.7 %collective-permute-start.2 = (bf16[352,3072]{1,0:T(8,128)(2,1)}, bf16[352,3072]{1,0:T(8,128)(2,1)}, u32[]{:S(2)}, u32[]{:S(2)}) collective-permute-start(bf16[352,3072]{1,0:T(8,128)(2,1)} %mix.18), channel_id=1, source_target_pairs={{0,4},{2,6},{4,0},{6,2},{1,5},{3,7},{5,1},{7,3}} | collective-permute-start | bytes 6488072 | tf_op jit(solution)/shard_map/ppermute | solution.py:376
  684.5 87.3 %collective-permute-start.17 = (bf16[1408,768]{1,0:T(8,128)(2,1)}, bf16[1408,768]{1,0:T(8,128)(2,1)}, u32[]{:S(2)}, u32[]{:S(2)}) collective-permute-start(bf16[1408,768]{1,0:T(8,128)(2,1)} %mix.26), channel_id=1, source_target_pairs={{0,2},{2,0},{4,6},{6,4},{1,3},{3,1},{5,7},{7,5}} | collective-permute-start | bytes 6488072 | tf_op jit(solution)/shard_map/ppermute | solution.py:375
  724.0 92.7 %collective-permute-start.8 = (bf16[352,3072]{1,0:T(8,128)(2,1)}, bf16[352,3072]{1,0:T(8,128)(2,1)}, u32[]{:S(2)}, u32[]{:S(2)}) collective-permute-start(bf16[352,3072]{1,0:T(8,128)(2,1)} %mix.21.piece_ref), channel_id=1, source_target_pairs={{0,4},{2,6},{4,0},{6,2},{1,5},{3,7},{5,1},{7,3}} | collective-permute-start | bytes 6488072 | tf_op jit(solution)/shard_map/ppermute | solution.py:376
  724.0 92.7 %collective-permute-start.10 = (bf16[352,3072]{1,0:T(8,128)(2,1)}, bf16[352,3072]{1,0:T(8,128)(2,1)}, u32[]{:S(2)}, u32[]{:S(2)}) collective-permute-start(bf16[352,3072]{1,0:T(8,128)(2,1)} %mix.21.piece_ref), channel_id=1, source_target_pairs={{0,2},{2,0},{4,6},{6,4},{1,3},{3,1},{5,7},{7,5}} | collective-permute-start | bytes 6488072 | tf_op jit(solution)/shard_map/ppermute | solution.py:375
  725.6 137.4 %collective-permute-start.12 = (bf16[352,3072]{1,0:T(8,128)(2,1)S(1)}, bf16[352,3072]{1,0:T(8,128)(2,1)}, u32[]{:S(2)}, u32[]{:S(2)}) collective-permute-start(bf16[352,3072]{1,0:T(8,128)(2,1)S(1)} %mix.23.piece_ref), channel_id=1, source_target_pairs={{0,4},{2,6},{4,0},{6,2},{1,5},{3,7},{5,1},{7,3}} | collective-permute-start | bytes 6488072 | tf_op jit(solution)/shard_map/ppermute | solution.py:376
  770.3 107.5 %collective-permute-start.14 = (bf16[352,3072]{1,0:T(8,128)(2,1)S(1)}, bf16[352,3072]{1,0:T(8,128)(2,1)}, u32[]{:S(2)}, u32[]{:S(2)}) collective-permute-start(bf16[352,3072]{1,0:T(8,128)(2,1)S(1)} %mix.23.piece_ref), channel_id=1, source_target_pairs={{0,2},{2,0},{4,6},{6,4},{1,3},{3,1},{5,7},{7,5}} | collective-permute-start | bytes 6488072 | tf_op jit(solution)/shard_map/ppermute | solution.py:375
  771.8 131.0 %collective-permute-start.23 = (bf16[1408,768]{1,0:T(8,128)(2,1)}, bf16[1408,768]{1,0:T(8,128)(2,1)}, u32[]{:S(2)}, u32[]{:S(2)}) collective-permute-start(bf16[1408,768]{1,0:T(8,128)(2,1)} %mix.29.piece_ref), channel_id=1, source_target_pairs={{0,2},{2,0},{4,6},{6,4},{1,3},{3,1},{5,7},{7,5}} | collective-permute-start | bytes 6488072 | tf_op jit(solution)/shard_map/ppermute | solution.py:375
  816.7 92.7 %collective-permute-start.25 = (bf16[1408,768]{1,0:T(8,128)(2,1)}, bf16[1408,768]{1,0:T(8,128)(2,1)}, u32[]{:S(2)}, u32[]{:S(2)}) collective-permute-start(bf16[1408,768]{1,0:T(8,128)(2,1)} %mix.29.piece_ref), channel_id=1, source_target_pairs={{0,4},{2,6},{4,0},{6,2},{1,5},{3,7},{5,1},{7,3}} | collective-permute-start | bytes 6488072 | tf_op jit(solution)/shard_map/ppermute | solution.py:376
  816.7 132.5 %collective-permute-start.27 = (bf16[1408,768]{1,0:T(8,128)(2,1)}, bf16[1408,768]{1,0:T(8,128)(2,1)}, u32[]{:S(2)}, u32[]{:S(2)}) collective-permute-start(bf16[1408,768]{1,0:T(8,128)(2,1)} %mix.31.piece_ref), channel_id=1, source_target_pairs={{0,2},{2,0},{4,6},{6,4},{1,3},{3,1},{5,7},{7,5}} | collective-permute-start | bytes 6488072 | tf_op jit(solution)/shard_map/ppermute | solution.py:375
  863.0 92.7 %collective-permute-start.29 = (bf16[1408,768]{1,0:T(8,128)(2,1)}, bf16[1408,768]{1,0:T(8,128)(2,1)}, u32[]{:S(2)}, u32[]{:S(2)}) collective-permute-start(bf16[1408,768]{1,0:T(8,128)(2,1)} %mix.31.piece_ref), channel_id=1, source_target_pairs={{0,4},{2,6},{4,0},{6,2},{1,5},{3,7},{5,1},{7,3}} | collective-permute-start | bytes 6488072 | tf_op jit(solution)/shard_map/ppermute | solution.py:376
  877.8 124.3 %collective-permute-start.3 = (bf16[352,3072]{1,0:T(8,128)(2,1)}, bf16[352,3072]{1,0:T(8,128)(2,1)}, u32[]{:S(2)}, u32[]{:S(2)}) collective-permute-start(bf16[352,3072]{1,0:T(8,128)(2,1)} %mix.19.piece_ref), channel_id=1, source_target_pairs={{0,4},{2,6},{4,0},{6,2},{1,5},{3,7},{5,1},{7,3}} | collective-permute-start | bytes 6488072 | tf_op jit(solution)/shard_map/ppermute | solution.py:376
  902.8 100.7 %collective-permute-start.18 = (bf16[1408,768]{1,0:T(8,128)(2,1)}, bf16[1408,768]{1,0:T(8,128)(2,1)}, u32[]{:S(2)}, u32[]{:S(2)}) collective-permute-start(bf16[1408,768]{1,0:T(8,128)(2,1)} %mix.27.piece_ref), channel_id=1, source_target_pairs={{0,2},{2,0},{4,6},{6,4},{1,3},{3,1},{5,7},{7,5}} | collective-permute-start | bytes 6488072 | tf_op jit(solution)/shard_map/ppermute | solution.py:375
  909.3 132.4 %collective-permute-start.9 = (bf16[352,3072]{1,0:T(8,128)(2,1)}, bf16[352,3072]{1,0:T(8,128)(2,1)S(1)}, u32[]{:S(2)}, u32[]{:S(2)}) collective-permute-start(bf16[352,3072]{1,0:T(8,128)(2,1)} %collective-permute-done.8.piece_ref), channel_id=1, source_target_pairs={{0,2},{2,0},{4,6},{6,4},{1,3},{3,1},{5,7},{7,5}} | collective-permute-start | bytes 6488072 | tf_op jit(solution)/shard_map/ppermute | solution.py:375
  949.1 138.9 %collective-permute-start.13 = (bf16[352,3072]{1,0:T(8,128)(2,1)}, bf16[352,3072]{1,0:T(8,128)(2,1)S(1)}, u32[]{:S(2)}, u32[]{:S(2)}) collective-permute-start(bf16[352,3072]{1,0:T(8,128)(2,1)} %collective-permute-done.12.piece_ref), channel_id=1, source_target_pairs={{0,2},{2,0},{4,6},{6,4},{1,3},{3,1},{5,7},{7,5}} | collective-permute-start | bytes 6488072 | tf_op jit(solution)/shard_map/ppermute | solution.py:375
  955.7 134.3 %collective-permute-start.28 = (bf16[1408,768]{1,0:T(8,128)(2,1)}, bf16[1408,768]{1,0:T(8,128)(2,1)S(1)}, u32[]{:S(2)}, u32[]{:S(2)}) collective-permute-start(bf16[1408,768]{1,0:T(8,128)(2,1)} %collective-permute-done.27.piece_ref), channel_id=1, source_target_pairs={{0,4},{2,6},{4,0},{6,2},{1,5},{3,7},{5,1},{7,3}} | collective-permute-start | bytes 6488072 | tf_op jit(solution)/shard_map/ppermute | solution.py:376
  1002.0 206.5 %collective-permute-start.5 = (bf16[352,3072]{1,0:T(8,128)(2,1)}, bf16[352,3072]{1,0:T(8,128)(2,1)}, u32[]{:S(2)}, u32[]{:S(2)}) collective-permute-start(bf16[352,3072]{1,0:T(8,128)(2,1)} %mix.19.piece_ref), channel_id=1, source_target_pairs={{0,2},{2,0},{4,6},{6,4},{1,3},{3,1},{5,7},{7,5}} | collective-permute-start | bytes 6488072 | tf_op jit(solution)/shard_map/ppermute | solution.py:375
  1003.5 210.2 %collective-permute-start.20 = (bf16[1408,768]{1,0:T(8,128)(2,1)}, bf16[1408,768]{1,0:T(8,128)(2,1)}, u32[]{:S(2)}, u32[]{:S(2)}) collective-permute-start(bf16[1408,768]{1,0:T(8,128)(2,1)} %mix.27.piece_ref), channel_id=1, source_target_pairs={{0,4},{2,6},{4,0},{6,2},{1,5},{3,7},{5,1},{7,3}} | collective-permute-start | bytes 6488072 | tf_op jit(solution)/shard_map/ppermute | solution.py:376
  1041.7 1.4 copy-start
  1043.1 140.6 %collective-permute-start.24 = (bf16[1408,768]{1,0:T(8,128)(2,1)}, bf16[1408,768]{1,0:T(8,128)(2,1)}, u32[]{:S(2)}, u32[]{:S(2)}) collective-permute-start(bf16[1408,768]{1,0:T(8,128)(2,1)} %collective-permute-done.23.piece_ref), channel_id=1, source_target_pairs={{0,4},{2,6},{4,0},{6,2},{1,5},{3,7},{5,1},{7,3}} | collective-permute-start | bytes 6488072 | tf_op jit(solution)/shard_map/ppermute | solution.py:376
  1088.1 1.3 copy-start.4
  1089.4 130.8 %collective-permute-start.4 = (bf16[352,3072]{1,0:T(8,128)(2,1)}, bf16[352,3072]{1,0:T(8,128)(2,1)}, u32[]{:S(2)}, u32[]{:S(2)}) collective-permute-start(bf16[352,3072]{1,0:T(8,128)(2,1)} %collective-permute-done.3.piece_ref), channel_id=1, source_target_pairs={{0,2},{2,0},{4,6},{6,4},{1,3},{3,1},{5,7},{7,5}} | collective-permute-start | bytes 6488072 | tf_op jit(solution)/shard_map/ppermute | solution.py:375
  1090.0 1.4 copy-start.2
  1091.4 134.0 %collective-permute-start.19 = (bf16[1408,768]{1,0:T(8,128)(2,1)}, bf16[1408,768]{1,0:T(8,128)(2,1)}, u32[]{:S(2)}, u32[]{:S(2)}) collective-permute-start(bf16[1408,768]{1,0:T(8,128)(2,1)} %collective-permute-done.18.piece_ref), channel_id=1, source_target_pairs={{0,4},{2,6},{4,0},{6,2},{1,5},{3,7},{5,1},{7,3}} | collective-permute-start | bytes 6488072 | tf_op jit(solution)/shard_map/ppermute | solution.py:376
  1121.5 6.8 copy-start.5
  1143.0 5.2 copy-start.1
  1152.7 5.2 copy-start.3

commit v4 on v3

--- a/solution.py
+++ b/solution.py
@@ -12,7 +12,7 @@
 LOG2_E = 1.4426950408889634
 F_BLOCK = 512
 T_CHUNK = 256
-IN_SLOTS = 3
+IN_SLOTS = 4
 ROW_STEPS = 2
 VMEM_LIMIT = 66_500_000
 
@@ -212,11 +212,11 @@
 
     @pl.when(task < n_early)
     def _():
-        lax.fori_loop(0, ROW_STEPS, functools.partial(weight_grads, True), 0)
+        lax.fori_loop(0, ROW_STEPS, functools.partial(weight_grads, True), 0, unroll=True)
 
     @pl.when(task >= n_early)
     def _():
-        lax.fori_loop(0, ROW_STEPS, functools.partial(weight_grads, False), 0)
+        lax.fori_loop(0, ROW_STEPS, functools.partial(weight_grads, False), 0, unroll=True)
 
     @pl.when(ends_early)
     def _():
@@ -384,7 +384,6 @@
 
         noise_in4 = noise_in.reshape(n_layers, 4, d_model // 4, d_ff)
         noise_out4 = noise_out.reshape(n_layers, 4, d_ff // 4, d_model)
-        grad_in = grad_out = None
 
         shapes = ((d_model // 4, d_ff), (d_model, d_ff // 4))
         at_half, at_side = (x_pos, y_pos), (y_pos, x_pos)
@@ -416,17 +415,24 @@
             terms += [(v[None], 0, 0) for v in more]
             return mix(which, shapes[which], terms, coefs + [1.0] * len(more))
 
+        places = {}
         for layer in range(n_layers - 1, -1, -1):
             got = [over_side[which](pair_sum(layer, which, True)) for which in (0, 1)]
-            own1, own2 = [pair_sum(layer, which, False, got[which]) for which in (0, 1)]
-            near1, near2 = over_y(own1), over_x(own2)
-            side1, side2 = over_x(own1), over_y(own2)
-            diag1, diag2 = over_x(near1), over_y(near2)
-            q1 = lambda a, b: 2 * a + b
-            for a, b, v in ((x_pos, y_pos, own1), (x_pos, 1 - y_pos, near1), (1 - x_pos, y_pos, side1), (1 - x_pos, 1 - y_pos, diag1)):
-                grad_in = put_piece(False, grad_in, layer, q1(a, b), coef, v, noise_in4)
-            for a, b, v in ((y_pos, x_pos, own2), (y_pos, 1 - x_pos, near2), (1 - y_pos, x_pos, side2), (1 - y_pos, 1 - x_pos, diag2)):
-                grad_out = put_piece(True, grad_out, layer, q1(a, b), coef, v, noise_out4)
+            for which in (0, 1):
+                half_pos, pos = at_half[which], at_side[which]
+                own = pair_sum(layer, which, False, got[which])
+                near, side = over_side[which](own), over_half[which](own)
+                diag = over_half[which](near)
+                places[layer, which] = (
+                    (2 * half_pos + pos, own), (2 * half_pos + 1 - pos, near),
+                    (2 * (1 - half_pos) + pos, side), (2 * (1 - half_pos) + 1 - pos, diag))
+        grads, noises = [None, None], (noise_in4, noise_out4)
+        for kind in range(4):
+            for layer in range(n_layers - 1, -1, -1):
+                for which in (0, 1):
+                    at, piece = places[layer, which][kind]
+                    grads[which] = put_piece(which == 1, grads[which], layer, at, coef, piece, noises[which])
+        grad_in, grad_out = grads
         return grad_in.reshape(n_layers, d_model, d_ff), grad_out.reshape(n_layers, d_ff, d_model)
 
     return jax.shard_map(

time: 1230 us -> 1250 us (1.016); the launches traced: 1230 us -> 1220 us
    ppermute x15, waiting for transfers between devices: 286 us -> 144 us  [local_step(): over_y = lambda v: lax.ppermute(v, 'dp', swap_y)]
    ppermute x15, waiting for transfers between devices: 144 us -> 280 us  [local_step(): over_x = lambda v: lax.ppermute(v, 'dp', swap_x)]
  transfers between devices with their start and end apart: 30 -> 30, of which waited for: 15 -> 14; matrix products, arithmetic and copies ran while one was open for 0% -> 0% of each run, Pallas kernels for 19% -> 20%
where the time goes in v4:
time: 1250 us; the launch traced here: 1220 us
  Pallas kernels  756 us (60%)
  waiting for transfers between devices  424 us (34%)
  starting transfers between devices  35.3 us (3%)
    pallas_call x1, Pallas kernels, run_stack(): pl.pallas_call(functools.partial(stack_kernel, n_layers, n_ex, n_steps),...  506 us
    ppermute x15, waiting for transfers between devices, local_step(): over_x = lambda v: lax.ppermute(v, 'dp', swap_x)  280 us
    ppermute x15, waiting for transfers between devices, local_step(): over_y = lambda v: lax.ppermute(v, 'dp', swap_y)  144 us
    pallas_call x24, Pallas kernels, put_piece(): pl.pallas_call(put_out_kernel if transposed else put_in_kernel, out_shape...  140 us
    pallas_call x16, Pallas kernels, mix(): pl.pallas_call(mix_kernel, out_shape=jax.ShapeDtypeStruct((rows, width),...  111 us
  transfers between devices with their start and end apart: 30, of which 14 were waited for; matrix products, arithmetic and copies ran while one was open for 0% of the time, Pallas kernels for 20%

profile of v4, /device:TPU:0, one launch (start us, length us, event | category | flops | bytes accessed | tf_op | source)
XLA Modules:
  0.0 1224.4 jit_solution(15551614397589298547)
XLA Ops:
  0.6 505.8 %stack.306 = (bf16[4,2048,1408]{2,1,0:T(8,128)(2,1)}, bf16[4,2048,1408]{2,1,0:T(8,128)(2,1)}, bf16[2,2048,1408]{2,1,0:T(8,128)(2,1)}, f32[4,704,3072]{2,1,0:T(8,...) custom-call(bf16[3,2,2048,3072]{3,2,1,0:T(8,128)(2,1)} %u_ref.1, ...), custom_call_target="tpu_custom_call" | custom-call | flops 389768282112 | bytes 500000000 | tf_op jit(solution)/shard_map/stack/pallas_call | solution.py:281
  515.3 5.9 mix.25
  521.3 5.3 mix.17
  527.8 7.3 mix.30
  536.6 5.9 mix.24
  544.6 5.3 mix.16
  549.9 7.3 mix.28
  557.8 7.4 mix.22
  565.1 7.3 mix.20
  578.8 44.2 %collective-permute-done.24 = bf16[1408,768]{1,0:T(8,128)(2,1)S(1)} collective-permute-done((bf16[1408,768]{1,0:T(8,128)(2,1)}, bf16[1408,768]{1,0:T(8,128)(2,1)S(1)}, u32[]{:S(2)}, u32[]{:S(2)}) %collective-permute-start.24) | collective-permute-done | bytes 2162720 | tf_op jit(solution)/shard_map/ppermute | solution.py:375
  625.5 6.6 mix.26
  632.1 6.5 mix.18
  638.7 6.4 mix.31.piece_ref
  645.1 24.5 %collective-permute-done.21 = bf16[1408,768]{1,0:T(8,128)(2,1)} collective-permute-done((bf16[1408,768]{1,0:T(8,128)(2,1)}, bf16[1408,768]{1,0:T(8,128)(2,1)}, u32[]{:S(2)}, u32[]{:S(2)}) %collective-permute-start.21) | collective-permute-done | bytes 2162720 | tf_op jit(solution)/shard_map/ppermute | solution.py:375
  670.1 8.0 mix.29.piece_ref
  680.1 35.8 %collective-permute-done = bf16[352,3072]{1,0:T(8,128)(2,1)} collective-permute-done((bf16[352,3072]{1,0:T(8,128)(2,1)}, bf16[352,3072]{1,0:T(8,128)(2,1)}, u32[]{:S(2)}, u32[]{:S(2)}) %collective-permute-start) | collective-permute-done | bytes 2162720 | tf_op jit(solution)/shard_map/ppermute | solution.py:375
  720.0 8.2 mix.23.piece_ref
  728.2 8.1 mix.21.piece_ref
  736.3 25.9 %collective-permute-done.17 = bf16[1408,768]{1,0:T(8,128)(2,1)} collective-permute-done((bf16[1408,768]{1,0:T(8,128)(2,1)}, bf16[1408,768]{1,0:T(8,128)(2,1)}, u32[]{:S(2)}, u32[]{:S(2)}) %collective-permute-start.17) | collective-permute-done | bytes 2162720 | tf_op jit(solution)/shard_map/ppermute | solution.py:375
  764.3 44.3 %collective-permute-done.25.piece_ref = bf16[1408,768]{1,0:T(8,128)(2,1)} collective-permute-done((bf16[1408,768]{1,0:T(8,128)(2,1)S(1)}, bf16[1408,768]{1,0:T(8,128)(2,1)}, u32[]{:S(2)}, u32[]{:S(2)}) %collective-permute-start.25) | collective-permute-done | bytes 2162720 | tf_op jit(solution)/shard_map/ppermute | solution.py:375
  810.6 43.0 %collective-permute-done.22.piece_ref = bf16[1408,768]{1,0:T(8,128)(2,1)} collective-permute-done((bf16[1408,768]{1,0:T(8,128)(2,1)}, bf16[1408,768]{1,0:T(8,128)(2,1)}, u32[]{:S(2)}, u32[]{:S(2)}) %collective-permute-start.22) | collective-permute-done | bytes 2162720 | tf_op jit(solution)/shard_map/ppermute | solution.py:375
  855.7 7.3 mix.27.piece_ref
  863.0 7.4 mix.19.piece_ref
  871.0 24.8 %collective-permute-done.10.piece_ref = bf16[352,3072]{1,0:T(8,128)(2,1)} collective-permute-done((bf16[352,3072]{1,0:T(8,128)(2,1)}, bf16[352,3072]{1,0:T(8,128)(2,1)}, u32[]{:S(2)}, u32[]{:S(2)}) %collective-permute-start.10) | collective-permute-done | bytes 2162720 | tf_op jit(solution)/shard_map/ppermute | solution.py:376
  895.8 46.3 %collective-permute-done.7.piece_ref = bf16[352,3072]{1,0:T(8,128)(2,1)} collective-permute-done((bf16[352,3072]{1,0:T(8,128)(2,1)}, bf16[352,3072]{1,0:T(8,128)(2,1)}, u32[]{:S(2)}, u32[]{:S(2)}) %collective-permute-start.7) | collective-permute-done | bytes 2162720 | tf_op jit(solution)/shard_map/ppermute | solution.py:376
  942.8 7.4 collective-permute-done.13.piece_ref
  952.2 44.3 %collective-permute-done.18.piece_ref = bf16[1408,768]{1,0:T(8,128)(2,1)} collective-permute-done((bf16[1408,768]{1,0:T(8,128)(2,1)}, bf16[1408,768]{1,0:T(8,128)(2,1)}, u32[]{:S(2)}, u32[]{:S(2)}) %collective-permute-start.18) | collective-permute-done | bytes 2162720 | tf_op jit(solution)/shard_map/ppermute | solution.py:375
  998.8 36.1 %collective-permute-done.3.piece_ref = bf16[352,3072]{1,0:T(8,128)(2,1)} collective-permute-done((bf16[352,3072]{1,0:T(8,128)(2,1)}, bf16[352,3072]{1,0:T(8,128)(2,1)}, u32[]{:S(2)}, u32[]{:S(2)}) %collective-permute-start.3) | collective-permute-done | bytes 2162720 | tf_op jit(solution)/shard_map/ppermute | solution.py:376
  1035.4 7.4 collective-permute-done.12.piece_ref
  1044.5 36.7 %collective-permute-done.26.piece_ref = bf16[1408,768]{1,0:T(8,128)(2,1)} collective-permute-done((bf16[1408,768]{1,0:T(8,128)(2,1)}, bf16[1408,768]{1,0:T(8,128)(2,1)}, u32[]{:S(2)}, u32[]{:S(2)}) %collective-permute-start.26) | collective-permute-done | bytes 2162720 | tf_op jit(solution)/shard_map/ppermute | solution.py:376
  1083.9 6.1 put_out.12.rest_0_
  1090.0 6.6 put_out.13.rest_0_
  1106.8 6.8 put_out.14.rest_0_
  1113.6 5.1 put_in.14.rest_0_
  1118.7 6.6 put_out.15.rest_0_
  1125.3 6.6 put_out.16.rest_0_
  1137.0 5.1 put_in.16.rest_0_
  1142.1 6.6 put_out.17.rest_0_
  1148.7 5.1 put_in.17.rest_0_
  1153.8 6.6 put_out.18.rest_0_
  1160.4 6.6 put_out.19.rest_0_
  1166.9 6.6 put_out.20.rest_0_
  1188.9 6.6 put_out.21.rest_0_
  1195.5 6.6 put_out.22.rest_0_
  1202.0 5.1 put_in.21.rest_0_
  1207.2 5.1 put_in.22.rest_0_
  1212.3 6.6 put_out.23
  1218.9 5.1 put_in.23
  (107 shorter events, 75.8 us)
Async XLA Ops:
  510.5 16.7 %collective-permute-start.20 = (f32[2]{0:T(128)S(1)}, f32[2]{0:T(128)S(1)}, u32[]{:S(2)}, u32[]{:S(2)}) collective-permute-start(f32[2]{0:T(128)S(1)} %multiply_minimum_fusion.coef_ref), channel_id=1, source_target_pairs={{0,4},{2,6},{4,0},{6,2},{1,5},{3,7},{5,1},{7,3}} | collective-permute-start | bytes 32 | tf_op jit(solution)/shard_map/ppermute | solution.py:376
  513.7 13.5 %collective-permute-start.5 = (f32[2]{0:T(128)S(1)}, f32[2]{0:T(128)S(1)}, u32[]{:S(2)}, u32[]{:S(2)}) collective-permute-start(f32[2]{0:T(128)S(1)} %multiply_minimum_fusion.coef_ref), channel_id=1, source_target_pairs={{0,2},{2,0},{4,6},{6,4},{1,3},{3,1},{5,7},{7,5}} | collective-permute-start | bytes 32 | tf_op jit(solution)/shard_map/ppermute | solution.py:375
  521.2 51.3 %collective-permute-start.16 = (bf16[1408,768]{1,0:T(8,128)(2,1)}, bf16[1408,768]{1,0:T(8,128)(2,1)}, u32[]{:S(2)}, u32[]{:S(2)}) collective-permute-start(bf16[1408,768]{1,0:T(8,128)(2,1)} %mix.25), channel_id=1, source_target_pairs={{0,4},{2,6},{4,0},{6,2},{1,5},{3,7},{5,1},{7,3}} | collective-permute-start | bytes 6488072 | tf_op jit(solution)/shard_map/ppermute | solution.py:376
  526.6 50.2 %collective-permute-start.1 = (bf16[352,3072]{1,0:T(8,128)(2,1)}, bf16[352,3072]{1,0:T(8,128)(2,1)}, u32[]{:S(2)}, u32[]{:S(2)}) collective-permute-start(bf16[352,3072]{1,0:T(8,128)(2,1)} %mix.17), channel_id=1, source_target_pairs={{0,2},{2,0},{4,6},{6,4},{1,3},{3,1},{5,7},{7,5}} | collective-permute-start | bytes 6488072 | tf_op jit(solution)/shard_map/ppermute | solution.py:375
  527.2 0.5 copy-start.2
  527.2 0.6 copy-start.4
  535.1 88.0 %collective-permute-start.24 = (bf16[1408,768]{1,0:T(8,128)(2,1)}, bf16[1408,768]{1,0:T(8,128)(2,1)S(1)}, u32[]{:S(2)}, u32[]{:S(2)}) collective-permute-start(bf16[1408,768]{1,0:T(8,128)(2,1)} %mix.30), channel_id=1, source_target_pairs={{0,2},{2,0},{4,6},{6,4},{1,3},{3,1},{5,7},{7,5}} | collective-permute-start | bytes 6488072 | tf_op jit(solution)/shard_map/ppermute | solution.py:375
  542.6 135.6 %collective-permute-start.15 = (bf16[1408,768]{1,0:T(8,128)(2,1)}, bf16[1408,768]{1,0:T(8,128)(2,1)}, u32[]{:S(2)}, u32[]{:S(2)}) collective-permute-start(bf16[1408,768]{1,0:T(8,128)(2,1)} %mix.24), channel_id=1, source_target_pairs={{0,4},{2,6},{4,0},{6,2},{1,5},{3,7},{5,1},{7,3}} | collective-permute-start | bytes 6488072 | tf_op jit(solution)/shard_map/ppermute | solution.py:376
  557.2 112.3 %collective-permute-start.21 = (bf16[1408,768]{1,0:T(8,128)(2,1)}, bf16[1408,768]{1,0:T(8,128)(2,1)}, u32[]{:S(2)}, u32[]{:S(2)}) collective-permute-start(bf16[1408,768]{1,0:T(8,128)(2,1)} %mix.28), channel_id=1, source_target_pairs={{0,2},{2,0},{4,6},{6,4},{1,3},{3,1},{5,7},{7,5}} | collective-permute-start | bytes 6488072 | tf_op jit(solution)/shard_map/ppermute | solution.py:375
  565.1 60.3 %copy-start.3 = (f32[2]{0:T(128)S(1)}, f32[2]{0:T(128)}, u32[]{:S(2)}) copy-start(f32[2]{0:T(128)} %copy-done.2) | copy-start | bytes 28
  565.1 60.3 %copy-start.5 = (f32[2]{0:T(128)S(1)}, f32[2]{0:T(128)}, u32[]{:S(2)}) copy-start(f32[2]{0:T(128)} %copy-done.4) | copy-start | bytes 28
  572.5 143.4 %collective-permute-start = (bf16[352,3072]{1,0:T(8,128)(2,1)}, bf16[352,3072]{1,0:T(8,128)(2,1)}, u32[]{:S(2)}, u32[]{:S(2)}) collective-permute-start(bf16[352,3072]{1,0:T(8,128)(2,1)} %mix.16), channel_id=1, source_target_pairs={{0,2},{2,0},{4,6},{6,4},{1,3},{3,1},{5,7},{7,5}} | collective-permute-start | bytes 6488072 | tf_op jit(solution)/shard_map/ppermute | solution.py:375
  576.8 139.6 %collective-permute-start.9 = (bf16[352,3072]{1,0:T(8,128)(2,1)}, bf16[352,3072]{1,0:T(8,128)(2,1)}, u32[]{:S(2)}, u32[]{:S(2)}) collective-permute-start(bf16[352,3072]{1,0:T(8,128)(2,1)} %mix.22), channel_id=1, source_target_pairs={{0,4},{2,6},{4,0},{6,2},{1,5},{3,7},{5,1},{7,3}} | collective-permute-start | bytes 6488072 | tf_op jit(solution)/shard_map/ppermute | solution.py:376
  623.1 9.0 copy-start
  623.1 94.8 %collective-permute-start.6 = (bf16[352,3072]{1,0:T(8,128)(2,1)}, bf16[352,3072]{1,0:T(8,128)(2,1)}, u32[]{:S(2)}, u32[]{:S(2)}) collective-permute-start(bf16[352,3072]{1,0:T(8,128)(2,1)} %mix.20), channel_id=1, source_target_pairs={{0,4},{2,6},{4,0},{6,2},{1,5},{3,7},{5,1},{7,3}} | collective-permute-start | bytes 6488072 | tf_op jit(solution)/shard_map/ppermute | solution.py:376
  632.1 6.5 copy-start.1
  669.5 92.7 %collective-permute-start.17 = (bf16[1408,768]{1,0:T(8,128)(2,1)}, bf16[1408,768]{1,0:T(8,128)(2,1)}, u32[]{:S(2)}, u32[]{:S(2)}) collective-permute-start(bf16[1408,768]{1,0:T(8,128)(2,1)} %mix.26), channel_id=1, source_target_pairs={{0,2},{2,0},{4,6},{6,4},{1,3},{3,1},{5,7},{7,5}} | collective-permute-start | bytes 6488072 | tf_op jit(solution)/shard_map/ppermute | solution.py:375
  678.1 86.1 %collective-permute-start.2 = (bf16[352,3072]{1,0:T(8,128)(2,1)}, bf16[352,3072]{1,0:T(8,128)(2,1)}, u32[]{:S(2)}, u32[]{:S(2)}) collective-permute-start(bf16[352,3072]{1,0:T(8,128)(2,1)} %mix.18), channel_id=1, source_target_pairs={{0,4},{2,6},{4,0},{6,2},{1,5},{3,7},{5,1},{7,3}} | collective-permute-start | bytes 6488072 | tf_op jit(solution)/shard_map/ppermute | solution.py:376
  715.9 92.7 %collective-permute-start.25 = (bf16[1408,768]{1,0:T(8,128)(2,1)S(1)}, bf16[1408,768]{1,0:T(8,128)(2,1)}, u32[]{:S(2)}, u32[]{:S(2)}) collective-permute-start(bf16[1408,768]{1,0:T(8,128)(2,1)S(1)} %mix.31.piece_ref), channel_id=1, source_target_pairs={{0,2},{2,0},{4,6},{6,4},{1,3},{3,1},{5,7},{7,5}} | collective-permute-start | bytes 6488072 | tf_op jit(solution)/shard_map/ppermute | solution.py:375
  716.5 137.1 %collective-permute-start.22 = (bf16[1408,768]{1,0:T(8,128)(2,1)}, bf16[1408,768]{1,0:T(8,128)(2,1)}, u32[]{:S(2)}, u32[]{:S(2)}) collective-permute-start(bf16[1408,768]{1,0:T(8,128)(2,1)} %mix.29.piece_ref), channel_id=1, source_target_pairs={{0,2},{2,0},{4,6},{6,4},{1,3},{3,1},{5,7},{7,5}} | collective-permute-start | bytes 6488072 | tf_op jit(solution)/shard_map/ppermute | solution.py:375
  717.9 136.2 %collective-permute-start.29 = (bf16[1408,768]{1,0:T(8,128)(2,1)S(1)}, bf16[1408,768]{1,0:T(8,128)(2,1)}, u32[]{:S(2)}, u32[]{:S(2)}) collective-permute-start(bf16[1408,768]{1,0:T(8,128)(2,1)S(1)} %mix.31.piece_ref), channel_id=1, source_target_pairs={{0,4},{2,6},{4,0},{6,2},{1,5},{3,7},{5,1},{7,3}} | collective-permute-start | bytes 6488072 | tf_op jit(solution)/shard_map/ppermute | solution.py:376
  762.2 108.2 %collective-permute-start.28 = (bf16[1408,768]{1,0:T(8,128)(2,1)}, bf16[1408,768]{1,0:T(8,128)(2,1)}, u32[]{:S(2)}, u32[]{:S(2)}) collective-permute-start(bf16[1408,768]{1,0:T(8,128)(2,1)} %mix.29.piece_ref), channel_id=1, source_target_pairs={{0,4},{2,6},{4,0},{6,2},{1,5},{3,7},{5,1},{7,3}} | collective-permute-start | bytes 6488072 | tf_op jit(solution)/shard_map/ppermute | solution.py:376
  764.2 131.6 %collective-permute-start.10 = (bf16[352,3072]{1,0:T(8,128)(2,1)}, bf16[352,3072]{1,0:T(8,128)(2,1)}, u32[]{:S(2)}, u32[]{:S(2)}) collective-permute-start(bf16[352,3072]{1,0:T(8,128)(2,1)} %mix.23.piece_ref), channel_id=1, source_target_pairs={{0,4},{2,6},{4,0},{6,2},{1,5},{3,7},{5,1},{7,3}} | collective-permute-start | bytes 6488072 | tf_op jit(solution)/shard_map/ppermute | solution.py:376
  808.6 133.6 %collective-permute-start.7 = (bf16[352,3072]{1,0:T(8,128)(2,1)}, bf16[352,3072]{1,0:T(8,128)(2,1)}, u32[]{:S(2)}, u32[]{:S(2)}) collective-permute-start(bf16[352,3072]{1,0:T(8,128)(2,1)} %mix.21.piece_ref), channel_id=1, source_target_pairs={{0,4},{2,6},{4,0},{6,2},{1,5},{3,7},{5,1},{7,3}} | collective-permute-start | bytes 6488072 | tf_op jit(solution)/shard_map/ppermute | solution.py:376
  853.6 88.6 %collective-permute-start.14 = (bf16[352,3072]{1,0:T(8,128)(2,1)}, bf16[352,3072]{1,0:T(8,128)(2,1)}, u32[]{:S(2)}, u32[]{:S(2)}) collective-permute-start(bf16[352,3072]{1,0:T(8,128)(2,1)} %mix.23.piece_ref), channel_id=1, source_target_pairs={{0,2},{2,0},{4,6},{6,4},{1,3},{3,1},{5,7},{7,5}} | collective-permute-start | bytes 6488072 | tf_op jit(solution)/shard_map/ppermute | solution.py:375
  854.1 96.0 %collective-permute-start.13 = (bf16[352,3072]{1,0:T(8,128)(2,1)}, bf16[352,3072]{1,0:T(8,128)(2,1)}, u32[]{:S(2)}, u32[]{:S(2)}) collective-permute-start(bf16[352,3072]{1,0:T(8,128)(2,1)} %mix.21.piece_ref), channel_id=1, source_target_pairs={{0,2},{2,0},{4,6},{6,4},{1,3},{3,1},{5,7},{7,5}} | collective-permute-start | bytes 6488072 | tf_op jit(solution)/shard_map/ppermute | solution.py:375
  870.4 126.0 %collective-permute-start.18 = (bf16[1408,768]{1,0:T(8,128)(2,1)}, bf16[1408,768]{1,0:T(8,128)(2,1)}, u32[]{:S(2)}, u32[]{:S(2)}) collective-permute-start(bf16[1408,768]{1,0:T(8,128)(2,1)} %mix.27.piece_ref), channel_id=1, source_target_pairs={{0,2},{2,0},{4,6},{6,4},{1,3},{3,1},{5,7},{7,5}} | collective-permute-start | bytes 6488072 | tf_op jit(solution)/shard_map/ppermute | solution.py:375
  895.8 102.4 %collective-permute-start.27 = (bf16[1408,768]{1,0:T(8,128)(2,1)}, bf16[1408,768]{1,0:T(8,128)(2,1)}, u32[]{:S(2)}, u32[]{:S(2)}) collective-permute-start(bf16[1408,768]{1,0:T(8,128)(2,1)} %mix.27.piece_ref), channel_id=1, source_target_pairs={{0,4},{2,6},{4,0},{6,2},{1,5},{3,7},{5,1},{7,3}} | collective-permute-start | bytes 6488072 | tf_op jit(solution)/shard_map/ppermute | solution.py:376
  942.2 92.7 %collective-permute-start.3 = (bf16[352,3072]{1,0:T(8,128)(2,1)}, bf16[352,3072]{1,0:T(8,128)(2,1)}, u32[]{:S(2)}, u32[]{:S(2)}) collective-permute-start(bf16[352,3072]{1,0:T(8,128)(2,1)} %mix.19.piece_ref), channel_id=1, source_target_pairs={{0,4},{2,6},{4,0},{6,2},{1,5},{3,7},{5,1},{7,3}} | collective-permute-start | bytes 6488072 | tf_op jit(solution)/shard_map/ppermute | solution.py:376
  942.2 100.6 %collective-permute-start.12 = (bf16[352,3072]{1,0:T(8,128)(2,1)}, bf16[352,3072]{1,0:T(8,128)(2,1)}, u32[]{:S(2)}, u32[]{:S(2)}) collective-permute-start(bf16[352,3072]{1,0:T(8,128)(2,1)} %mix.19.piece_ref), channel_id=1, source_target_pairs={{0,2},{2,0},{4,6},{6,4},{1,3},{3,1},{5,7},{7,5}} | collective-permute-start | bytes 6488072 | tf_op jit(solution)/shard_map/ppermute | solution.py:375
  950.1 131.1 %collective-permute-start.26 = (bf16[1408,768]{1,0:T(8,128)(2,1)}, bf16[1408,768]{1,0:T(8,128)(2,1)}, u32[]{:S(2)}, u32[]{:S(2)}) collective-permute-start(bf16[1408,768]{1,0:T(8,128)(2,1)} %collective-permute-done.25.piece_ref), channel_id=1, source_target_pairs={{0,4},{2,6},{4,0},{6,2},{1,5},{3,7},{5,1},{7,3}} | collective-permute-start | bytes 6488072 | tf_op jit(solution)/shard_map/ppermute | solution.py:376
  996.5 199.0 %collective-permute-start.23 = (bf16[1408,768]{1,0:T(8,128)(2,1)}, bf16[1408,768]{1,0:T(8,128)(2,1)}, u32[]{:S(2)}, u32[]{:S(2)}) collective-permute-start(bf16[1408,768]{1,0:T(8,128)(2,1)} %collective-permute-done.22.piece_ref), channel_id=1, source_target_pairs={{0,4},{2,6},{4,0},{6,2},{1,5},{3,7},{5,1},{7,3}} | collective-permute-start | bytes 6488072 | tf_op jit(solution)/shard_map/ppermute | solution.py:376
  998.2 203.8 %collective-permute-start.11 = (bf16[352,3072]{1,0:T(8,128)(2,1)}, bf16[352,3072]{1,0:T(8,128)(2,1)}, u32[]{:S(2)}, u32[]{:S(2)}) collective-permute-start(bf16[352,3072]{1,0:T(8,128)(2,1)} %collective-permute-done.10.piece_ref), channel_id=1, source_target_pairs={{0,2},{2,0},{4,6},{6,4},{1,3},{3,1},{5,7},{7,5}} | collective-permute-start | bytes 6488072 | tf_op jit(solution)/shard_map/ppermute | solution.py:375
  1034.8 172.3 %collective-permute-start.8 = (bf16[352,3072]{1,0:T(8,128)(2,1)}, bf16[352,3072]{1,0:T(8,128)(2,1)}, u32[]{:S(2)}, u32[]{:S(2)}) collective-permute-start(bf16[352,3072]{1,0:T(8,128)(2,1)} %collective-permute-done.7.piece_ref), channel_id=1, source_target_pairs={{0,2},{2,0},{4,6},{6,4},{1,3},{3,1},{5,7},{7,5}} | collective-permute-start | bytes 6488072 | tf_op jit(solution)/shard_map/ppermute | solution.py:375
  1042.8 169.5 %collective-permute-start.19 = (bf16[1408,768]{1,0:T(8,128)(2,1)}, bf16[1408,768]{1,0:T(8,128)(2,1)}, u32[]{:S(2)}, u32[]{:S(2)}) collective-permute-start(bf16[1408,768]{1,0:T(8,128)(2,1)} %collective-permute-done.18.piece_ref), channel_id=1, source_target_pairs={{0,4},{2,6},{4,0},{6,2},{1,5},{3,7},{5,1},{7,3}} | collective-permute-start | bytes 6488072 | tf_op jit(solution)/shard_map/ppermute | solution.py:376
  1081.2 137.7 %collective-permute-start.4 = (bf16[352,3072]{1,0:T(8,128)(2,1)}, bf16[352,3072]{1,0:T(8,128)(2,1)}, u32[]{:S(2)}, u32[]{:S(2)}) collective-permute-start(bf16[352,3072]{1,0:T(8,128)(2,1)} %collective-permute-done.3.piece_ref), channel_id=1, source_target_pairs={{0,2},{2,0},{4,6},{6,4},{1,3},{3,1},{5,7},{7,5}} | collective-permute-start | bytes 6488072 | tf_op jit(solution)/shard_map/ppermute | solution.py:375

commit v5 on v4

v5 whole, which is shorter than its diff:
```python
import functools

import jax
import jax.numpy as jnp
from jax import lax
from jax.experimental import pallas as pl
from jax.experimental.pallas import tpu as pltpu
from jax.sharding import PartitionSpec as P


INV_SQRT2 = 0.7071067811865476
INV_SQRT_2PI = 0.3989422804014327
LOG2_E = 1.4426950408889634
F_BLOCK = 512
T_CHUNK = 256
IN_SLOTS = 4
LOAD_CHUNKS = 2
VMEM_LIMIT = 66_500_000

F32 = jnp.float32
BF16 = jnp.bfloat16
ANY = pl.ANY
MESH = pl.DeviceIdType.MESH


def dot_nn(a, b):
    return lax.dot_general(a, b, (((1,), (0,)), ((), ())), preferred_element_type=F32)


def dot_nt(a, b):
    return lax.dot_general(a, b, (((1,), (1,)), ((), ())), preferred_element_type=F32)


def block_at(j, n_half, x_pos, y_pos):
    far = n_half * (1 - y_pos) + x_pos * j + (1 - x_pos) * (n_half - 1 - j)
    own = n_half * y_pos + j - n_half
    is_far = 1 - j // n_half
    return is_far * far + (1 - is_far) * own


def stack_kernel(n_layers, n_ex, n_steps, u_ref, w1_ref, w2_ref, x_hbm, dout_hbm,
                 p_hbm, q_hbm, dzo_hbm, g1k_hbm, g1s_hbm, g1r_hbm, g2k_hbm, g2s_hbm, g2r_hbm,
                 g1l_hbm, g2l_hbm, g1e_hbm, g1er_hbm, g2e_hbm, g2er_hbm, ss_ref,
                 x_t, dz, dz_t, dh, h, acc, x_st, z_st, p_st, q_st, g1_st, g1s_st, g2_st, g2s_st,
                 in_sem, out_sem, io_sem, tp_send, tp_recv, far_send, far_recv):
    task, step = pl.program_id(0), pl.program_id(1)
    n_early = (n_layers - 1) * n_ex
    n_task = n_early + n_ex
    dp = lax.axis_index('dp')
    x_pos, y_pos = lax.rem(dp, 2), dp // 2
    x_far = {'dp': dp + 1 - 2 * x_pos}
    y_far = {'dp': dp + 2 - 4 * y_pos}
    tp_far = {'tp': 1 - lax.axis_index('tp')}
    n_tok, d_model = dz.shape
    half_d, quarter_d = d_model // 2, d_model // 4
    n_half = n_steps // 2
    half_b = F_BLOCK // 2
    n_t = n_tok // T_CHUNK
    example = lax.rem(task, n_ex)
    cols = lambda k: pl.ds(pl.multiple_of(k * F_BLOCK, F_BLOCK), F_BLOCK)
    chunk = lambda c: pl.ds(c * T_CHUNK if isinstance(c, int) else pl.multiple_of(c * T_CHUNK, T_CHUNK), T_CHUNK)

    def in_start(t, c):
        slot, rows, ex = lax.rem(c, IN_SLOTS), chunk(c), lax.rem(t, n_ex)
        copy = lambda k, src, dst: pltpu.make_async_copy(src, dst.at[slot], in_sem.at[k, slot]).start()
        copy(0, x_hbm.at[n_layers - 1 - t // n_ex, ex, rows, :], x_st)

        @pl.when(t < n_early)
        def _():
            copy(1, dout_hbm.at[ex, rows, :], z_st)

        @pl.when(t >= n_early)
        def _():
            copy(1, dzo_hbm.at[ex, rows, :], z_st)

        @pl.when(t >= n_ex)
        def _():
            copy(2, p_hbm.at[t - n_ex, rows, :], p_st)
            copy(3, q_hbm.at[t - n_ex, rows, :], q_st)

    def in_wait(c):
        slot, rows = lax.rem(c, IN_SLOTS), chunk(c)
        wait = lambda k, dst: pltpu.make_async_copy(dout_hbm.at[0, rows, :], dst.at[slot], in_sem.at[k, slot]).wait()
        wait(0, x_st)
        wait(1, z_st)

        @pl.when(task >= n_ex)
        def _():
            wait(2, p_st)
            wait(3, q_st)

    def tp_copy(t):
        return pltpu.make_async_remote_copy(
            src_ref=p_hbm.at[t], dst_ref=q_hbm.at[t], send_sem=tp_send.at[t], recv_sem=tp_recv.at[t],
            device_id=tp_far, device_id_type=MESH)

    def front(load, to_dx):
        n_in = LOAD_CHUNKS if load else (n_t if to_dx else n_t // 2)

        def trip(i, carry):
            def dx_part(rows):
                part = dot_nt(dh[rows, :], w1_ref[0])
                acc[rows, :] = part if load else acc[rows, :] + part

            for s in range(n_in):
                c = i * n_in + s
                rows = chunk(c)
                if load:
                    @pl.when(c + IN_SLOTS - 1 < n_t)
                    def _():
                        in_start(task, c + IN_SLOTS - 1)

                    in_wait(c)
                    slot = lax.rem(c, IN_SLOTS)
                    z = z_st[slot]
                    moved = (z.astype(F32) + (p_st[slot].astype(F32) + q_st[slot].astype(F32))).astype(BF16)
                    z = jnp.where(task >= n_ex, moved, z) if to_dx else moved
                    dz[rows, :] = z
                    dz_t[:, rows] = z.T
                    x_t[:, rows] = x_st[slot].T
                u = u_ref[0, 0, rows, :].astype(F32)
                t = u * INV_SQRT2
                cdf = 0.5 * lax.erf(t) + 0.5
                h[rows, :] = (u * cdf).astype(BF16)
                slope = cdf + (t * (INV_SQRT_2PI / INV_SQRT2)) * jnp.exp2((t * t) * -LOG2_E)
                dh[rows, :] = (slope * dot_nt(dz[rows, :], w2_ref[0])).astype(BF16)
                if to_dx and s:
                    dx_part(chunk(c - 1))
            if to_dx:
                dx_part(chunk(i * n_in + n_in - 1))
            return carry

        if n_in == n_t:
            trip(0, 0)
        else:
            lax.fori_loop(0, n_t // n_in, trip, 0)

    @pl.when((task == 0) & (step == 0))
    def _():
        ss_ref[...] = jnp.zeros_like(ss_ref)
        for c in range(IN_SLOTS - 1):
            in_start(task, c)

    for load in (True, False):
        for to_dx in (True, False):
            @pl.when(((step == 0) if load else (step > 0)) & ((task < n_early) if to_dx else (task >= n_early)))
            def _():
                front(load, to_dx)

    dz_keep = pltpu.make_async_copy(dz, dzo_hbm.at[example], io_sem.at[0])
    is_mid = (task >= n_ex) & (task < n_early)
    pl.when(is_mid & (step == 0))(dz_keep.start)
    ends_early = (step == n_steps - 1) & (task < n_early)
    dx_out = pltpu.make_async_copy(dz, p_hbm.at[task], io_sem.at[1])

    @pl.when(ends_early)
    def _():
        pl.when(is_mid)(dz_keep.wait)

        def put(c, carry):
            dz[chunk(c), :] = acc[chunk(c), :].astype(BF16)
            return carry

        lax.fori_loop(0, n_t, put, 0)
        dx_out.start()

    def out_copies(t, j):
        early, is_far, fb = t < n_early, j < n_half, block_at(j, n_half, x_pos, y_pos)
        copy = lambda n, src, dst: pltpu.make_async_copy(src, dst, out_sem.at[n])
        t_e, t_l = jnp.minimum(t, n_early - 1), jnp.maximum(t - n_early, 0)
        own_rows = pl.ds(pl.multiple_of(x_pos * half_d, 16), half_d)
        pass_rows = pl.ds(pl.multiple_of((1 - y_pos) * quarter_d, 16), quarter_d)
        in_half = cols(lax.rem(fb, n_half))
        src_half = pl.ds(pl.multiple_of((1 - x_pos) * half_b, half_b), half_b)
        dst_half = pl.ds(pl.multiple_of(x_pos * F_BLOCK, half_b), half_b)
        dst_full = pl.ds(pl.multiple_of((1 - x_pos) * half_b, half_b), F_BLOCK)
        return [
            (early, copy(0, g1_st.at[own_rows, :], g1k_hbm.at[t_e, :, cols(fb)])),
            (early, copy(1, g1s_st, g1s_hbm.at[t_e, :, cols(fb)])),
            (early & is_far, copy(2, g2s_st, g2s_hbm.at[t_e, :, in_half])),
            (early & ~is_far, copy(3, g2_st, g2k_hbm.at[t_e, :, in_half])),
            (~early, copy(0, g1_st, g1l_hbm.at[t_l, :, cols(fb)])),
            (~early, copy(1, g1s_st.at[pass_rows, :], g1e_hbm.at[t_l, :, cols(fb)])),
            (~early & (j == 0), copy(2, g2s_st, g2e_hbm.at[t_l, :, dst_full])),
            (~early & (j == 1), copy(2, g2s_st.at[:, src_half], g2e_hbm.at[t_l, :, dst_half])),
            (~early, copy(3, g2_st, g2l_hbm.at[t_l, :, cols(fb)])),
        ]

    def far_copy(axis, src, dst):
        return pltpu.make_async_remote_copy(
            src_ref=src, dst_ref=dst, send_sem=far_send.at[axis], recv_sem=far_recv.at[axis],
            device_id=y_far if axis % 2 else x_far, device_id_type=MESH)

    def send_far(t, j):
        early, is_far, fb = t < n_early, j < n_half, block_at(j, n_half, x_pos, y_pos)
        t_l = jnp.maximum(t - n_early, 0)
        in_half = cols(lax.rem(fb, n_half))
        half = pl.ds(pl.multiple_of(x_pos * F_BLOCK, half_b), half_b)
        full = pl.ds(pl.multiple_of((1 - x_pos) * half_b, half_b), F_BLOCK)

        @pl.when(early)
        def _():
            far_copy(0, g1s_hbm.at[t, :, cols(fb)], g1r_hbm.at[t, :, cols(fb)]).start()

        @pl.when(early & is_far)
        def _():
            far_copy(1, g2s_hbm.at[t, :, in_half], g2r_hbm.at[t, :, in_half]).start()

        @pl.when(~early)
        def _():
            far_copy(2, g1e_hbm.at[t_l, :, cols(fb)], g1er_hbm.at[t_l, :, cols(fb)]).start()

        @pl.when(~early & (j == 0))
        def _():
            far_copy(3, g2e_hbm.at[t_l, :, full], g2er_hbm.at[t_l, :, full]).start()

        @pl.when(~early & (j == 1))
        def _():
            far_copy(3, g2e_hbm.at[t_l, :, half], g2er_hbm.at[t_l, :, half]).start()

    def finish_block(t, j):
        for cond, cp in out_copies(t, j):
            pl.when(cond)(cp.wait)
        send_far(t, j)

    @pl.when((task > 0) | (step > 0))
    def _():
        finish_block(jnp.where(step > 0, task, task - 1), jnp.where(step > 0, step - 1, n_steps - 1))

    def square(g):
        return jnp.sum((g * g).reshape(g.shape[0] // 8, 8, g.shape[1]), axis=0)

    total = ss_ref[example]
    for r in range(2):
        part = pl.ds(r * quarter_d, quarter_d)
        own = pl.ds(pl.multiple_of(r * quarter_d + x_pos * half_d, 16), quarter_d)
        far = pl.ds(pl.multiple_of(r * quarter_d + (1 - x_pos) * half_d, 16), quarter_d)
        g = dot_nn(x_t[own, :], dh[...])
        g1_st[own, :] = g
        total = total + square(g)
        g = dot_nn(x_t[far, :], dh[...])
        g1_st[far, :] = g
        g1s_st[part, :] = g.astype(BF16)
        total = total + square(g)
        for at in (part, pl.ds(r * quarter_d + half_d, quarter_d)):
            g = dot_nn(dz_t[at, :], h[...])
            g2_st[at, :] = g
            g2s_st[at, :] = g.astype(BF16)
            total = total + square(g)
    ss_ref[example] = total
    for cond, cp in out_copies(task, step):
        pl.when(cond)(cp.start)

    @pl.when(ends_early)
    def _():
        dx_out.wait()
        tp_copy(task).start()

    @pl.when((step == n_steps - 1) & (task < n_task - 1))
    def _():
        nxt = task + 1

        @pl.when(nxt >= n_ex)
        def _():
            tp_copy(nxt - n_ex).wait()

        for c in range(IN_SLOTS - 1):
            in_start(nxt, c)

    @pl.when((step == n_steps - 1) & (task == n_task - 1))
    def _():
        finish_block(task, step)
        far_copy(0, g1s_hbm, g1r_hbm).wait()
        far_copy(1, g2s_hbm, g2r_hbm).wait()
        far_copy(2, g1e_hbm, g1er_hbm).wait()
        far_copy(3, g2e_hbm, g2er_hbm).wait()


def run_stack(pre_act, w_in, w_out, block_in, d_out):
    n_layers, n_ex, n_tok, d_model = block_in.shape
    d_ff = pre_act.shape[3]
    n_steps = d_ff // F_BLOCK
    half_d, half_f = d_model // 2, d_ff // 2
    n_early = (n_layers - 1) * n_ex
    top = n_layers - 1

    def fb(j):
        dp = lax.axis_index('dp')
        return block_at(j, n_steps // 2, lax.rem(dp, 2), dp // 2)

    def w1_at(t, j):
        is_last = t // n_early
        return jnp.maximum(top - t // n_ex, 1), 0, fb((1 - is_last) * j + is_last * (n_steps - 1))

    in_specs = [
        pl.BlockSpec((1, 1, n_tok, F_BLOCK), lambda t, j: (top - t // n_ex, lax.rem(t, n_ex), 0, fb(j))),
        pl.BlockSpec((1, d_model, F_BLOCK), w1_at),
        pl.BlockSpec((1, F_BLOCK, d_model), lambda t, j: (top - t // n_ex, fb(j), 0)),
        pl.BlockSpec(memory_space=ANY),
        pl.BlockSpec(memory_space=ANY),
    ]
    sds = jax.ShapeDtypeStruct
    outs = [
        sds((n_early, n_tok, d_model), BF16), sds((n_early, n_tok, d_model), BF16), sds((n_ex, n_tok, d_model), BF16),
        sds((n_early, half_d, d_ff), F32), sds((n_early, half_d, d_ff), BF16), sds((n_early, half_d, d_ff), BF16),
        sds((n_early, d_model, half_f), F32), sds((n_early, d_model, half_f), BF16), sds((n_early, d_model, half_f), BF16),
        sds((n_ex, d_model, d_ff), F32), sds((n_ex, d_model, d_ff), F32),
        sds((n_ex, d_model // 4, d_ff), BF16), sds((n_ex, d_model // 4, d_ff), BF16),
        sds((n_ex, d_model, d_ff // 4), BF16), sds((n_ex, d_model, d_ff // 4), BF16),
        sds((n_ex, 8, F_BLOCK), F32),
    ]
    out_specs = [pl.BlockSpec(memory_space=ANY)] * (len(outs) - 1) + [pl.BlockSpec((n_ex, 8, F_BLOCK), lambda t, j: (0, 0, 0))]
    vm = pltpu.VMEM
    scratch = [
        vm((d_model, n_tok), BF16), vm((n_tok, d_model), BF16), vm((d_model, n_tok), BF16),
        vm((n_tok, F_BLOCK), BF16), vm((n_tok, F_BLOCK), BF16), vm((n_tok, d_model), F32),
        *[vm((IN_SLOTS, T_CHUNK, d_model), BF16)] * 4,
        vm((d_model, F_BLOCK), F32), vm((half_d, F_BLOCK), BF16), vm((d_model, F_BLOCK), F32), vm((d_model, F_BLOCK), BF16),
        pltpu.SemaphoreType.DMA((4, IN_SLOTS)), pltpu.SemaphoreType.DMA((4,)), pltpu.SemaphoreType.DMA((2,)),
        pltpu.SemaphoreType.DMA((n_early,)), pltpu.SemaphoreType.DMA((n_early,)),
        pltpu.SemaphoreType.DMA((4,)), pltpu.SemaphoreType.DMA((4,)),
    ]
    n_dots = 4 * n_early + 3 * n_ex
    return pl.pallas_call(
        functools.partial(stack_kernel, n_layers, n_ex, n_steps),
        out_shape=outs,
        grid_spec=pltpu.PrefetchScalarGridSpec(
            num_scalar_prefetch=0, grid=(n_early + n_ex, n_steps), in_specs=in_specs, out_specs=out_specs, scratch_shapes=scratch),
        compiler_params=pltpu.CompilerParams(
            dimension_semantics=('arbitrary', 'arbitrary'), vmem_limit_bytes=VMEM_LIMIT, has_side_effects=True),
        cost_estimate=pl.CostEstimate(
            flops=2 * n_dots * n_tok * d_model * d_ff, bytes_accessed=500_000_000, transcendentals=2 * n_tok * d_ff),
        name='stack',
    )(pre_act, w_in, w_out, block_in, d_out)


def mix_kernel(sc_ref, coef_ref, *refs):
    total = refs[0][0].astype(F32) * coef_ref[0]
    for k, ref in enumerate(refs[1:-1]):
        total = total + ref[0].astype(F32) * coef_ref[k + 1]
    refs[-1][...] = total.astype(BF16)


def mix(which, shape, terms, coefs):
    rows, width = shape
    block = (32, width) if which == 0 else (rows // 8, width)

    def spec(k, lead):
        if which == 0:
            return pl.BlockSpec((1, *block), lambda i, sc: (lead, (rows // block[0]) * sc[k] + i, 0))
        return pl.BlockSpec((1, *block), lambda i, sc: (lead, i, sc[k]))

    out_map = lambda i, sc: (i, 0)
    places = jnp.stack([jnp.asarray(p, jnp.int32) for _, _, p in terms])
    return pl.pallas_call(
        mix_kernel,
        out_shape=jax.ShapeDtypeStruct((rows, width), BF16),
        grid_spec=pltpu.PrefetchScalarGridSpec(
            num_scalar_prefetch=1, grid=(rows // block[0],),
            in_specs=[pl.BlockSpec(memory_space=pltpu.SMEM)] + [spec(k, lead) for k, (_, lead, _) in enumerate(terms)],
            out_specs=pl.BlockSpec(block, out_map)),
        compiler_params=pltpu.CompilerParams(dimension_semantics=('arbitrary',), vmem_limit_bytes=40_000_000),
        cost_estimate=pl.CostEstimate(flops=2 * len(terms) * rows * width, bytes_accessed=14 * rows * width, transcendentals=0),
        name='mix',
    )(places, coefs, *[v for v, _, _ in terms])


def put_in_kernel(sc_ref, coef_ref, piece_ref, noise_ref, *rest):
    out_ref = rest[-1]
    out_ref[0, 0] = (piece_ref[...].astype(F32) + coef_ref[0] * noise_ref[0, 0]) * coef_ref[1]


def put_out_kernel(sc_ref, coef_ref, piece_ref, noise_ref, *rest):
    out_ref = rest[-1]
    out_ref[0, 0] = (piece_ref[...].astype(F32).T + coef_ref[0] * noise_ref[0, 0]) * coef_ref[1]


def put_piece(transposed, total, layer, quarter, coef, piece, noise):
    if transposed:
        rows, width = piece.shape[1], piece.shape[0]
        block = 256
        piece_spec = pl.BlockSpec((width, block), lambda i, sc: (0, i))
    else:
        rows, width = piece.shape
        block = rows // 2
        piece_spec = pl.BlockSpec((block, width), lambda i, sc: (i, 0))
    big_spec = pl.BlockSpec((1, 1, block, width), lambda i, sc: (sc[0], sc[1], i, 0))
    args = [jnp.stack([jnp.int32(layer), quarter]), coef, piece, noise]
    in_specs = [pl.BlockSpec(memory_space=pltpu.SMEM), piece_spec, big_spec]
    aliases = {}
    if total is not None:
        args.append(total)
        in_specs.append(pl.BlockSpec(memory_space=ANY))
        aliases = {4: 0}
    return pl.pallas_call(
        put_out_kernel if transposed else put_in_kernel,
        out_shape=jax.ShapeDtypeStruct(noise.shape, F32),
        grid_spec=pltpu.PrefetchScalarGridSpec(
            num_scalar_prefetch=1, grid=(rows // block,), in_specs=in_specs, out_specs=big_spec),
        input_output_aliases=aliases,
        compiler_params=pltpu.CompilerParams(dimension_semantics=('arbitrary',), vmem_limit_bytes=40_000_000),
        cost_estimate=pl.CostEstimate(flops=4 * rows * width, bytes_accessed=10 * rows * width, transcendentals=0),
        name='put_out' if transposed else 'put_in',
    )(*args)


def solution(mesh):
    data_size = mesh.shape['dp']
    swap_x = [(i, i ^ 1) for i in range(data_size)]
    swap_y = [(i, i ^ 2) for i in range(data_size)]

    def local_step(block_in, pre_act, w_in, w_out, d_out, noise_in, noise_out, clip_norm, noise_mult):
        n_layers, local_batch, _, d_model = block_in.shape
        d_ff = pre_act.shape[3]
        batch_total = local_batch * data_size
        dp = lax.axis_index('dp')
        x_pos, y_pos = lax.rem(dp, 2), dp // 2
        over_x = lambda v: lax.ppermute(v, 'dp', swap_x)
        over_y = lambda v: lax.ppermute(v, 'dp', swap_y)
        res = run_stack(pre_act, w_in, w_out, block_in, d_out)
        g1k, _, g1r, g2k, _, g2r, g1l, g2l, _, g1er, _, g2er, squares = res[3:]
        part_sq = jnp.sum(squares, axis=(1, 2))
        clip = jnp.minimum(1.0, clip_norm / jnp.sqrt(lax.psum(part_sq, 'tp')))
        clip, clip_x, clip_y = lax.optimization_barrier((clip, over_x(clip), over_y(clip)))
        c_own, c_x, c_y = [[v[k] for k in range(local_batch)] for v in (clip, clip_x, clip_y)]
        coef = jnp.stack([noise_mult * clip_norm, jnp.float32(1.0 / batch_total)])

        noise_in4 = noise_in.reshape(n_layers, 4, d_model // 4, d_ff)
        noise_out4 = noise_out.reshape(n_layers, 4, d_ff // 4, d_model)

        shapes = ((d_model // 4, d_ff), (d_model, d_ff // 4))
        at_half, at_side = (x_pos, y_pos), (y_pos, x_pos)
        over_half, over_side = (over_x, over_y), (over_y, over_x)
        early, early_far, late = (g1k, g2k), (g1r, g2r), (g1l, g2l)

        def own_terms(layer, which, half_pos, pos):
            if layer == 0:
                return [(late[which], k, 2 * half_pos + pos) for k in range(local_batch)]
            first = (n_layers - 1 - layer) * local_batch
            return [(early[which], first + k, pos) for k in range(local_batch)]

        def mixed(which, terms, coefs):
            return mix(which, shapes[which], terms, jnp.stack([jnp.asarray(c, F32) for c in coefs]))

        made = []

        def send(which, terms, coefs, over):
            coefs = jnp.stack([jnp.asarray(c, F32) for c in coefs])
            if made:
                coefs, _ = lax.optimization_barrier((coefs, made[-1]))
            made.append(mix(which, shapes[which], terms, coefs))
            return over(made[-1])

        def pair_terms(layer, which, to_send, *more):
            pos = 1 - at_side[which] if to_send else at_side[which]
            terms, coefs = own_terms(layer, which, at_half[which], pos), list(c_own)
            if layer == 0 and not to_send:
                more = (far_last[which], *more)
            else:
                if layer == 0:
                    terms += [((g1er, g2er)[which], k, 0) for k in range(local_batch)]
                else:
                    first = (n_layers - 1 - layer) * local_batch
                    terms += [(early_far[which], first + k, pos) for k in range(local_batch)]
                coefs += c_y if which else c_x
            terms += [(v[None], 0, 0) for v in more]
            return terms, coefs + [1.0] * len(more)

        got = {}
        for layer in range(n_layers - 1, 0, -1):
            for which in (0, 1):
                got[layer, which] = send(which, *pair_terms(layer, which, True), over_side[which])
        far_last = [
            send(which, own_terms(0, which, 1 - at_half[which], at_side[which]), c_own, over_half[which]) for which in (0, 1)]
        for which in (0, 1):
            got[0, which] = send(which, *pair_terms(0, which, True), over_side[which])

        places = {}
        for layer in range(n_layers - 1, -1, -1):
            for which in (0, 1):
                half_pos, pos = at_half[which], at_side[which]
                own = mixed(which, *pair_terms(layer, which, False, got[layer, which]))
                near, side = over_side[which](own), over_half[which](own)
                diag = over_half[which](near)
                places[layer, which] = (
                    (2 * half_pos + pos, own), (2 * half_pos + 1 - pos, near),
                    (2 * (1 - half_pos) + pos, side), (2 * (1 - half_pos) + 1 - pos, diag))
        grads, noises = [None, None], (noise_in4, noise_out4)
        for kind in range(4):
            for layer in range(n_layers - 1, -1, -1):
                for which in (0, 1):
                    at, piece = places[layer, which][kind]
                    grads[which] = put_piece(which == 1, grads[which], layer, at, coef, piece, noises[which])
        grad_in, grad_out = grads
        return grad_in.reshape(n_layers, d_model, d_ff), grad_out.reshape(n_layers, d_ff, d_model)

    return jax.shard_map(
        local_step,
        mesh=mesh,
        in_specs=(P(None, 'dp', None, None), P(None, 'dp', None, 'tp'), P(None, None, 'tp'), P(None, 'tp', None),
                  P('dp', None, None), P(None, None, 'tp'), P(None, 'tp', None), P(), P()),
        out_specs=(P(None, None, 'tp'), P(None, 'tp', None)),
        check_vma=False,
    )
```

time: 1250 us -> 1270 us (1.016); the launches traced: 1220 us -> 1260 us
  Pallas kernels: 756 us -> 793 us
    ppermute x15 -> x14, waiting for transfers between devices: 144 us -> 291 us  [local_step(): over_y = lambda v: lax.ppermute(v, 'dp', swap_y)]
    ppermute x15 -> x14, waiting for transfers between devices: 280 us -> 136 us  [local_step(): over_x = lambda v: lax.ppermute(v, 'dp', swap_x)]
    pallas_call x16 -> x14, Pallas kernels: 111 us -> 131 us  [mix(): pl.pallas_call(mix_kernel, out_shape=jax.ShapeDtypeStruct((rows, width),...]
    pallas_call x1, Pallas kernels: 506 us -> 523 us  [run_stack(): pl.pallas_call(functools.partial(stack_kernel, n_layers, n_ex, n_steps),...]
  transfers between devices with their start and end apart: 30 -> 28, of which waited for: 14 -> 14; matrix products, arithmetic and copies ran while one was open for 0% -> 0% of each run, Pallas kernels for 20% -> 19%
where the time goes in v5:
time: 1270 us; the launch traced here: 1260 us
  Pallas kernels  793 us (62%)
  waiting for transfers between devices  428 us (34%)
  starting transfers between devices  28.8 us (2%)
    pallas_call x1, Pallas kernels, run_stack(): pl.pallas_call(functools.partial(stack_kernel, n_layers, n_ex, n_steps),...  523 us
    ppermute x14, waiting for transfers between devices, local_step(): over_y = lambda v: lax.ppermute(v, 'dp', swap_y)  291 us
    pallas_call x24, Pallas kernels, put_piece(): pl.pallas_call(put_out_kernel if transposed else put_in_kernel, out_shape...  139 us
    ppermute x14, waiting for transfers between devices, local_step(): over_x = lambda v: lax.ppermute(v, 'dp', swap_x)  136 us
    pallas_call x14, Pallas kernels, mix(): pl.pallas_call(mix_kernel, out_shape=jax.ShapeDtypeStruct((rows, width),...  131 us
  transfers between devices with their start and end apart: 28, of which 14 were waited for; matrix products, arithmetic and copies ran while one was open for 0% of the time, Pallas kernels for 19%

profile of v5, /device:TPU:0, one launch (start us, length us, event | category | flops | bytes accessed | tf_op | source)
XLA Modules:
  0.0 1264.6 jit_solution(18004846607291260711)
XLA Ops:
  0.6 523.2 %stack.284 = (bf16[4,2048,1408]{2,1,0:T(8,128)(2,1)}, bf16[4,2048,1408]{2,1,0:T(8,128)(2,1)}, bf16[2,2048,1408]{2,1,0:T(8,128)(2,1)}, f32[4,704,3072]{2,1,0:T(8,...) custom-call(bf16[3,2,2048,3072]{3,2,1,0:T(8,128)(2,1)} %u_ref.1, ...), custom_call_target="tpu_custom_call" | custom-call | flops 389768282112 | bytes 500000000 | tf_op jit(solution)/shard_map/stack/pallas_call | solution.py:324
  531.9 10.3 mix.14
  542.2 8.8 mix.15
  552.9 10.3 mix.16
  563.2 8.8 mix.17
  572.4 9.3 mix.18
  581.7 8.0 mix.19
  589.7 9.5 mix.20
  599.2 8.1 mix.24
  615.6 7.9 mix.27.piece_ref
  623.5 24.0 %collective-permute-done.19 = bf16[1408,768]{1,0:T(8,128)(2,1)} collective-permute-done((bf16[1408,768]{1,0:T(8,128)(2,1)}, bf16[1408,768]{1,0:T(8,128)(2,1)}, u32[]{:S(2)}, u32[]{:S(2)}) %collective-permute-start.19) | collective-permute-done | bytes 2162720 | tf_op jit(solution)/shard_map/ppermute | solution.py:418
  649.2 9.5 mix.26.piece_ref
  658.6 33.1 %collective-permute-done.16 = bf16[1408,768]{1,0:T(8,128)(2,1)} collective-permute-done((bf16[1408,768]{1,0:T(8,128)(2,1)}, bf16[1408,768]{1,0:T(8,128)(2,1)}, u32[]{:S(2)}, u32[]{:S(2)}) %collective-permute-start.16) | collective-permute-done | bytes 2162720 | tf_op jit(solution)/shard_map/ppermute | solution.py:418
  693.7 8.8 mix.25.piece_ref
  705.9 46.0 %collective-permute-done.6 = bf16[352,3072]{1,0:T(8,128)(2,1)} collective-permute-done((bf16[352,3072]{1,0:T(8,128)(2,1)}, bf16[352,3072]{1,0:T(8,128)(2,1)}, u32[]{:S(2)}, u32[]{:S(2)}) %collective-permute-start.6) | collective-permute-done | bytes 2162720 | tf_op jit(solution)/shard_map/ppermute | solution.py:419
  752.3 10.9 mix.23.piece_ref
  763.3 10.9 mix.22.piece_ref
  774.2 21.2 %collective-permute-done.3 = bf16[352,3072]{1,0:T(8,128)(2,1)} collective-permute-done((bf16[352,3072]{1,0:T(8,128)(2,1)}, bf16[352,3072]{1,0:T(8,128)(2,1)}, u32[]{:S(2)}, u32[]{:S(2)}) %collective-permute-start.3) | collective-permute-done | bytes 2162720 | tf_op jit(solution)/shard_map/ppermute | solution.py:419
  798.9 35.7 %collective-permute-done.20.piece_ref = bf16[1408,768]{1,0:T(8,128)(2,1)} collective-permute-done((bf16[1408,768]{1,0:T(8,128)(2,1)}, bf16[1408,768]{1,0:T(8,128)(2,1)}, u32[]{:S(2)}, u32[]{:S(2)}) %collective-permute-start.20) | collective-permute-done | bytes 2162720 | tf_op jit(solution)/shard_map/ppermute | solution.py:418
  836.2 41.7 %collective-permute-done.17.piece_ref = bf16[1408,768]{1,0:T(8,128)(2,1)} collective-permute-done((bf16[1408,768]{1,0:T(8,128)(2,1)}, bf16[1408,768]{1,0:T(8,128)(2,1)}, u32[]{:S(2)}, u32[]{:S(2)}) %collective-permute-start.17) | collective-permute-done | bytes 2162720 | tf_op jit(solution)/shard_map/ppermute | solution.py:418
  879.4 10.3 mix.21.piece_ref
  894.6 43.4 %collective-permute-done.25.piece_ref = bf16[1408,768]{1,0:T(8,128)(2,1)S(1)} collective-permute-done((bf16[1408,768]{1,0:T(8,128)(2,1)}, bf16[1408,768]{1,0:T(8,128)(2,1)S(1)}, u32[]{:S(2)}, u32[]{:S(2)}) %collective-permute-start.25) | collective-permute-done | bytes 2162720 | tf_op jit(solution)/shard_map/ppermute | solution.py:419
  939.8 44.7 %collective-permute-done.10.piece_ref = bf16[352,3072]{1,0:T(8,128)(2,1)} collective-permute-done((bf16[352,3072]{1,0:T(8,128)(2,1)}, bf16[352,3072]{1,0:T(8,128)(2,1)}, u32[]{:S(2)}, u32[]{:S(2)}) %collective-permute-start.10) | collective-permute-done | bytes 2162720 | tf_op jit(solution)/shard_map/ppermute | solution.py:419
  984.8 46.0 %collective-permute-done.7.piece_ref = bf16[352,3072]{1,0:T(8,128)(2,1)} collective-permute-done((bf16[352,3072]{1,0:T(8,128)(2,1)}, bf16[352,3072]{1,0:T(8,128)(2,1)}, u32[]{:S(2)}, u32[]{:S(2)}) %collective-permute-start.7) | collective-permute-done | bytes 2162720 | tf_op jit(solution)/shard_map/ppermute | solution.py:419
  1032.6 44.6 %collective-permute-done.4.piece_ref = bf16[352,3072]{1,0:T(8,128)(2,1)} collective-permute-done((bf16[352,3072]{1,0:T(8,128)(2,1)}, bf16[352,3072]{1,0:T(8,128)(2,1)}, u32[]{:S(2)}, u32[]{:S(2)}) %collective-permute-start.4) | collective-permute-done | bytes 2162720 | tf_op jit(solution)/shard_map/ppermute | solution.py:419
  1081.2 42.3 %collective-permute-done.24.piece_ref = bf16[1408,768]{1,0:T(8,128)(2,1)} collective-permute-done((bf16[1408,768]{1,0:T(8,128)(2,1)}, bf16[1408,768]{1,0:T(8,128)(2,1)}, u32[]{:S(2)}, u32[]{:S(2)}) %collective-permute-start.24) | collective-permute-done | bytes 2162720 | tf_op jit(solution)/shard_map/ppermute | solution.py:419
  1126.1 6.1 put_out.12.rest_0_
  1132.1 6.6 put_out.13.rest_0_
  1138.7 6.6 put_out.14.rest_0_
  1145.3 5.1 put_in.12.rest_0_
  1150.4 5.1 put_in.13.rest_0_
  1155.5 5.1 put_in.14.rest_0_
  1160.7 6.6 put_out.15.rest_0_
  1167.2 6.6 put_out.16.rest_0_
  1173.8 6.6 put_out.17.rest_0_
  1180.3 5.1 put_in.15.rest_0_
  1185.5 5.1 put_in.16.rest_0_
  1190.6 5.2 put_in.17.rest_0_
  1195.8 6.1 put_out.18.rest_0_
  1201.9 6.1 put_out.19.rest_0_
  1208.0 6.1 put_out.20.rest_0_
  1219.3 5.1 put_in.19.rest_0_
  1229.5 6.6 put_out.21.rest_0_
  1236.1 6.6 put_out.22.rest_0_
  1242.7 6.6 put_out.23
  1249.2 5.1 put_in.21.rest_0_
  1254.4 5.1 put_in.22.rest_0_
  1259.5 5.1 put_in.23
  (119 shorter events, 57.1 us)
Async XLA Ops:
  527.8 3.6 collective-permute-start
  528.2 3.6 collective-permute-start.1
  531.4 10.8 copy-start.8
  531.8 10.4 copy-start.10
  551.0 60.0 %collective-permute-start.22 = (bf16[1408,768]{1,0:T(8,128)(2,1)}, bf16[1408,768]{1,0:T(8,128)(2,1)S(1)}, u32[]{:S(2)}, u32[]{:S(2)}) collective-permute-start(bf16[1408,768]{1,0:T(8,128)(2,1)} %mix.15), channel_id=1, source_target_pairs={{0,2},{2,0},{4,6},{6,4},{1,3},{3,1},{5,7},{7,5}} | collective-permute-start | bytes 6488072 | tf_op jit(solution)/shard_map/ppermute | solution.py:418
  572.0 75.6 %collective-permute-start.19 = (bf16[1408,768]{1,0:T(8,128)(2,1)}, bf16[1408,768]{1,0:T(8,128)(2,1)}, u32[]{:S(2)}, u32[]{:S(2)}) collective-permute-start(bf16[1408,768]{1,0:T(8,128)(2,1)} %mix.17), channel_id=1, source_target_pairs={{0,2},{2,0},{4,6},{6,4},{1,3},{3,1},{5,7},{7,5}} | collective-permute-start | bytes 6488072 | tf_op jit(solution)/shard_map/ppermute | solution.py:418
  572.4 17.3 %slice-start.2 = ((s8[4325376]{0:T(1024)(128)(4,1)}), s8[4194304]{0:T(1024)(128)(4,1)S(1)}, s32[]{:S(2)}) async-start(s8[4325376]{0:T(1024)(128)(4,1)} %bitcast.27), calls=%async_computation.2 | async-start | bytes 8388608
  581.7 8.0 slice-start.3
  581.7 17.5 %slice-start = ((s8[4325376]{0:T(1024)(128)(4,1)}), s8[4194304]{0:T(1024)(128)(4,1)S(1)}, s32[]{:S(2)}) async-start(s8[4325376]{0:T(1024)(128)(4,1)} %bitcast.25), calls=%async_computation | async-start | bytes 8388608
  589.7 9.5 slice-start.1
  599.2 14.7 %copy-start.9 = (f32[2]{0:T(128)S(1)}, f32[2]{0:T(128)}, u32[]{:S(2)}) copy-start(f32[2]{0:T(128)} %copy-done.8) | copy-start | bytes 28
  599.2 14.7 %copy-start.11 = (f32[2]{0:T(128)S(1)}, f32[2]{0:T(128)}, u32[]{:S(2)}) copy-start(f32[2]{0:T(128)} %copy-done.10) | copy-start | bytes 28
  607.3 84.4 %collective-permute-start.16 = (bf16[1408,768]{1,0:T(8,128)(2,1)}, bf16[1408,768]{1,0:T(8,128)(2,1)}, u32[]{:S(2)}, u32[]{:S(2)}) collective-permute-start(bf16[1408,768]{1,0:T(8,128)(2,1)} %mix.24), channel_id=1, source_target_pairs={{0,2},{2,0},{4,6},{6,4},{1,3},{3,1},{5,7},{7,5}} | collective-permute-start | bytes 6488072 | tf_op jit(solution)/shard_map/ppermute | solution.py:418
  609.0 84.4 %collective-permute-start.15 = (bf16[1408,768]{1,0:T(8,128)(2,1)}, bf16[1408,768]{1,0:T(8,128)(2,1)}, u32[]{:S(2)}, u32[]{:S(2)}) collective-permute-start(bf16[1408,768]{1,0:T(8,128)(2,1)} %mix.19), channel_id=1, source_target_pairs={{0,4},{2,6},{4,0},{6,2},{1,5},{3,7},{5,1},{7,3}} | collective-permute-start | bytes 6488072 | tf_op jit(solution)/shard_map/ppermute | solution.py:419
  610.4 95.2 %collective-permute-start.9 = (bf16[352,3072]{1,0:T(8,128)(2,1)}, bf16[352,3072]{1,0:T(8,128)(2,1)}, u32[]{:S(2)}, u32[]{:S(2)}) collective-permute-start(bf16[352,3072]{1,0:T(8,128)(2,1)} %mix.14), channel_id=1, source_target_pairs={{0,4},{2,6},{4,0},{6,2},{1,5},{3,7},{5,1},{7,3}} | collective-permute-start | bytes 6488072 | tf_op jit(solution)/shard_map/ppermute | solution.py:419
  611.0 1.5 copy-start
  612.4 139.4 %collective-permute-start.6 = (bf16[352,3072]{1,0:T(8,128)(2,1)}, bf16[352,3072]{1,0:T(8,128)(2,1)}, u32[]{:S(2)}, u32[]{:S(2)}) collective-permute-start(bf16[352,3072]{1,0:T(8,128)(2,1)} %mix.16), channel_id=1, source_target_pairs={{0,4},{2,6},{4,0},{6,2},{1,5},{3,7},{5,1},{7,3}} | collective-permute-start | bytes 6488072 | tf_op jit(solution)/shard_map/ppermute | solution.py:419
  614.0 1.6 copy-start.1
  647.6 147.8 %collective-permute-start.3 = (bf16[352,3072]{1,0:T(8,128)(2,1)}, bf16[352,3072]{1,0:T(8,128)(2,1)}, u32[]{:S(2)}, u32[]{:S(2)}) collective-permute-start(bf16[352,3072]{1,0:T(8,128)(2,1)} %mix.20), channel_id=1, source_target_pairs={{0,4},{2,6},{4,0},{6,2},{1,5},{3,7},{5,1},{7,3}} | collective-permute-start | bytes 6488072 | tf_op jit(solution)/shard_map/ppermute | solution.py:419
  691.7 105.1 %collective-permute-start.2 = (bf16[352,3072]{1,0:T(8,128)(2,1)}, bf16[352,3072]{1,0:T(8,128)(2,1)}, u32[]{:S(2)}, u32[]{:S(2)}) collective-permute-start(bf16[352,3072]{1,0:T(8,128)(2,1)} %mix.18), channel_id=1, source_target_pairs={{0,2},{2,0},{4,6},{6,4},{1,3},{3,1},{5,7},{7,5}} | collective-permute-start | bytes 6488072 | tf_op jit(solution)/shard_map/ppermute | solution.py:418
  693.3 104.1 %collective-permute-start.23 = (bf16[1408,768]{1,0:T(8,128)(2,1)S(1)}, bf16[1408,768]{1,0:T(8,128)(2,1)}, u32[]{:S(2)}, u32[]{:S(2)}) collective-permute-start(bf16[1408,768]{1,0:T(8,128)(2,1)S(1)} %mix.27.piece_ref), channel_id=1, source_target_pairs={{0,2},{2,0},{4,6},{6,4},{1,3},{3,1},{5,7},{7,5}} | collective-permute-start | bytes 6488072 | tf_op jit(solution)/shard_map/ppermute | solution.py:418
  705.5 129.1 %collective-permute-start.20 = (bf16[1408,768]{1,0:T(8,128)(2,1)}, bf16[1408,768]{1,0:T(8,128)(2,1)}, u32[]{:S(2)}, u32[]{:S(2)}) collective-permute-start(bf16[1408,768]{1,0:T(8,128)(2,1)} %mix.26.piece_ref), channel_id=1, source_target_pairs={{0,2},{2,0},{4,6},{6,4},{1,3},{3,1},{5,7},{7,5}} | collective-permute-start | bytes 6488072 | tf_op jit(solution)/shard_map/ppermute | solution.py:418
  751.9 126.0 %collective-permute-start.17 = (bf16[1408,768]{1,0:T(8,128)(2,1)}, bf16[1408,768]{1,0:T(8,128)(2,1)}, u32[]{:S(2)}, u32[]{:S(2)}) collective-permute-start(bf16[1408,768]{1,0:T(8,128)(2,1)} %mix.25.piece_ref), channel_id=1, source_target_pairs={{0,2},{2,0},{4,6},{6,4},{1,3},{3,1},{5,7},{7,5}} | collective-permute-start | bytes 6488072 | tf_op jit(solution)/shard_map/ppermute | solution.py:418
  795.4 94.3 %collective-permute-start.27 = (bf16[1408,768]{1,0:T(8,128)(2,1)S(1)}, bf16[1408,768]{1,0:T(8,128)(2,1)S(1)}, u32[]{:S(2)}, u32[]{:S(2)}) collective-permute-start(bf16[1408,768]{1,0:T(8,128)(2,1)S(1)} %mix.27.piece_ref), channel_id=1, source_target_pairs={{0,4},{2,6},{4,0},{6,2},{1,5},{3,7},{5,1},{7,3}} | collective-permute-start | bytes 6488072 | tf_op jit(solution)/shard_map/ppermute | solution.py:419
  796.8 94.9 %collective-permute-start.26 = (bf16[1408,768]{1,0:T(8,128)(2,1)}, bf16[1408,768]{1,0:T(8,128)(2,1)S(1)}, u32[]{:S(2)}, u32[]{:S(2)}) collective-permute-start(bf16[1408,768]{1,0:T(8,128)(2,1)} %mix.26.piece_ref), channel_id=1, source_target_pairs={{0,4},{2,6},{4,0},{6,2},{1,5},{3,7},{5,1},{7,3}} | collective-permute-start | bytes 6488072 | tf_op jit(solution)/shard_map/ppermute | solution.py:419
  797.4 140.6 %collective-permute-start.25 = (bf16[1408,768]{1,0:T(8,128)(2,1)}, bf16[1408,768]{1,0:T(8,128)(2,1)S(1)}, u32[]{:S(2)}, u32[]{:S(2)}) collective-permute-start(bf16[1408,768]{1,0:T(8,128)(2,1)} %mix.25.piece_ref), channel_id=1, source_target_pairs={{0,4},{2,6},{4,0},{6,2},{1,5},{3,7},{5,1},{7,3}} | collective-permute-start | bytes 6488072 | tf_op jit(solution)/shard_map/ppermute | solution.py:419
  834.6 149.9 %collective-permute-start.10 = (bf16[352,3072]{1,0:T(8,128)(2,1)}, bf16[352,3072]{1,0:T(8,128)(2,1)}, u32[]{:S(2)}, u32[]{:S(2)}) collective-permute-start(bf16[352,3072]{1,0:T(8,128)(2,1)} %mix.23.piece_ref), channel_id=1, source_target_pairs={{0,4},{2,6},{4,0},{6,2},{1,5},{3,7},{5,1},{7,3}} | collective-permute-start | bytes 6488072 | tf_op jit(solution)/shard_map/ppermute | solution.py:419
  877.9 152.9 %collective-permute-start.7 = (bf16[352,3072]{1,0:T(8,128)(2,1)}, bf16[352,3072]{1,0:T(8,128)(2,1)}, u32[]{:S(2)}, u32[]{:S(2)}) collective-permute-start(bf16[352,3072]{1,0:T(8,128)(2,1)} %mix.22.piece_ref), channel_id=1, source_target_pairs={{0,4},{2,6},{4,0},{6,2},{1,5},{3,7},{5,1},{7,3}} | collective-permute-start | bytes 6488072 | tf_op jit(solution)/shard_map/ppermute | solution.py:419
  889.7 1.5 copy-start.2
  891.2 185.9 %collective-permute-start.4 = (bf16[352,3072]{1,0:T(8,128)(2,1)}, bf16[352,3072]{1,0:T(8,128)(2,1)}, u32[]{:S(2)}, u32[]{:S(2)}) collective-permute-start(bf16[352,3072]{1,0:T(8,128)(2,1)} %mix.21.piece_ref), channel_id=1, source_target_pairs={{0,4},{2,6},{4,0},{6,2},{1,5},{3,7},{5,1},{7,3}} | collective-permute-start | bytes 6488072 | tf_op jit(solution)/shard_map/ppermute | solution.py:419
  891.7 1.3 copy-start.4
  893.0 185.5 %collective-permute-start.14 = (bf16[352,3072]{1,0:T(8,128)(2,1)}, bf16[352,3072]{1,0:T(8,128)(2,1)}, u32[]{:S(2)}, u32[]{:S(2)}) collective-permute-start(bf16[352,3072]{1,0:T(8,128)(2,1)} %mix.23.piece_ref), channel_id=1, source_target_pairs={{0,2},{2,0},{4,6},{6,4},{1,3},{3,1},{5,7},{7,5}} | collective-permute-start | bytes 6488072 | tf_op jit(solution)/shard_map/ppermute | solution.py:418
  938.0 1.4 copy-start.6
  939.4 139.8 %collective-permute-start.13 = (bf16[352,3072]{1,0:T(8,128)(2,1)}, bf16[352,3072]{1,0:T(8,128)(2,1)}, u32[]{:S(2)}, u32[]{:S(2)}) collective-permute-start(bf16[352,3072]{1,0:T(8,128)(2,1)} %mix.22.piece_ref), channel_id=1, source_target_pairs={{0,2},{2,0},{4,6},{6,4},{1,3},{3,1},{5,7},{7,5}} | collective-permute-start | bytes 6488072 | tf_op jit(solution)/shard_map/ppermute | solution.py:418
  984.5 95.1 %collective-permute-start.12 = (bf16[352,3072]{1,0:T(8,128)(2,1)}, bf16[352,3072]{1,0:T(8,128)(2,1)}, u32[]{:S(2)}, u32[]{:S(2)}) collective-permute-start(bf16[352,3072]{1,0:T(8,128)(2,1)} %mix.21.piece_ref), channel_id=1, source_target_pairs={{0,2},{2,0},{4,6},{6,4},{1,3},{3,1},{5,7},{7,5}} | collective-permute-start | bytes 6488072 | tf_op jit(solution)/shard_map/ppermute | solution.py:418
  1030.8 92.7 %collective-permute-start.24 = (bf16[1408,768]{1,0:T(8,128)(2,1)}, bf16[1408,768]{1,0:T(8,128)(2,1)}, u32[]{:S(2)}, u32[]{:S(2)}) collective-permute-start(bf16[1408,768]{1,0:T(8,128)(2,1)} %collective-permute-done.23.piece_ref), channel_id=1, source_target_pairs={{0,4},{2,6},{4,0},{6,2},{1,5},{3,7},{5,1},{7,3}} | collective-permute-start | bytes 6488072 | tf_op jit(solution)/shard_map/ppermute | solution.py:419
  1077.1 158.9 %collective-permute-start.21 = (bf16[1408,768]{1,0:T(8,128)(2,1)}, bf16[1408,768]{1,0:T(8,128)(2,1)}, u32[]{:S(2)}, u32[]{:S(2)}) collective-permute-start(bf16[1408,768]{1,0:T(8,128)(2,1)} %collective-permute-done.20.piece_ref), channel_id=1, source_target_pairs={{0,4},{2,6},{4,0},{6,2},{1,5},{3,7},{5,1},{7,3}} | collective-permute-start | bytes 6488072 | tf_op jit(solution)/shard_map/ppermute | solution.py:419
  1078.6 164.1 %collective-permute-start.18 = (bf16[1408,768]{1,0:T(8,128)(2,1)}, bf16[1408,768]{1,0:T(8,128)(2,1)}, u32[]{:S(2)}, u32[]{:S(2)}) collective-permute-start(bf16[1408,768]{1,0:T(8,128)(2,1)} %collective-permute-done.17.piece_ref), channel_id=1, source_target_pairs={{0,4},{2,6},{4,0},{6,2},{1,5},{3,7},{5,1},{7,3}} | collective-permute-start | bytes 6488072 | tf_op jit(solution)/shard_map/ppermute | solution.py:419
  1079.2 170.0 %collective-permute-start.11 = (bf16[352,3072]{1,0:T(8,128)(2,1)}, bf16[352,3072]{1,0:T(8,128)(2,1)}, u32[]{:S(2)}, u32[]{:S(2)}) collective-permute-start(bf16[352,3072]{1,0:T(8,128)(2,1)} %collective-permute-done.10.piece_ref), channel_id=1, source_target_pairs={{0,2},{2,0},{4,6},{6,4},{1,3},{3,1},{5,7},{7,5}} | collective-permute-start | bytes 6488072 | tf_op jit(solution)/shard_map/ppermute | solution.py:418
  1079.6 174.8 %collective-permute-start.8 = (bf16[352,3072]{1,0:T(8,128)(2,1)}, bf16[352,3072]{1,0:T(8,128)(2,1)}, u32[]{:S(2)}, u32[]{:S(2)}) collective-permute-start(bf16[352,3072]{1,0:T(8,128)(2,1)} %collective-permute-done.7.piece_ref), channel_id=1, source_target_pairs={{0,2},{2,0},{4,6},{6,4},{1,3},{3,1},{5,7},{7,5}} | collective-permute-start | bytes 6488072 | tf_op jit(solution)/shard_map/ppermute | solution.py:418
  1123.5 136.0 %collective-permute-start.5 = (bf16[352,3072]{1,0:T(8,128)(2,1)}, bf16[352,3072]{1,0:T(8,128)(2,1)}, u32[]{:S(2)}, u32[]{:S(2)}) collective-permute-start(bf16[352,3072]{1,0:T(8,128)(2,1)} %collective-permute-done.4.piece_ref), channel_id=1, source_target_pairs={{0,2},{2,0},{4,6},{6,4},{1,3},{3,1},{5,7},{7,5}} | collective-permute-start | bytes 6488072 | tf_op jit(solution)/shard_map/ppermute | solution.py:418
  1190.6 5.2 copy-start.3
  1195.8 6.1 copy-start.5
  1201.9 6.1 copy-start.7

commit v6 on v5

--- a/solution.py
+++ b/solution.py
@@ -15,6 +15,7 @@
 T_CHUNK = 256
 IN_SLOTS = 4
 LOAD_CHUNKS = 2
+MIX_ROWS = 32
 VMEM_LIMIT = 66_500_000
 
 F32 = jnp.float32
@@ -95,7 +96,7 @@
             device_id=tp_far, device_id_type=MESH)
 
     def front(load, to_dx):
-        n_in = LOAD_CHUNKS if load else (n_t if to_dx else n_t // 2)
+        n_in = (2 if to_dx else 1) * LOAD_CHUNKS if load else n_t
 
         def trip(i, carry):
             def dx_part(rows):
@@ -335,28 +336,33 @@
 
 
 def mix_kernel(sc_ref, coef_ref, *refs):
-    total = refs[0][0].astype(F32) * coef_ref[0]
-    for k, ref in enumerate(refs[1:-1]):
-        total = total + ref[0].astype(F32) * coef_ref[k + 1]
-    refs[-1][...] = total.astype(BF16)
+    def group(r, carry):
+        rows = pl.ds(pl.multiple_of(r * MIX_ROWS, MIX_ROWS), MIX_ROWS)
+        total = refs[0][0, rows, :].astype(F32) * coef_ref[0]
+        for k, ref in enumerate(refs[1:-1]):
+            total = total + ref[0, rows, :].astype(F32) * coef_ref[k + 1]
+        refs[-1][rows, :] = total.astype(BF16)
+        return carry
+
+    lax.fori_loop(0, refs[-1].shape[0] // MIX_ROWS, group, 0)
 
 
 def mix(which, shape, terms, coefs):
     rows, width = shape
-    block = (32, width) if which == 0 else (rows // 8, width)
+    block = (rows, width // 4) if which == 0 else (rows // 4, width)
 
     def spec(k, lead):
         if which == 0:
-            return pl.BlockSpec((1, *block), lambda i, sc: (lead, (rows // block[0]) * sc[k] + i, 0))
+            return pl.BlockSpec((1, *block), lambda i, sc: (lead, sc[k], i))
         return pl.BlockSpec((1, *block), lambda i, sc: (lead, i, sc[k]))
 
-    out_map = lambda i, sc: (i, 0)
+    out_map = (lambda i, sc: (0, i)) if which == 0 else (lambda i, sc: (i, 0))
     places = jnp.stack([jnp.asarray(p, jnp.int32) for _, _, p in terms])
     return pl.pallas_call(
         mix_kernel,
         out_shape=jax.ShapeDtypeStruct((rows, width), BF16),
         grid_spec=pltpu.PrefetchScalarGridSpec(
-            num_scalar_prefetch=1, grid=(rows // block[0],),
+            num_scalar_prefetch=1, grid=(4,),
             in_specs=[pl.BlockSpec(memory_space=pltpu.SMEM)] + [spec(k, lead) for k, (_, lead, _) in enumerate(terms)],
             out_specs=pl.BlockSpec(block, out_map)),
         compiler_params=pltpu.CompilerParams(dimension_semantics=('arbitrary',), vmem_limit_bytes=40_000_000),
@@ -421,7 +427,8 @@
         g1k, _, g1r, g2k, _, g2r, g1l, g2l, _, g1er, _, g2er, squares = res[3:]
         part_sq = jnp.sum(squares, axis=(1, 2))
         clip = jnp.minimum(1.0, clip_norm / jnp.sqrt(lax.psum(part_sq, 'tp')))
-        clip, clip_x, clip_y = lax.optimization_barrier((clip, over_x(clip), over_y(clip)))
+        clip_x = over_x(clip)
+        clip_y = over_y(clip)
         c_own, c_x, c_y = [[v[k] for k in range(local_batch)] for v in (clip, clip_x, clip_y)]
         coef = jnp.stack([noise_mult * clip_norm, jnp.float32(1.0 / batch_total)])
 
@@ -439,17 +446,14 @@
             first = (n_layers - 1 - layer) * local_batch
             return [(early[which], first + k, pos) for k in range(local_batch)]
 
+        made = []
+
         def mixed(which, terms, coefs):
-            return mix(which, shapes[which], terms, jnp.stack([jnp.asarray(c, F32) for c in coefs]))
-
-        made = []
-
-        def send(which, terms, coefs, over):
             coefs = jnp.stack([jnp.asarray(c, F32) for c in coefs])
             if made:
                 coefs, _ = lax.optimization_barrier((coefs, made[-1]))
             made.append(mix(which, shapes[which], terms, coefs))
-            return over(made[-1])
+            return made[-1]
 
         def pair_terms(layer, which, to_send, *more):
             pos = 1 - at_side[which] if to_send else at_side[which]
@@ -466,21 +470,19 @@
             terms += [(v[None], 0, 0) for v in more]
             return terms, coefs + [1.0] * len(more)
 
-        got = {}
-        for layer in range(n_layers - 1, 0, -1):
+        got, far_last, places = {}, {}, {}
+        for which in (0, 1):
+            far_last[which] = over_half[which](
+                mixed(which, own_terms(0, which, 1 - at_half[which], at_side[which]), c_own))
+        for layer in range(n_layers - 1, -1, -1):
             for which in (0, 1):
-                got[layer, which] = send(which, *pair_terms(layer, which, True), over_side[which])
-        far_last = [
-            send(which, own_terms(0, which, 1 - at_half[which], at_side[which]), c_own, over_half[which]) for which in (0, 1)]
-        for which in (0, 1):
-            got[0, which] = send(which, *pair_terms(0, which, True), over_side[which])
-
-        places = {}
+                got[layer, which] = over_side[which](mixed(which, *pair_terms(layer, which, True)))
         for layer in range(n_layers - 1, -1, -1):
             for which in (0, 1):
                 half_pos, pos = at_half[which], at_side[which]
                 own = mixed(which, *pair_terms(layer, which, False, got[layer, which]))
-                near, side = over_side[which](own), over_half[which](own)
+                near = over_side[which](own)
+                side = over_half[which](own)
                 diag = over_half[which](near)
                 places[layer, which] = (
                     (2 * half_pos + pos, own), (2 * half_pos + 1 - pos, near),

time: 1270 us -> 1220 us (0.961)
  Pallas kernels: 793 us -> 756 us
    ppermute x14, waiting for transfers between devices: 291 us -> 254 us  [local_step(): over_y = lambda v: lax.ppermute(v, 'dp', swap_y)]
    pallas_call x14, Pallas kernels: 131 us -> 98.8 us  [mix(): pl.pallas_call(mix_kernel, out_shape=jax.ShapeDtypeStruct((rows, width),...]
    ppermute x14, waiting for transfers between devices: 136 us -> 162 us  [local_step(): over_x = lambda v: lax.ppermute(v, 'dp', swap_x)]
  transfers between devices with their start and end apart: 28 -> 28, of which waited for: 14 -> 14; matrix products, arithmetic and copies ran while one was open for 0% -> 0% of each run, Pallas kernels for 19% -> 18%
where the time goes in v6:
time: 1220 us
  Pallas kernels  756 us (62%)
  waiting for transfers between devices  416 us (34%)
  starting transfers between devices  30.4 us (2%)
    pallas_call x1, Pallas kernels, run_stack(): pl.pallas_call(functools.partial(stack_kernel, n_layers, n_ex, n_steps),...  521 us
    ppermute x14, waiting for transfers between devices, local_step(): over_y = lambda v: lax.ppermute(v, 'dp', swap_y)  254 us
    ppermute x14, waiting for transfers between devices, local_step(): over_x = lambda v: lax.ppermute(v, 'dp', swap_x)  162 us
    pallas_call x24, Pallas kernels, put_piece(): pl.pallas_call(put_out_kernel if transposed else put_in_kernel, out_shape...  137 us
    pallas_call x14, Pallas kernels, mix(): pl.pallas_call(mix_kernel, out_shape=jax.ShapeDtypeStruct((rows, width),...  98.8 us
  transfers between devices with their start and end apart: 28, of which 14 were waited for; matrix products, arithmetic and copies ran while one was open for 0% of the time, Pallas kernels for 18%

profile of v6, /device:TPU:0, one launch (start us, length us, event | category | flops | bytes accessed | tf_op | source)
XLA Modules:
  0.0 1221.7 jit_solution(17399511202165387064)
XLA Ops:
  0.6 520.6 %stack.288 = (bf16[4,2048,1408]{2,1,0:T(8,128)(2,1)}, bf16[4,2048,1408]{2,1,0:T(8,128)(2,1)}, bf16[2,2048,1408]{2,1,0:T(8,128)(2,1)}, f32[4,704,3072]{2,1,0:T(8,...) custom-call(bf16[3,2,2048,3072]{3,2,1,0:T(8,128)(2,1)} %u_ref.1, ...), custom_call_target="tpu_custom_call" | custom-call | flops 389768282112 | bytes 500000000 | tf_op jit(solution)/shard_map/stack/pallas_call | solution.py:325
  527.3 6.1 mix.14
  533.5 6.1 mix.15
  539.7 7.5 mix.16
  547.6 7.5 mix.17
  556.7 7.6 mix.18
  566.3 7.8 mix.19
  577.8 6.5 mix.20
  584.3 13.0 %collective-permute-done.2 = bf16[352,3072]{1,0:T(8,128)(2,1)S(1)} collective-permute-done((bf16[352,3072]{1,0:T(8,128)(2,1)}, bf16[352,3072]{1,0:T(8,128)(2,1)S(1)}, u32[]{:S(2)}, u32[]{:S(2)}) %collective-permute-start.2) | collective-permute-done | bytes 2162720 | tf_op jit(solution)/shard_map/ppermute | solution.py:425
  597.8 6.5 mix.21
  606.9 36.8 %collective-permute-done.4 = bf16[352,3072]{1,0:T(8,128)(2,1)} collective-permute-done((bf16[352,3072]{1,0:T(8,128)(2,1)}, bf16[352,3072]{1,0:T(8,128)(2,1)}, u32[]{:S(2)}, u32[]{:S(2)}) %collective-permute-start.4) | collective-permute-done | bytes 2162720 | tf_op jit(solution)/shard_map/ppermute | solution.py:425
  647.1 6.8 mix.22.piece_ref
  653.9 7.1 mix.23.piece_ref
  661.0 8.5 mix.24.piece_ref
  669.4 28.6 %collective-permute-done.5 = bf16[1408,768]{1,0:T(8,128)(2,1)} collective-permute-done((bf16[1408,768]{1,0:T(8,128)(2,1)}, bf16[1408,768]{1,0:T(8,128)(2,1)}, u32[]{:S(2)}, u32[]{:S(2)}) %collective-permute-start.5) | collective-permute-done | bytes 2162720 | tf_op jit(solution)/shard_map/ppermute | solution.py:424
  699.6 7.1 mix.25.piece_ref
  707.1 7.6 mix.26.piece_ref
  714.8 20.3 %collective-permute-done.17 = bf16[1408,768]{1,0:T(8,128)(2,1)} collective-permute-done((bf16[1408,768]{1,0:T(8,128)(2,1)}, bf16[1408,768]{1,0:T(8,128)(2,1)}, u32[]{:S(2)}, u32[]{:S(2)}) %collective-permute-start.17) | collective-permute-done | bytes 2162720 | tf_op jit(solution)/shard_map/ppermute | solution.py:425
  735.1 9.2 collective-permute-done.18
  744.3 6.4 mix.27.piece_ref
  754.4 36.3 %collective-permute-done.23.piece_ref = bf16[1408,768]{1,0:T(8,128)(2,1)} collective-permute-done((bf16[1408,768]{1,0:T(8,128)(2,1)S(1)}, bf16[1408,768]{1,0:T(8,128)(2,1)}, u32[]{:S(2)}, u32[]{:S(2)}) %collective-permute-start.23) | collective-permute-done | bytes 2162720 | tf_op jit(solution)/shard_map/ppermute | solution.py:424
  793.6 43.4 %collective-permute-done.21.piece_ref = bf16[1408,768]{1,0:T(8,128)(2,1)} collective-permute-done((bf16[1408,768]{1,0:T(8,128)(2,1)S(1)}, bf16[1408,768]{1,0:T(8,128)(2,1)}, u32[]{:S(2)}, u32[]{:S(2)}) %collective-permute-start.21) | collective-permute-done | bytes 2162720 | tf_op jit(solution)/shard_map/ppermute | solution.py:424
  838.7 43.1 %collective-permute-done.19.piece_ref = bf16[1408,768]{1,0:T(8,128)(2,1)} collective-permute-done((bf16[1408,768]{1,0:T(8,128)(2,1)S(1)}, bf16[1408,768]{1,0:T(8,128)(2,1)}, u32[]{:S(2)}, u32[]{:S(2)}) %collective-permute-start.19) | collective-permute-done | bytes 2162720 | tf_op jit(solution)/shard_map/ppermute | solution.py:424
  888.2 6.7 collective-permute-done.25.piece_ref
  896.7 44.7 %collective-permute-done.12.piece_ref = bf16[352,3072]{1,0:T(8,128)(2,1)} collective-permute-done((bf16[352,3072]{1,0:T(8,128)(2,1)S(1)}, bf16[352,3072]{1,0:T(8,128)(2,1)}, u32[]{:S(2)}, u32[]{:S(2)}) %collective-permute-start.12) | collective-permute-done | bytes 2162720 | tf_op jit(solution)/shard_map/ppermute | solution.py:425
  941.8 46.0 %collective-permute-done.10.piece_ref = bf16[352,3072]{1,0:T(8,128)(2,1)} collective-permute-done((bf16[352,3072]{1,0:T(8,128)(2,1)}, bf16[352,3072]{1,0:T(8,128)(2,1)}, u32[]{:S(2)}, u32[]{:S(2)}) %collective-permute-start.10) | collective-permute-done | bytes 2162720 | tf_op jit(solution)/shard_map/ppermute | solution.py:425
  989.6 44.5 %collective-permute-done.8.piece_ref = bf16[352,3072]{1,0:T(8,128)(2,1)} collective-permute-done((bf16[352,3072]{1,0:T(8,128)(2,1)}, bf16[352,3072]{1,0:T(8,128)(2,1)}, u32[]{:S(2)}, u32[]{:S(2)}) %collective-permute-start.8) | collective-permute-done | bytes 2162720 | tf_op jit(solution)/shard_map/ppermute | solution.py:425
  1038.2 42.3 %collective-permute-done.24.piece_ref = bf16[1408,768]{1,0:T(8,128)(2,1)} collective-permute-done((bf16[1408,768]{1,0:T(8,128)(2,1)}, bf16[1408,768]{1,0:T(8,128)(2,1)}, u32[]{:S(2)}, u32[]{:S(2)}) %collective-permute-start.24) | collective-permute-done | bytes 2162720 | tf_op jit(solution)/shard_map/ppermute | solution.py:425
  1084.6 6.1 put_out.12.rest_0_
  1090.8 6.1 put_out.13.rest_0_
  1096.9 6.1 put_out.14.rest_0_
  1107.5 5.1 put_in.13.rest_0_
  1112.6 5.1 put_in.14.rest_0_
  1117.7 6.6 put_out.15.rest_0_
  1124.3 6.6 put_out.16.rest_0_
  1130.9 6.6 put_out.17.rest_0_
  1137.4 5.1 put_in.15.rest_0_
  1147.7 5.2 put_in.17.rest_0_
  1152.9 6.1 put_out.18.rest_0_
  1159.0 6.1 put_out.19.rest_0_
  1165.1 6.1 put_out.20.rest_0_
  1181.5 5.1 put_in.20.rest_0_
  1186.6 6.6 put_out.21.rest_0_
  1193.2 6.6 put_out.22.rest_0_
  1199.7 6.6 put_out.23
  1206.3 5.1 put_in.21.rest_0_
  1211.4 5.1 put_in.22.rest_0_
  1216.6 5.1 put_in.23
  (132 shorter events, 68.1 us)
Async XLA Ops:
  525.2 14.4 %copy-start.15 = (f32[2]{0:T(128)}, f32[2]{0:T(128)S(1)}, u32[]{:S(2)}) copy-start(f32[2]{0:T(128)S(1)} %multiply_minimum_fusion.coef_ref) | copy-start | bytes 28
  525.2 14.3 %collective-permute-start = (f32[2]{0:T(128)S(1)}, f32[2]{0:T(128)S(1)}, u32[]{:S(2)}, u32[]{:S(2)}) collective-permute-start(f32[2]{0:T(128)S(1)} %multiply_minimum_fusion.coef_ref), channel_id=1, source_target_pairs={{0,4},{2,6},{4,0},{6,2},{1,5},{3,7},{5,1},{7,3}} | collective-permute-start | bytes 32 | tf_op jit(solution)/shard_map/ppermute | solution.py:425
  526.7 12.9 %collective-permute-start.1 = (f32[2]{0:T(128)S(1)}, f32[2]{0:T(128)S(1)}, u32[]{:S(2)}, u32[]{:S(2)}) collective-permute-start(f32[2]{0:T(128)S(1)} %multiply_minimum_fusion.coef_ref), channel_id=1, source_target_pairs={{0,2},{2,0},{4,6},{6,4},{1,3},{3,1},{5,7},{7,5}} | collective-permute-start | bytes 32 | tf_op jit(solution)/shard_map/ppermute | solution.py:424
  539.6 7.6 copy-start.17
  539.6 7.6 copy-start.19
  547.2 50.1 %collective-permute-start.2 = (bf16[352,3072]{1,0:T(8,128)(2,1)}, bf16[352,3072]{1,0:T(8,128)(2,1)S(1)}, u32[]{:S(2)}, u32[]{:S(2)}) collective-permute-start(bf16[352,3072]{1,0:T(8,128)(2,1)} %mix.16), channel_id=1, source_target_pairs={{0,4},{2,6},{4,0},{6,2},{1,5},{3,7},{5,1},{7,3}} | collective-permute-start | bytes 6488072 | tf_op jit(solution)/shard_map/ppermute | solution.py:425
  555.1 50.2 %collective-permute-start.3 = (bf16[1408,768]{1,0:T(8,128)(2,1)}, bf16[1408,768]{1,0:T(8,128)(2,1)}, u32[]{:S(2)}, u32[]{:S(2)}) collective-permute-start(bf16[1408,768]{1,0:T(8,128)(2,1)} %mix.17), channel_id=1, source_target_pairs={{0,2},{2,0},{4,6},{6,4},{1,3},{3,1},{5,7},{7,5}} | collective-permute-start | bytes 6488072 | tf_op jit(solution)/shard_map/ppermute | solution.py:424
  556.7 41.0 %slice-start = ((s8[4325376]{0:T(1024)(128)(4,1)}), s8[131072]{0:T(1024)(128)(4,1)S(1)}, s32[]{:S(2)}) async-start(s8[4325376]{0:T(1024)(128)(4,1)} %bitcast.25), calls=%async_computation | async-start | bytes 262144
  564.3 79.5 %collective-permute-start.4 = (bf16[352,3072]{1,0:T(8,128)(2,1)}, bf16[352,3072]{1,0:T(8,128)(2,1)}, u32[]{:S(2)}, u32[]{:S(2)}) collective-permute-start(bf16[352,3072]{1,0:T(8,128)(2,1)} %mix.18), channel_id=1, source_target_pairs={{0,4},{2,6},{4,0},{6,2},{1,5},{3,7},{5,1},{7,3}} | collective-permute-start | bytes 6488072 | tf_op jit(solution)/shard_map/ppermute | solution.py:425
  565.7 141.0 %collective-permute-start.6 = (bf16[352,3072]{1,0:T(8,128)(2,1)}, bf16[352,3072]{1,0:T(8,128)(2,1)}, u32[]{:S(2)}, u32[]{:S(2)}) collective-permute-start(bf16[352,3072]{1,0:T(8,128)(2,1)} %mix.14), channel_id=1, source_target_pairs={{0,2},{2,0},{4,6},{6,4},{1,3},{3,1},{5,7},{7,5}} | collective-permute-start | bytes 6488072 | tf_op jit(solution)/shard_map/ppermute | solution.py:424
  566.3 31.4 %slice-start.1 = ((s8[4325376]{0:T(1024)(128)(4,1)}), s8[4194304]{0:T(1024)(128)(4,1)S(1)}, s32[]{:S(2)}) async-start(s8[4325376]{0:T(1024)(128)(4,1)} %bitcast.25), calls=%async_computation.1 | async-start | bytes 8388608
  574.1 123.9 %collective-permute-start.5 = (bf16[1408,768]{1,0:T(8,128)(2,1)}, bf16[1408,768]{1,0:T(8,128)(2,1)}, u32[]{:S(2)}, u32[]{:S(2)}) collective-permute-start(bf16[1408,768]{1,0:T(8,128)(2,1)} %mix.19), channel_id=1, source_target_pairs={{0,2},{2,0},{4,6},{6,4},{1,3},{3,1},{5,7},{7,5}} | collective-permute-start | bytes 6488072 | tf_op jit(solution)/shard_map/ppermute | solution.py:424
  575.6 2.2 copy-start
  597.3 6.9 copy-start.7
  597.3 109.8 %collective-permute-start.7 = (bf16[352,3072]{1,0:T(8,128)(2,1)}, bf16[352,3072]{1,0:T(8,128)(2,1)}, u32[]{:S(2)}, u32[]{:S(2)}) collective-permute-start(bf16[352,3072]{1,0:T(8,128)(2,1)} %mix.20), channel_id=1, source_target_pairs={{0,4},{2,6},{4,0},{6,2},{1,5},{3,7},{5,1},{7,3}} | collective-permute-start | bytes 6488072 | tf_op jit(solution)/shard_map/ppermute | solution.py:425
  597.7 47.7 %copy-start.16 = (f32[2]{0:T(128)S(1)}, f32[2]{0:T(128)}, u32[]{:S(2)}) copy-start(f32[2]{0:T(128)} %copy-done.15) | copy-start | bytes 28
  597.7 47.7 %copy-start.18 = (f32[2]{0:T(128)S(1)}, f32[2]{0:T(128)}, u32[]{:S(2)}) copy-start(f32[2]{0:T(128)} %copy-done.17) | copy-start | bytes 28
  597.7 47.7 %copy-start.20 = (f32[2]{0:T(128)S(1)}, f32[2]{0:T(128)}, u32[]{:S(2)}) copy-start(f32[2]{0:T(128)} %copy-done.19) | copy-start | bytes 28
  605.3 129.8 %collective-permute-start.17 = (bf16[1408,768]{1,0:T(8,128)(2,1)}, bf16[1408,768]{1,0:T(8,128)(2,1)}, u32[]{:S(2)}, u32[]{:S(2)}) collective-permute-start(bf16[1408,768]{1,0:T(8,128)(2,1)} %mix.15), channel_id=1, source_target_pairs={{0,4},{2,6},{4,0},{6,2},{1,5},{3,7},{5,1},{7,3}} | collective-permute-start | bytes 6488072 | tf_op jit(solution)/shard_map/ppermute | solution.py:425
  643.8 100.6 %collective-permute-start.18 = (bf16[1408,768]{1,0:T(8,128)(2,1)}, bf16[1408,768]{1,0:T(8,128)(2,1)}, u32[]{:S(2)}, u32[]{:S(2)}) collective-permute-start(bf16[1408,768]{1,0:T(8,128)(2,1)} %mix.21), channel_id=1, source_target_pairs={{0,2},{2,0},{4,6},{6,4},{1,3},{3,1},{5,7},{7,5}} | collective-permute-start | bytes 6488072 | tf_op jit(solution)/shard_map/ppermute | solution.py:424
  645.5 1.6 copy-start.8
  661.0 91.4 %copy-start.1 = (bf16[1408,768]{1,0:T(8,128)(2,1)}, bf16[1408,768]{1,0:T(8,128)(2,1)S(1)}, u32[]{:S(2)}) copy-start(bf16[1408,768]{1,0:T(8,128)(2,1)S(1)} %mix.23.piece_ref) | copy-start | bytes 6488068
  698.0 92.7 %collective-permute-start.23 = (bf16[1408,768]{1,0:T(8,128)(2,1)S(1)}, bf16[1408,768]{1,0:T(8,128)(2,1)}, u32[]{:S(2)}, u32[]{:S(2)}) collective-permute-start(bf16[1408,768]{1,0:T(8,128)(2,1)S(1)} %mix.23.piece_ref), channel_id=1, source_target_pairs={{0,2},{2,0},{4,6},{6,4},{1,3},{3,1},{5,7},{7,5}} | collective-permute-start | bytes 6488072 | tf_op jit(solution)/shard_map/ppermute | solution.py:424
  706.7 47.1 %copy-start.3 = (bf16[1408,768]{1,0:T(8,128)(2,1)}, bf16[1408,768]{1,0:T(8,128)(2,1)S(1)}, u32[]{:S(2)}) copy-start(bf16[1408,768]{1,0:T(8,128)(2,1)S(1)} %mix.25.piece_ref) | copy-start | bytes 6488068
  706.7 130.3 %collective-permute-start.21 = (bf16[1408,768]{1,0:T(8,128)(2,1)S(1)}, bf16[1408,768]{1,0:T(8,128)(2,1)}, u32[]{:S(2)}, u32[]{:S(2)}) collective-permute-start(bf16[1408,768]{1,0:T(8,128)(2,1)S(1)} %mix.25.piece_ref), channel_id=1, source_target_pairs={{0,2},{2,0},{4,6},{6,4},{1,3},{3,1},{5,7},{7,5}} | collective-permute-start | bytes 6488072 | tf_op jit(solution)/shard_map/ppermute | solution.py:424
  750.7 131.0 %collective-permute-start.19 = (bf16[1408,768]{1,0:T(8,128)(2,1)S(1)}, bf16[1408,768]{1,0:T(8,128)(2,1)}, u32[]{:S(2)}, u32[]{:S(2)}) collective-permute-start(bf16[1408,768]{1,0:T(8,128)(2,1)S(1)} %mix.27.piece_ref), channel_id=1, source_target_pairs={{0,2},{2,0},{4,6},{6,4},{1,3},{3,1},{5,7},{7,5}} | collective-permute-start | bytes 6488072 | tf_op jit(solution)/shard_map/ppermute | solution.py:424
  752.4 131.0 %collective-permute-start.27 = (bf16[1408,768]{1,0:T(8,128)(2,1)S(1)}, bf16[1408,768]{1,0:T(8,128)(2,1)S(1)}, u32[]{:S(2)}, u32[]{:S(2)}) collective-permute-start(bf16[1408,768]{1,0:T(8,128)(2,1)S(1)} %mix.23.piece_ref), channel_id=1, source_target_pairs={{0,4},{2,6},{4,0},{6,2},{1,5},{3,7},{5,1},{7,3}} | collective-permute-start | bytes 6488072 | tf_op jit(solution)/shard_map/ppermute | solution.py:425
  753.8 131.4 %collective-permute-start.26 = (bf16[1408,768]{1,0:T(8,128)(2,1)S(1)}, bf16[1408,768]{1,0:T(8,128)(2,1)S(1)}, u32[]{:S(2)}, u32[]{:S(2)}) collective-permute-start(bf16[1408,768]{1,0:T(8,128)(2,1)S(1)} %mix.25.piece_ref), channel_id=1, source_target_pairs={{0,4},{2,6},{4,0},{6,2},{1,5},{3,7},{5,1},{7,3}} | collective-permute-start | bytes 6488072 | tf_op jit(solution)/shard_map/ppermute | solution.py:425
  790.7 104.3 %collective-permute-start.25 = (bf16[1408,768]{1,0:T(8,128)(2,1)S(1)}, bf16[1408,768]{1,0:T(8,128)(2,1)S(1)}, u32[]{:S(2)}, u32[]{:S(2)}) collective-permute-start(bf16[1408,768]{1,0:T(8,128)(2,1)S(1)} %mix.27.piece_ref), channel_id=1, source_target_pairs={{0,4},{2,6},{4,0},{6,2},{1,5},{3,7},{5,1},{7,3}} | collective-permute-start | bytes 6488072 | tf_op jit(solution)/shard_map/ppermute | solution.py:425
  837.0 104.4 %collective-permute-start.12 = (bf16[352,3072]{1,0:T(8,128)(2,1)S(1)}, bf16[352,3072]{1,0:T(8,128)(2,1)}, u32[]{:S(2)}, u32[]{:S(2)}) collective-permute-start(bf16[352,3072]{1,0:T(8,128)(2,1)S(1)} %mix.22.piece_ref), channel_id=1, source_target_pairs={{0,4},{2,6},{4,0},{6,2},{1,5},{3,7},{5,1},{7,3}} | collective-permute-start | bytes 6488072 | tf_op jit(solution)/shard_map/ppermute | solution.py:425
  881.7 106.0 %collective-permute-start.10 = (bf16[352,3072]{1,0:T(8,128)(2,1)}, bf16[352,3072]{1,0:T(8,128)(2,1)}, u32[]{:S(2)}, u32[]{:S(2)}) collective-permute-start(bf16[352,3072]{1,0:T(8,128)(2,1)} %mix.24.piece_ref), channel_id=1, source_target_pairs={{0,4},{2,6},{4,0},{6,2},{1,5},{3,7},{5,1},{7,3}} | collective-permute-start | bytes 6488072 | tf_op jit(solution)/shard_map/ppermute | solution.py:425
  883.4 1.5 copy-start.9
  884.8 149.3 %collective-permute-start.8 = (bf16[352,3072]{1,0:T(8,128)(2,1)}, bf16[352,3072]{1,0:T(8,128)(2,1)}, u32[]{:S(2)}, u32[]{:S(2)}) collective-permute-start(bf16[352,3072]{1,0:T(8,128)(2,1)} %mix.26.piece_ref), channel_id=1, source_target_pairs={{0,4},{2,6},{4,0},{6,2},{1,5},{3,7},{5,1},{7,3}} | collective-permute-start | bytes 6488072 | tf_op jit(solution)/shard_map/ppermute | solution.py:425
  886.6 149.0 %collective-permute-start.16 = (bf16[352,3072]{1,0:T(8,128)(2,1)S(1)}, bf16[352,3072]{1,0:T(8,128)(2,1)}, u32[]{:S(2)}, u32[]{:S(2)}) collective-permute-start(bf16[352,3072]{1,0:T(8,128)(2,1)S(1)} %mix.22.piece_ref), channel_id=1, source_target_pairs={{0,2},{2,0},{4,6},{6,4},{1,3},{3,1},{5,7},{7,5}} | collective-permute-start | bytes 6488072 | tf_op jit(solution)/shard_map/ppermute | solution.py:424
  896.3 139.8 %collective-permute-start.15 = (bf16[352,3072]{1,0:T(8,128)(2,1)}, bf16[352,3072]{1,0:T(8,128)(2,1)}, u32[]{:S(2)}, u32[]{:S(2)}) collective-permute-start(bf16[352,3072]{1,0:T(8,128)(2,1)} %mix.24.piece_ref), channel_id=1, source_target_pairs={{0,2},{2,0},{4,6},{6,4},{1,3},{3,1},{5,7},{7,5}} | collective-permute-start | bytes 6488072 | tf_op jit(solution)/shard_map/ppermute | solution.py:424
  941.4 95.1 %collective-permute-start.14 = (bf16[352,3072]{1,0:T(8,128)(2,1)}, bf16[352,3072]{1,0:T(8,128)(2,1)}, u32[]{:S(2)}, u32[]{:S(2)}) collective-permute-start(bf16[352,3072]{1,0:T(8,128)(2,1)} %mix.26.piece_ref), channel_id=1, source_target_pairs={{0,2},{2,0},{4,6},{6,4},{1,3},{3,1},{5,7},{7,5}} | collective-permute-start | bytes 6488072 | tf_op jit(solution)/shard_map/ppermute | solution.py:424
  987.8 92.7 %collective-permute-start.24 = (bf16[1408,768]{1,0:T(8,128)(2,1)}, bf16[1408,768]{1,0:T(8,128)(2,1)}, u32[]{:S(2)}, u32[]{:S(2)}) collective-permute-start(bf16[1408,768]{1,0:T(8,128)(2,1)} %collective-permute-done.23.piece_ref), channel_id=1, source_target_pairs={{0,4},{2,6},{4,0},{6,2},{1,5},{3,7},{5,1},{7,3}} | collective-permute-start | bytes 6488072 | tf_op jit(solution)/shard_map/ppermute | solution.py:425
  1034.1 159.0 %collective-permute-start.22 = (bf16[1408,768]{1,0:T(8,128)(2,1)}, bf16[1408,768]{1,0:T(8,128)(2,1)}, u32[]{:S(2)}, u32[]{:S(2)}) collective-permute-start(bf16[1408,768]{1,0:T(8,128)(2,1)} %collective-permute-done.21.piece_ref), channel_id=1, source_target_pairs={{0,4},{2,6},{4,0},{6,2},{1,5},{3,7},{5,1},{7,3}} | collective-permute-start | bytes 6488072 | tf_op jit(solution)/shard_map/ppermute | solution.py:425
  1035.6 164.2 %collective-permute-start.20 = (bf16[1408,768]{1,0:T(8,128)(2,1)}, bf16[1408,768]{1,0:T(8,128)(2,1)}, u32[]{:S(2)}, u32[]{:S(2)}) collective-permute-start(bf16[1408,768]{1,0:T(8,128)(2,1)} %collective-permute-done.19.piece_ref), channel_id=1, source_target_pairs={{0,4},{2,6},{4,0},{6,2},{1,5},{3,7},{5,1},{7,3}} | collective-permute-start | bytes 6488072 | tf_op jit(solution)/shard_map/ppermute | solution.py:425
  1036.2 170.2 %collective-permute-start.13 = (bf16[352,3072]{1,0:T(8,128)(2,1)}, bf16[352,3072]{1,0:T(8,128)(2,1)}, u32[]{:S(2)}, u32[]{:S(2)}) collective-permute-start(bf16[352,3072]{1,0:T(8,128)(2,1)} %collective-permute-done.12.piece_ref), channel_id=1, source_target_pairs={{0,2},{2,0},{4,6},{6,4},{1,3},{3,1},{5,7},{7,5}} | collective-permute-start | bytes 6488072 | tf_op jit(solution)/shard_map/ppermute | solution.py:424
  1036.6 174.9 %collective-permute-start.11 = (bf16[352,3072]{1,0:T(8,128)(2,1)}, bf16[352,3072]{1,0:T(8,128)(2,1)}, u32[]{:S(2)}, u32[]{:S(2)}) collective-permute-start(bf16[352,3072]{1,0:T(8,128)(2,1)} %collective-permute-done.10.piece_ref), channel_id=1, source_target_pairs={{0,2},{2,0},{4,6},{6,4},{1,3},{3,1},{5,7},{7,5}} | collective-permute-start | bytes 6488072 | tf_op jit(solution)/shard_map/ppermute | solution.py:424
  1080.5 136.1 %collective-permute-start.9 = (bf16[352,3072]{1,0:T(8,128)(2,1)}, bf16[352,3072]{1,0:T(8,128)(2,1)}, u32[]{:S(2)}, u32[]{:S(2)}) collective-permute-start(bf16[352,3072]{1,0:T(8,128)(2,1)} %collective-permute-done.8.piece_ref), channel_id=1, source_target_pairs={{0,2},{2,0},{4,6},{6,4},{1,3},{3,1},{5,7},{7,5}} | collective-permute-start | bytes 6488072 | tf_op jit(solution)/shard_map/ppermute | solution.py:424
  1083.0 1.6 copy-start.2
  1084.6 6.1 copy-start.4
  1090.8 6.1 copy-start.6
  1147.7 5.2 copy-start.10
  1152.9 6.1 copy-start.12
  1159.0 6.1 copy-start.14
  (3 other events, 4.0 us)

commit v7 on v6

--- a/solution.py
+++ b/solution.py
@@ -16,7 +16,8 @@
 IN_SLOTS = 4
 LOAD_CHUNKS = 2
 MIX_ROWS = 32
-VMEM_LIMIT = 66_500_000
+N_SUM, N_FIRST, N_PUT = 20, 12, 32
+VMEM_LIMIT = 67_000_000
 
 F32 = jnp.float32
 BF16 = jnp.bfloat16
@@ -39,11 +40,11 @@
     return is_far * far + (1 - is_far) * own
 
 
-def stack_kernel(n_layers, n_ex, n_steps, u_ref, w1_ref, w2_ref, x_hbm, dout_hbm,
+def stack_kernel(n_layers, n_ex, n_steps, u_hbm, w1_hbm, w2_hbm, x_hbm, dout_hbm,
                  p_hbm, q_hbm, dzo_hbm, g1k_hbm, g1s_hbm, g1r_hbm, g2k_hbm, g2s_hbm, g2r_hbm,
                  g1l_hbm, g2l_hbm, g1e_hbm, g1er_hbm, g2e_hbm, g2er_hbm, ss_ref,
-                 x_t, dz, dz_t, dh, h, acc, x_st, z_st, p_st, q_st, g1_st, g1s_st, g2_st, g2s_st,
-                 in_sem, out_sem, io_sem, tp_send, tp_recv, far_send, far_recv):
+                 u_buf, w1_buf, w2_buf, x_t, dz, dz_t, dh, h, acc, x_st, z_st, p_st, q_st, g1_st, g1s_st, g2_st, g2s_st,
+                 block_sem, in_sem, out_sem, io_sem, tp_send, tp_recv, far_send, far_recv):
     task, step = pl.program_id(0), pl.program_id(1)
     n_early = (n_layers - 1) * n_ex
     n_task = n_early + n_ex
@@ -61,6 +62,30 @@
     cols = lambda k: pl.ds(pl.multiple_of(k * F_BLOCK, F_BLOCK), F_BLOCK)
     chunk = lambda c: pl.ds(c * T_CHUNK if isinstance(c, int) else pl.multiple_of(c * T_CHUNK, T_CHUNK), T_CHUNK)
 
+    def fetch(act, t, j, slot):
+        layer, at = n_layers - 1 - t // n_ex, cols(block_at(j, n_half, x_pos, y_pos))
+
+        def one(k, src, dst):
+            getattr(pltpu.make_async_copy(src, dst.at[slot], block_sem.at[k, slot]), act)()
+
+        one(0, u_hbm.at[layer, lax.rem(t, n_ex), :, at], u_buf)
+        one(1, w2_hbm.at[layer, at, :], w2_buf)
+        pl.when(t < n_early)(lambda: one(2, w1_hbm.at[layer, :, at], w1_buf))
+
+    ends = (step + 1) // n_steps
+    now = lax.rem(task * n_steps + step, 2)
+
+    def rarely(cond, body, n=1):
+        def trip(i, carry):
+            body(i)
+            return carry
+
+        lax.fori_loop(0, jnp.where(cond, n, 0), trip, 0)
+
+    is_first = (task == 0) & (step == 0)
+    rarely(is_first, lambda i: fetch('start', task, step, now))
+    pl.when(task + ends < n_task)(lambda: fetch('start', task + ends, step + 1 - n_steps * ends, 1 - now))
+
     def in_start(t, c):
         slot, rows, ex = lax.rem(c, IN_SLOTS), chunk(c), lax.rem(t, n_ex)
         copy = lambda k, src, dst: pltpu.make_async_copy(src, dst.at[slot], in_sem.at[k, slot]).start()
@@ -100,7 +125,7 @@
 
         def trip(i, carry):
             def dx_part(rows):
-                part = dot_nt(dh[rows, :], w1_ref[0])
+                part = dot_nt(dh[rows, :], w1_buf[now])
                 acc[rows, :] = part if load else acc[rows, :] + part
 
             for s in range(n_in):
@@ -119,12 +144,12 @@
                     dz[rows, :] = z
                     dz_t[:, rows] = z.T
                     x_t[:, rows] = x_st[slot].T
-                u = u_ref[0, 0, rows, :].astype(F32)
+                u = u_buf[now, rows, :].astype(F32)
                 t = u * INV_SQRT2
                 cdf = 0.5 * lax.erf(t) + 0.5
                 h[rows, :] = (u * cdf).astype(BF16)
                 slope = cdf + (t * (INV_SQRT_2PI / INV_SQRT2)) * jnp.exp2((t * t) * -LOG2_E)
-                dh[rows, :] = (slope * dot_nt(dz[rows, :], w2_ref[0])).astype(BF16)
+                dh[rows, :] = (slope * dot_nt(dz[rows, :], w2_buf[now])).astype(BF16)
                 if to_dx and s:
                     dx_part(chunk(c - 1))
             if to_dx:
@@ -136,12 +161,13 @@
         else:
             lax.fori_loop(0, n_t // n_in, trip, 0)
 
-    @pl.when((task == 0) & (step == 0))
-    def _():
+    def begin(c):
         ss_ref[...] = jnp.zeros_like(ss_ref)
-        for c in range(IN_SLOTS - 1):
-            in_start(task, c)
-
+        in_start(task, c)
+
+    rarely(is_first, begin, IN_SLOTS - 1)
+
+    fetch('wait', task, step, now)
     for load in (True, False):
         for to_dx in (True, False):
             @pl.when(((step == 0) if load else (step > 0)) & ((task < n_early) if to_dx else (task >= n_early)))
@@ -165,68 +191,66 @@
         lax.fori_loop(0, n_t, put, 0)
         dx_out.start()
 
-    def out_copies(t, j):
-        early, is_far, fb = t < n_early, j < n_half, block_at(j, n_half, x_pos, y_pos)
-        copy = lambda n, src, dst: pltpu.make_async_copy(src, dst, out_sem.at[n])
-        t_e, t_l = jnp.minimum(t, n_early - 1), jnp.maximum(t - n_early, 0)
-        own_rows = pl.ds(pl.multiple_of(x_pos * half_d, 16), half_d)
-        pass_rows = pl.ds(pl.multiple_of((1 - y_pos) * quarter_d, 16), quarter_d)
-        in_half = cols(lax.rem(fb, n_half))
-        src_half = pl.ds(pl.multiple_of((1 - x_pos) * half_b, half_b), half_b)
-        dst_half = pl.ds(pl.multiple_of(x_pos * F_BLOCK, half_b), half_b)
-        dst_full = pl.ds(pl.multiple_of((1 - x_pos) * half_b, half_b), F_BLOCK)
-        return [
-            (early, copy(0, g1_st.at[own_rows, :], g1k_hbm.at[t_e, :, cols(fb)])),
-            (early, copy(1, g1s_st, g1s_hbm.at[t_e, :, cols(fb)])),
-            (early & is_far, copy(2, g2s_st, g2s_hbm.at[t_e, :, in_half])),
-            (early & ~is_far, copy(3, g2_st, g2k_hbm.at[t_e, :, in_half])),
-            (~early, copy(0, g1_st, g1l_hbm.at[t_l, :, cols(fb)])),
-            (~early, copy(1, g1s_st.at[pass_rows, :], g1e_hbm.at[t_l, :, cols(fb)])),
-            (~early & (j == 0), copy(2, g2s_st, g2e_hbm.at[t_l, :, dst_full])),
-            (~early & (j == 1), copy(2, g2s_st.at[:, src_half], g2e_hbm.at[t_l, :, dst_half])),
-            (~early, copy(3, g2_st, g2l_hbm.at[t_l, :, cols(fb)])),
-        ]
-
     def far_copy(axis, src, dst):
         return pltpu.make_async_remote_copy(
             src_ref=src, dst_ref=dst, send_sem=far_send.at[axis], recv_sem=far_recv.at[axis],
             device_id=y_far if axis % 2 else x_far, device_id_type=MESH)
 
-    def send_far(t, j):
-        early, is_far, fb = t < n_early, j < n_half, block_at(j, n_half, x_pos, y_pos)
-        t_l = jnp.maximum(t - n_early, 0)
-        in_half = cols(lax.rem(fb, n_half))
-        half = pl.ds(pl.multiple_of(x_pos * F_BLOCK, half_b), half_b)
-        full = pl.ds(pl.multiple_of((1 - x_pos) * half_b, half_b), F_BLOCK)
-
-        @pl.when(early)
+    own_rows = pl.ds(pl.multiple_of(x_pos * half_d, 16), half_d)
+    pass_rows = pl.ds(pl.multiple_of((1 - y_pos) * quarter_d, 16), quarter_d)
+    cut_half = pl.ds(pl.multiple_of((1 - x_pos) * half_b, half_b), half_b)
+    to_half = pl.ds(pl.multiple_of(x_pos * F_BLOCK, half_b), half_b)
+    to_full = pl.ds(pl.multiple_of((1 - x_pos) * half_b, half_b), F_BLOCK)
+
+    def block(act, t, j):
+        far_k = x_pos * j + (1 - x_pos) * (n_half - 1 - j)
+        far_at, own_at = cols(far_k), cols(j - n_half)
+        fb_at = cols(block_at(j, n_half, x_pos, y_pos))
+
+        def local(n, src, dst):
+            cp = pltpu.make_async_copy(src, dst, out_sem.at[n])
+            (cp.start if act == 'start' else cp.wait)()
+
+        def far(axis, src, dst):
+            if act == 'end':
+                far_copy(axis, src, dst).start()
+
+        @pl.when(t < n_early)
         def _():
-            far_copy(0, g1s_hbm.at[t, :, cols(fb)], g1r_hbm.at[t, :, cols(fb)]).start()
-
-        @pl.when(early & is_far)
+            local(0, g1_st.at[own_rows, :], g1k_hbm.at[t, :, fb_at])
+            local(1, g1s_st, g1s_hbm.at[t, :, fb_at])
+            far(0, g1s_hbm.at[t, :, fb_at], g1r_hbm.at[t, :, fb_at])
+
+            @pl.when(j < n_half)
+            def _():
+                local(2, g2s_st, g2s_hbm.at[t, :, far_at])
+                far(1, g2s_hbm.at[t, :, far_at], g2r_hbm.at[t, :, far_at])
+
+            @pl.when(j >= n_half)
+            def _():
+                local(3, g2_st, g2k_hbm.at[t, :, own_at])
+
+        @pl.when(t >= n_early)
         def _():
-            far_copy(1, g2s_hbm.at[t, :, in_half], g2r_hbm.at[t, :, in_half]).start()
-
-        @pl.when(~early)
-        def _():
-            far_copy(2, g1e_hbm.at[t_l, :, cols(fb)], g1er_hbm.at[t_l, :, cols(fb)]).start()
-
-        @pl.when(~early & (j == 0))
-        def _():
-            far_copy(3, g2e_hbm.at[t_l, :, full], g2er_hbm.at[t_l, :, full]).start()
-
-        @pl.when(~early & (j == 1))
-        def _():
-            far_copy(3, g2e_hbm.at[t_l, :, half], g2er_hbm.at[t_l, :, half]).start()
-
-    def finish_block(t, j):
-        for cond, cp in out_copies(t, j):
-            pl.when(cond)(cp.wait)
-        send_far(t, j)
+            ex = t - n_early
+            local(1, g1s_st.at[pass_rows, :], g1e_hbm.at[ex, :, fb_at])
+            far(2, g1e_hbm.at[ex, :, fb_at], g1er_hbm.at[ex, :, fb_at])
+            local(0, g1_st, g1l_hbm.at[ex, :, fb_at])
+            local(3, g2_st, g2l_hbm.at[ex, :, fb_at])
+
+            @pl.when(j == 0)
+            def _():
+                local(2, g2s_st, g2e_hbm.at[ex, :, to_full])
+                far(3, g2e_hbm.at[ex, :, to_full], g2er_hbm.at[ex, :, to_full])
+
+            @pl.when(j == 1)
+            def _():
+                local(2, g2s_st.at[:, cut_half], g2e_hbm.at[ex, :, to_half])
+                far(3, g2e_hbm.at[ex, :, to_half], g2er_hbm.at[ex, :, to_half])
 
     @pl.when((task > 0) | (step > 0))
     def _():
-        finish_block(jnp.where(step > 0, task, task - 1), jnp.where(step > 0, step - 1, n_steps - 1))
+        block('end', jnp.where(step > 0, task, task - 1), jnp.where(step > 0, step - 1, n_steps - 1))
 
     def square(g):
         return jnp.sum((g * g).reshape(g.shape[0] // 8, 8, g.shape[1]), axis=0)
@@ -249,32 +273,25 @@
             g2s_st[at, :] = g.astype(BF16)
             total = total + square(g)
     ss_ref[example] = total
-    for cond, cp in out_copies(task, step):
-        pl.when(cond)(cp.start)
+    block('start', task, step)
 
     @pl.when(ends_early)
     def _():
         dx_out.wait()
         tp_copy(task).start()
 
-    @pl.when((step == n_steps - 1) & (task < n_task - 1))
-    def _():
-        nxt = task + 1
-
-        @pl.when(nxt >= n_ex)
-        def _():
-            tp_copy(nxt - n_ex).wait()
-
-        for c in range(IN_SLOTS - 1):
-            in_start(nxt, c)
-
-    @pl.when((step == n_steps - 1) & (task == n_task - 1))
-    def _():
-        finish_block(task, step)
+    ends_task, ends_all = (step == n_steps - 1) & (task < n_task - 1), (step == n_steps - 1) & (task == n_task - 1)
+    rarely(ends_task & (task + 1 >= n_ex), lambda i: tp_copy(task + 1 - n_ex).wait())
+    rarely(ends_task, lambda c: in_start(task + 1, c), IN_SLOTS - 1)
+
+    def finish(i):
+        block('end', task, step)
         far_copy(0, g1s_hbm, g1r_hbm).wait()
         far_copy(1, g2s_hbm, g2r_hbm).wait()
         far_copy(2, g1e_hbm, g1er_hbm).wait()
         far_copy(3, g2e_hbm, g2er_hbm).wait()
+
+    rarely(ends_all, finish)
 
 
 def run_stack(pre_act, w_in, w_out, block_in, d_out):
@@ -283,23 +300,6 @@
     n_steps = d_ff // F_BLOCK
     half_d, half_f = d_model // 2, d_ff // 2
     n_early = (n_layers - 1) * n_ex
-    top = n_layers - 1
-
-    def fb(j):
-        dp = lax.axis_index('dp')
-        return block_at(j, n_steps // 2, lax.rem(dp, 2), dp // 2)
-
-    def w1_at(t, j):
-        is_last = t // n_early
-        return jnp.maximum(top - t // n_ex, 1), 0, fb((1 - is_last) * j + is_last * (n_steps - 1))
-
-    in_specs = [
-        pl.BlockSpec((1, 1, n_tok, F_BLOCK), lambda t, j: (top - t // n_ex, lax.rem(t, n_ex), 0, fb(j))),
-        pl.BlockSpec((1, d_model, F_BLOCK), w1_at),
-        pl.BlockSpec((1, F_BLOCK, d_model), lambda t, j: (top - t // n_ex, fb(j), 0)),
-        pl.BlockSpec(memory_space=ANY),
-        pl.BlockSpec(memory_space=ANY),
-    ]
     sds = jax.ShapeDtypeStruct
     outs = [
         sds((n_early, n_tok, d_model), BF16), sds((n_early, n_tok, d_model), BF16), sds((n_ex, n_tok, d_model), BF16),
@@ -313,10 +313,12 @@
     out_specs = [pl.BlockSpec(memory_space=ANY)] * (len(outs) - 1) + [pl.BlockSpec((n_ex, 8, F_BLOCK), lambda t, j: (0, 0, 0))]
     vm = pltpu.VMEM
     scratch = [
+        vm((2, n_tok, F_BLOCK), BF16), vm((2, d_model, F_BLOCK), BF16), vm((2, F_BLOCK, d_model), BF16),
         vm((d_model, n_tok), BF16), vm((n_tok, d_model), BF16), vm((d_model, n_tok), BF16),
         vm((n_tok, F_BLOCK), BF16), vm((n_tok, F_BLOCK), BF16), vm((n_tok, d_model), F32),
         *[vm((IN_SLOTS, T_CHUNK, d_model), BF16)] * 4,
         vm((d_model, F_BLOCK), F32), vm((half_d, F_BLOCK), BF16), vm((d_model, F_BLOCK), F32), vm((d_model, F_BLOCK), BF16),
+        pltpu.SemaphoreType.DMA((3, 2)),
         pltpu.SemaphoreType.DMA((4, IN_SLOTS)), pltpu.SemaphoreType.DMA((4,)), pltpu.SemaphoreType.DMA((2,)),
         pltpu.SemaphoreType.DMA((n_early,)), pltpu.SemaphoreType.DMA((n_early,)),
         pltpu.SemaphoreType.DMA((4,)), pltpu.SemaphoreType.DMA((4,)),
@@ -326,7 +328,7 @@
         functools.partial(stack_kernel, n_layers, n_ex, n_steps),
         out_shape=outs,
         grid_spec=pltpu.PrefetchScalarGridSpec(
-            num_scalar_prefetch=0, grid=(n_early + n_ex, n_steps), in_specs=in_specs, out_specs=out_specs, scratch_shapes=scratch),
+            num_scalar_prefetch=0, grid=(n_early + n_ex, n_steps), in_specs=[pl.BlockSpec(memory_space=ANY)] * 5, out_specs=out_specs, scratch_shapes=scratch),
         compiler_params=pltpu.CompilerParams(
             dimension_semantics=('arbitrary', 'arbitrary'), vmem_limit_bytes=VMEM_LIMIT, has_side_effects=True),
         cost_estimate=pl.CostEstimate(
@@ -347,26 +349,33 @@
     lax.fori_loop(0, refs[-1].shape[0] // MIX_ROWS, group, 0)
 
 
-def mix(which, shape, terms, coefs):
+def mix(which, shape, terms, coefs, part, n_parts):
     rows, width = shape
-    block = (rows, width // 4) if which == 0 else (rows // 4, width)
-
-    def spec(k, lead):
+    part_width = width // n_parts
+    block = (rows, width // 4) if which == 0 else (rows // 4, part_width)
+    n_blocks = 4 // n_parts if which == 0 else 4
+
+    def spec(k, v, lead):
+        off = part * n_blocks if which == 0 and v.shape[2] > part_width else 0
         if which == 0:
-            return pl.BlockSpec((1, *block), lambda i, sc: (lead, sc[k], i))
+            return pl.BlockSpec((1, *block), lambda i, sc: (lead, sc[k], i + off))
         return pl.BlockSpec((1, *block), lambda i, sc: (lead, i, sc[k]))
 
+    def place(v, p):
+        return p * n_parts + part if which == 1 and v.shape[2] > part_width else p
+
     out_map = (lambda i, sc: (0, i)) if which == 0 else (lambda i, sc: (i, 0))
-    places = jnp.stack([jnp.asarray(p, jnp.int32) for _, _, p in terms])
+    places = jnp.stack([jnp.asarray(place(v, p), jnp.int32) for v, _, p in terms])
     return pl.pallas_call(
         mix_kernel,
-        out_shape=jax.ShapeDtypeStruct((rows, width), BF16),
+        out_shape=jax.ShapeDtypeStruct((rows, part_width), BF16),
         grid_spec=pltpu.PrefetchScalarGridSpec(
-            num_scalar_prefetch=1, grid=(4,),
-            in_specs=[pl.BlockSpec(memory_space=pltpu.SMEM)] + [spec(k, lead) for k, (_, lead, _) in enumerate(terms)],
+            num_scalar_prefetch=1, grid=(n_blocks,),
+            in_specs=[pl.BlockSpec(memory_space=pltpu.SMEM)] + [spec(k, v, lead) for k, (v, lead, _) in enumerate(terms)],
             out_specs=pl.BlockSpec(block, out_map)),
         compiler_params=pltpu.CompilerParams(dimension_semantics=('arbitrary',), vmem_limit_bytes=40_000_000),
-        cost_estimate=pl.CostEstimate(flops=2 * len(terms) * rows * width, bytes_accessed=14 * rows * width, transcendentals=0),
+        cost_estimate=pl.CostEstimate(
+            flops=2 * len(terms) * rows * part_width, bytes_accessed=14 * rows * part_width, transcendentals=0),
         name='mix',
     )(places, coefs, *[v for v, _, _ in terms])
 
@@ -381,16 +390,18 @@
     out_ref[0, 0] = (piece_ref[...].astype(F32).T + coef_ref[0] * noise_ref[0, 0]) * coef_ref[1]
 
 
-def put_piece(transposed, total, layer, quarter, coef, piece, noise):
+def put_piece(transposed, total, layer, quarter, part, coef, piece, noise):
     if transposed:
         rows, width = piece.shape[1], piece.shape[0]
-        block = 256
+        block = 256 if rows % 256 == 0 else 128
+        first = part * (rows // block)
         piece_spec = pl.BlockSpec((width, block), lambda i, sc: (0, i))
+        big_spec = pl.BlockSpec((1, 1, block, width), lambda i, sc: (sc[0], sc[1], first + i, 0))
     else:
         rows, width = piece.shape
         block = rows // 2
         piece_spec = pl.BlockSpec((block, width), lambda i, sc: (i, 0))
-    big_spec = pl.BlockSpec((1, 1, block, width), lambda i, sc: (sc[0], sc[1], i, 0))
+        big_spec = pl.BlockSpec((1, 1, block, width), lambda i, sc: (sc[0], sc[1], i, part))
     args = [jnp.stack([jnp.int32(layer), quarter]), coef, piece, noise]
     in_specs = [pl.BlockSpec(memory_space=pltpu.SMEM), piece_spec, big_spec]
     aliases = {}
@@ -448,18 +459,18 @@
 
         made = []
 
-        def mixed(which, terms, coefs):
+        def mixed(which, terms, coefs, part, n_parts):
             coefs = jnp.stack([jnp.asarray(c, F32) for c in coefs])
             if made:
                 coefs, _ = lax.optimization_barrier((coefs, made[-1]))
-            made.append(mix(which, shapes[which], terms, coefs))
+            made.append(mix(which, shapes[which], terms, coefs, part, n_parts))
             return made[-1]
 
-        def pair_terms(layer, which, to_send, *more):
+        def pair_terms(layer, which, part, to_send, *more):
             pos = 1 - at_side[which] if to_send else at_side[which]
             terms, coefs = own_terms(layer, which, at_half[which], pos), list(c_own)
             if layer == 0 and not to_send:
-                more = (far_last[which], *more)
+                more = (far_last[part, which], *more)
             else:
                 if layer == 0:
                     terms += [((g1er, g2er)[which], k, 0) for k in range(local_batch)]
@@ -470,30 +481,37 @@
             terms += [(v[None], 0, 0) for v in more]
             return terms, coefs + [1.0] * len(more)
 
+        last = [(0, part, 2) for part in range(2)]
+        turns = [(layer, 0, 1) for layer in range(n_layers - 1, 0, -1)] + last
         got, far_last, places = {}, {}, {}
-        for which in (0, 1):
-            far_last[which] = over_half[which](
-                mixed(which, own_terms(0, which, 1 - at_half[which], at_side[which]), c_own))
-        for layer in range(n_layers - 1, -1, -1):
+        for _, part, n_parts in last:
             for which in (0, 1):
-                got[layer, which] = over_side[which](mixed(which, *pair_terms(layer, which, True)))
-        for layer in range(n_layers - 1, -1, -1):
+                terms = own_terms(0, which, 1 - at_half[which], at_side[which])
+                far_last[part, which] = over_half[which](mixed(which, terms, c_own, part, n_parts))
+        for layer, part, n_parts in turns:
+            for which in (0, 1):
+                value = mixed(which, *pair_terms(layer, which, part, True), part, n_parts)
+                got[layer, part, which] = over_side[which](value)
+        n_first = len(made)
+        for layer, part, n_parts in turns:
             for which in (0, 1):
                 half_pos, pos = at_half[which], at_side[which]
-                own = mixed(which, *pair_terms(layer, which, False, got[layer, which]))
+                own = mixed(which, *pair_terms(layer, which, part, False, got[layer, part, which]), part, n_parts)
                 near = over_side[which](own)
                 side = over_half[which](own)
                 diag = over_half[which](near)
-                places[layer, which] = (
+                places[layer, part, which] = (
                     (2 * half_pos + pos, own), (2 * half_pos + 1 - pos, near),
                     (2 * (1 - half_pos) + pos, side), (2 * (1 - half_pos) + 1 - pos, diag))
-        grads, noises = [None, None], (noise_in4, noise_out4)
+        grads, noises, n_put = [None, None], (noise_in4, noise_out4), 0
         for kind in range(4):
-            for layer in range(n_layers - 1, -1, -1):
+            for layer, part, _ in turns:
                 for which in (0, 1):
-                    at, piece = places[layer, which][kind]
-                    grads[which] = put_piece(which == 1, grads[which], layer, at, coef, piece, noises[which])
+                    at, piece = places[layer, part, which][kind]
+                    grads[which] = put_piece(which == 1, grads[which], layer, at, part, coef, piece, noises[which])
+                    n_put += 1
         grad_in, grad_out = grads
+        assert (len(made), n_first, n_put) == (N_SUM, N_FIRST, N_PUT)
         return grad_in.reshape(n_layers, d_model, d_ff), grad_out.reshape(n_layers, d_ff, d_model)
 
     return jax.shard_map(

time: 1220 us -> 1340 us (1.098)
  waiting for transfers between devices: 416 us -> 484 us
  Pallas kernels: 756 us -> 780 us
    ppermute x14 -> x19, waiting for transfers between devices: 254 us -> 370 us  [local_step(): over_y = lambda v: lax.ppermute(v, 'dp', swap_y)]
    ppermute x14 -> x19, waiting for transfers between devices: 162 us -> 114 us  [local_step(): over_x = lambda v: lax.ppermute(v, 'dp', swap_x)]
    pallas_call x24 -> x32, Pallas kernels: 137 us -> 156 us  [put_piece(): pl.pallas_call(put_out_kernel if transposed else put_in_kernel, out_shape...]
    pallas_call x14 -> x20, Pallas kernels: 98.8 us -> 111 us  [mix(): pl.pallas_call(mix_kernel, out_shape=jax.ShapeDtypeStruct((rows, part_wid...]
  transfers between devices with their start and end apart: 28 -> 38, of which waited for: 14 -> 15; matrix products, arithmetic and copies ran while one was open for 0% -> 0% of each run, Pallas kernels for 18% -> 19%
where the time goes in v7:
time: 1340 us
  Pallas kernels  780 us (58%)
  waiting for transfers between devices  484 us (36%)
  starting transfers between devices  43.8 us (3%)
  local copies, waits for them, and re-layouts  20.8 us (2%)
    pallas_call x1, Pallas kernels, run_stack(): pl.pallas_call(functools.partial(stack_kernel, n_layers, n_ex, n_steps),...  513 us
    ppermute x19, waiting for transfers between devices, local_step(): over_y = lambda v: lax.ppermute(v, 'dp', swap_y)  370 us
    pallas_call x32, Pallas kernels, put_piece(): pl.pallas_call(put_out_kernel if transposed else put_in_kernel, out_shape...  156 us
    ppermute x19, waiting for transfers between devices, local_step(): over_x = lambda v: lax.ppermute(v, 'dp', swap_x)  114 us
    pallas_call x20, Pallas kernels, mix(): pl.pallas_call(mix_kernel, out_shape=jax.ShapeDtypeStruct((rows, part_wid...  111 us
  transfers between devices with their start and end apart: 38, of which 15 were waited for; matrix products, arithmetic and copies ran while one was open for 0% of the time, Pallas kernels for 19%

profile of v7, /device:TPU:0, one launch (start us, length us, event | category | flops | bytes accessed | tf_op | source)
XLA Modules:
  0.0 1336.1 jit_solution(17327251295358825038)
XLA Ops:
  0.6 512.8 %stack.352 = (bf16[4,2048,1408]{2,1,0:T(8,128)(2,1)}, bf16[4,2048,1408]{2,1,0:T(8,128)(2,1)}, bf16[2,2048,1408]{2,1,0:T(8,128)(2,1)}, f32[4,704,3072]{2,1,0:T(8,...) custom-call(bf16[3,2,2048,3072]{3,2,1,0:T(8,128)(2,1)} %u_hbm.1, ...), custom_call_target="tpu_custom_call" | custom-call | flops 389768282112 | bytes 500000000 | tf_op jit(solution)/shard_map/stack/pallas_call | solution.py:327
  521.9 4.8 mix.21
  534.3 4.8 mix.23
  539.1 13.6 %collective-permute-done = f32[2]{0:T(128)S(1)} collective-permute-done((f32[2]{0:T(128)S(1)}, f32[2]{0:T(128)S(1)}, u32[]{:S(2)}, u32[]{:S(2)}) %collective-permute-start) | collective-permute-done | bytes 40 | tf_op jit(solution)/shard_map/ppermute | solution.py:436
  552.7 7.6 mix.24
  561.9 7.5 mix.25
  570.8 7.5 mix.26
  579.0 7.5 mix.27
  594.2 5.0 mix.29
  599.3 78.8 %collective-permute-done.7 = bf16[352,1536]{1,0:T(8,128)(2,1)S(1)} collective-permute-done((bf16[352,1536]{1,0:T(8,128)(2,1)S(1)}, bf16[352,1536]{1,0:T(8,128)(2,1)S(1)}, u32[]{:S(2)}, u32[]{:S(2)}) %collective-permute-start.7) | collective-permute-done | bytes 1081376 | tf_op jit(solution)/shard_map/ppermute | solution.py:436
  689.4 5.0 mix.31
  699.9 7.3 mix.32.piece_ref
  707.3 6.6 mix.33.piece_ref
  713.9 8.4 mix.34.piece_ref
  722.3 7.1 mix.35.piece_ref
  738.2 4.9 collective-permute-done.11
  747.1 5.4 collective-permute-done.25
  763.0 12.5 collective-permute-done.28.piece_ref
  777.1 18.9 %collective-permute-done.26.piece_ref = bf16[1408,384]{1,0:T(8,128)(2,1)} collective-permute-done((bf16[1408,384]{1,0:T(8,128)(2,1)S(1)}, bf16[1408,384]{1,0:T(8,128)(2,1)}, u32[]{:S(2)}, u32[]{:S(2)}) %collective-permute-start.26) | collective-permute-done | bytes 1081376 | tf_op jit(solution)/shard_map/ppermute | solution.py:435
  799.0 9.5 collective-permute-done.34.piece_ref
  809.9 21.9 %collective-permute-done.14.piece_ref = bf16[352,1536]{1,0:T(8,128)(2,1)} collective-permute-done((bf16[352,1536]{1,0:T(8,128)(2,1)S(1)}, bf16[352,1536]{1,0:T(8,128)(2,1)}, u32[]{:S(2)}, u32[]{:S(2)}) %collective-permute-start.14) | collective-permute-done | bytes 1081376 | tf_op jit(solution)/shard_map/ppermute | solution.py:436
  833.2 21.8 %collective-permute-done.12.piece_ref = bf16[352,1536]{1,0:T(8,128)(2,1)} collective-permute-done((bf16[352,1536]{1,0:T(8,128)(2,1)S(1)}, bf16[352,1536]{1,0:T(8,128)(2,1)}, u32[]{:S(2)}, u32[]{:S(2)}) %collective-permute-start.12) | collective-permute-done | bytes 1081376 | tf_op jit(solution)/shard_map/ppermute | solution.py:436
  855.3 60.1 %collective-permute-done.21.piece_ref = bf16[352,1536]{1,0:T(8,128)(2,1)S(1)} collective-permute-done((bf16[352,1536]{1,0:T(8,128)(2,1)S(1)}, bf16[352,1536]{1,0:T(8,128)(2,1)S(1)}, u32[]{:S(2)}, u32[]{:S(2)}) %collective-permute-start.21) | collective-permute-done | bytes 1081376 | tf_op jit(solution)/shard_map/ppermute | solution.py:435
  918.0 17.0 %collective-permute-done.20.piece_ref = bf16[352,1536]{1,0:T(8,128)(2,1)S(1)} collective-permute-done((bf16[352,1536]{1,0:T(8,128)(2,1)S(1)}, bf16[352,1536]{1,0:T(8,128)(2,1)S(1)}, u32[]{:S(2)}, u32[]{:S(2)}) %collective-permute-start.20) | collective-permute-done | bytes 1081376 | tf_op jit(solution)/shard_map/ppermute | solution.py:435
  943.4 22.9 %collective-permute-done.36.piece_ref = bf16[1408,768]{1,0:T(8,128)(2,1)S(1)} collective-permute-done((bf16[1408,768]{1,0:T(8,128)(2,1)S(1)}, bf16[1408,768]{1,0:T(8,128)(2,1)S(1)}, u32[]{:S(2)}, u32[]{:S(2)}) %collective-permute-start.36) | collective-permute-done | bytes 2162720 | tf_op jit(solution)/shard_map/ppermute | solution.py:436
  969.4 108.9 %collective-permute-done.29.piece_ref = bf16[1408,384]{1,0:T(8,128)(2,1)S(1)} collective-permute-done((bf16[1408,384]{1,0:T(8,128)(2,1)S(1)}, bf16[1408,384]{1,0:T(8,128)(2,1)S(1)}, u32[]{:S(2)}, u32[]{:S(2)}) %collective-permute-start.29) | collective-permute-done | bytes 1081376 | tf_op jit(solution)/shard_map/ppermute | solution.py:436
  1086.7 42.8 %collective-permute-done.33.piece_ref = bf16[1408,768]{1,0:T(8,128)(2,1)} collective-permute-done((bf16[1408,768]{1,0:T(8,128)(2,1)}, bf16[1408,768]{1,0:T(8,128)(2,1)}, u32[]{:S(2)}, u32[]{:S(2)}) %collective-permute-start.33) | collective-permute-done | bytes 2162720 | tf_op jit(solution)/shard_map/ppermute | solution.py:436
  1131.1 44.7 %collective-permute-done.31.piece_ref = bf16[1408,768]{1,0:T(8,128)(2,1)} collective-permute-done((bf16[1408,768]{1,0:T(8,128)(2,1)}, bf16[1408,768]{1,0:T(8,128)(2,1)}, u32[]{:S(2)}, u32[]{:S(2)}) %collective-permute-start.31) | collective-permute-done | bytes 2162720 | tf_op jit(solution)/shard_map/ppermute | solution.py:436
  1179.8 6.1 put_out.16.rest_0_
  1185.9 6.1 put_out.17.rest_0_
  1196.6 4.6 put_out.19.rest_0_
  1205.8 5.1 put_in.17.rest_0_
  1217.5 6.6 put_out.20.rest_0_
  1224.0 6.6 put_out.21.rest_0_
  1230.6 4.6 put_out.22.rest_0_
  1235.2 4.8 put_out.23.rest_0_
  1240.0 5.1 put_in.20.rest_0_
  1245.2 5.1 put_in.21.rest_0_
  1257.6 6.1 put_out.24.rest_0_
  1263.7 6.1 put_out.25.rest_0_
  1274.4 4.6 put_out.27.rest_0_
  1279.0 5.1 put_in.24.rest_0_
  1284.1 5.1 put_in.25.rest_0_
  1296.1 6.6 put_out.28.rest_0_
  1302.6 6.6 put_out.29.rest_0_
  1313.8 4.8 put_out.31
  1318.6 5.1 put_in.28.rest_0_
  1323.7 5.1 put_in.29.rest_0_
  (205 shorter events, 148.5 us)
Async XLA Ops:
  517.5 35.1 %copy-start.33 = (f32[2]{0:T(128)}, f32[2]{0:T(128)S(1)}, u32[]{:S(2)}) copy-start(f32[2]{0:T(128)S(1)} %multiply_minimum_fusion.coef_ref) | copy-start | bytes 28
  521.4 65.0 %collective-permute-start.6 = (bf16[352,1536]{1,0:T(8,128)(2,1)}, bf16[352,1536]{1,0:T(8,128)(2,1)}, u32[]{:S(2)}, u32[]{:S(2)}) collective-permute-start(bf16[352,1536]{1,0:T(8,128)(2,1)} %mix.20), channel_id=1, source_target_pairs={{0,2},{2,0},{4,6},{6,4},{1,3},{3,1},{5,7},{7,5}} | collective-permute-start | bytes 3244040 | tf_op jit(solution)/shard_map/ppermute | solution.py:435
  526.7 65.9 %collective-permute-start.8 = (bf16[1408,384]{1,0:T(8,128)(2,1)}, bf16[1408,384]{1,0:T(8,128)(2,1)}, u32[]{:S(2)}, u32[]{:S(2)}) collective-permute-start(bf16[1408,384]{1,0:T(8,128)(2,1)} %mix.21), channel_id=1, source_target_pairs={{0,4},{2,6},{4,0},{6,2},{1,5},{3,7},{5,1},{7,3}} | collective-permute-start | bytes 3244040 | tf_op jit(solution)/shard_map/ppermute | solution.py:436
  528.3 24.3 %collective-permute-start = (f32[2]{0:T(128)S(1)}, f32[2]{0:T(128)S(1)}, u32[]{:S(2)}, u32[]{:S(2)}) collective-permute-start(f32[2]{0:T(128)S(1)} %multiply_minimum_fusion.coef_ref), channel_id=1, source_target_pairs={{0,4},{2,6},{4,0},{6,2},{1,5},{3,7},{5,1},{7,3}} | collective-permute-start | bytes 32 | tf_op jit(solution)/shard_map/ppermute | solution.py:436
  528.7 24.0 %collective-permute-start.1 = (f32[2]{0:T(128)S(1)}, f32[2]{0:T(128)S(1)}, u32[]{:S(2)}, u32[]{:S(2)}) collective-permute-start(f32[2]{0:T(128)S(1)} %multiply_minimum_fusion.coef_ref), channel_id=1, source_target_pairs={{0,2},{2,0},{4,6},{6,4},{1,3},{3,1},{5,7},{7,5}} | collective-permute-start | bytes 32 | tf_op jit(solution)/shard_map/ppermute | solution.py:435
  552.6 7.7 copy-start.35
  552.7 7.7 copy-start.37
  560.3 134.1 %collective-permute-start.2 = (bf16[352,3072]{1,0:T(8,128)(2,1)}, bf16[352,3072]{1,0:T(8,128)(2,1)}, u32[]{:S(2)}, u32[]{:S(2)}) collective-permute-start(bf16[352,3072]{1,0:T(8,128)(2,1)} %mix.24), channel_id=1, source_target_pairs={{0,4},{2,6},{4,0},{6,2},{1,5},{3,7},{5,1},{7,3}} | collective-permute-start | bytes 6488072 | tf_op jit(solution)/shard_map/ppermute | solution.py:436
  569.4 125.5 %collective-permute-start.3 = (bf16[1408,768]{1,0:T(8,128)(2,1)}, bf16[1408,768]{1,0:T(8,128)(2,1)S(1)}, u32[]{:S(2)}, u32[]{:S(2)}) collective-permute-start(bf16[1408,768]{1,0:T(8,128)(2,1)} %mix.25), channel_id=1, source_target_pairs={{0,2},{2,0},{4,6},{6,4},{1,3},{3,1},{5,7},{7,5}} | collective-permute-start | bytes 6488072 | tf_op jit(solution)/shard_map/ppermute | solution.py:435
  578.3 119.5 %collective-permute-start.4 = (bf16[352,3072]{1,0:T(8,128)(2,1)}, bf16[352,3072]{1,0:T(8,128)(2,1)}, u32[]{:S(2)}, u32[]{:S(2)}) collective-permute-start(bf16[352,3072]{1,0:T(8,128)(2,1)} %mix.26), channel_id=1, source_target_pairs={{0,4},{2,6},{4,0},{6,2},{1,5},{3,7},{5,1},{7,3}} | collective-permute-start | bytes 6488072 | tf_op jit(solution)/shard_map/ppermute | solution.py:436
  586.4 111.8 %collective-permute-start.5 = (bf16[1408,768]{1,0:T(8,128)(2,1)}, bf16[1408,768]{1,0:T(8,128)(2,1)}, u32[]{:S(2)}, u32[]{:S(2)}) collective-permute-start(bf16[1408,768]{1,0:T(8,128)(2,1)} %mix.27), channel_id=1, source_target_pairs={{0,2},{2,0},{4,6},{6,4},{1,3},{3,1},{5,7},{7,5}} | collective-permute-start | bytes 6488072 | tf_op jit(solution)/shard_map/ppermute | solution.py:435
  592.6 85.4 %collective-permute-start.7 = (bf16[352,1536]{1,0:T(8,128)(2,1)S(1)}, bf16[352,1536]{1,0:T(8,128)(2,1)S(1)}, u32[]{:S(2)}, u32[]{:S(2)}) collective-permute-start(bf16[352,1536]{1,0:T(8,128)(2,1)S(1)} %mix.28), channel_id=1, source_target_pairs={{0,4},{2,6},{4,0},{6,2},{1,5},{3,7},{5,1},{7,3}} | collective-permute-start | bytes 3244040 | tf_op jit(solution)/shard_map/ppermute | solution.py:436
  679.0 54.2 %collective-permute-start.9 = (bf16[1408,384]{1,0:T(8,128)(2,1)}, bf16[1408,384]{1,0:T(8,128)(2,1)}, u32[]{:S(2)}, u32[]{:S(2)}) collective-permute-start(bf16[1408,384]{1,0:T(8,128)(2,1)} %mix.29), channel_id=1, source_target_pairs={{0,2},{2,0},{4,6},{6,4},{1,3},{3,1},{5,7},{7,5}} | collective-permute-start | bytes 3244040 | tf_op jit(solution)/shard_map/ppermute | solution.py:435
  689.4 10.4 copy-start.34
  689.4 10.4 copy-start.36
  689.4 10.4 copy-start.38
  694.5 43.8 %collective-permute-start.10 = (bf16[352,1536]{1,0:T(8,128)(2,1)}, bf16[352,1536]{1,0:T(8,128)(2,1)}, u32[]{:S(2)}, u32[]{:S(2)}) collective-permute-start(bf16[352,1536]{1,0:T(8,128)(2,1)} %mix.22), channel_id=1, source_target_pairs={{0,2},{2,0},{4,6},{6,4},{1,3},{3,1},{5,7},{7,5}} | collective-permute-start | bytes 3244040 | tf_op jit(solution)/shard_map/ppermute | solution.py:435
  696.2 50.9 %collective-permute-start.24 = (bf16[1408,384]{1,0:T(8,128)(2,1)}, bf16[1408,384]{1,0:T(8,128)(2,1)}, u32[]{:S(2)}, u32[]{:S(2)}) collective-permute-start(bf16[1408,384]{1,0:T(8,128)(2,1)} %mix.23), channel_id=1, source_target_pairs={{0,4},{2,6},{4,0},{6,2},{1,5},{3,7},{5,1},{7,3}} | collective-permute-start | bytes 3244040 | tf_op jit(solution)/shard_map/ppermute | solution.py:436
  697.8 45.3 %collective-permute-start.11 = (bf16[352,1536]{1,0:T(8,128)(2,1)}, bf16[352,1536]{1,0:T(8,128)(2,1)}, u32[]{:S(2)}, u32[]{:S(2)}) collective-permute-start(bf16[352,1536]{1,0:T(8,128)(2,1)} %mix.30), channel_id=1, source_target_pairs={{0,4},{2,6},{4,0},{6,2},{1,5},{3,7},{5,1},{7,3}} | collective-permute-start | bytes 3244040 | tf_op jit(solution)/shard_map/ppermute | solution.py:436
  698.2 54.2 %collective-permute-start.25 = (bf16[1408,384]{1,0:T(8,128)(2,1)}, bf16[1408,384]{1,0:T(8,128)(2,1)}, u32[]{:S(2)}, u32[]{:S(2)}) collective-permute-start(bf16[1408,384]{1,0:T(8,128)(2,1)} %mix.31), channel_id=1, source_target_pairs={{0,2},{2,0},{4,6},{6,4},{1,3},{3,1},{5,7},{7,5}} | collective-permute-start | bytes 3244040 | tf_op jit(solution)/shard_map/ppermute | solution.py:435
  713.9 117.9 %copy-start.3 = (bf16[1408,768]{1,0:T(8,128)(2,1)}, bf16[1408,768]{1,0:T(8,128)(2,1)S(1)}, u32[]{:S(2)}) copy-start(bf16[1408,768]{1,0:T(8,128)(2,1)S(1)} %mix.33.piece_ref) | copy-start | bytes 6488068
  729.4 186.0 %copy-start.5 = (bf16[1408,768]{1,0:T(8,128)(2,1)}, bf16[1408,768]{1,0:T(8,128)(2,1)S(1)}, u32[]{:S(2)}) copy-start(bf16[1408,768]{1,0:T(8,128)(2,1)S(1)} %mix.35.piece_ref) | copy-start | bytes 6488068
  733.2 75.3 %copy-start.7 = (bf16[352,1536]{1,0:T(8,128)(2,1)}, bf16[352,1536]{1,0:T(8,128)(2,1)S(1)}, u32[]{:S(2)}) copy-start(bf16[352,1536]{1,0:T(8,128)(2,1)S(1)} %mix.36.piece_ref) | copy-start | bytes 3244036
  737.7 37.8 %collective-permute-start.28 = (bf16[1408,384]{1,0:T(8,128)(2,1)S(1)}, bf16[1408,384]{1,0:T(8,128)(2,1)S(1)}, u32[]{:S(2)}, u32[]{:S(2)}) collective-permute-start(bf16[1408,384]{1,0:T(8,128)(2,1)S(1)} %mix.37.piece_ref), channel_id=1, source_target_pairs={{0,2},{2,0},{4,6},{6,4},{1,3},{3,1},{5,7},{7,5}} | collective-permute-start | bytes 3244040 | tf_op jit(solution)/shard_map/ppermute | solution.py:435
  747.0 107.9 %copy-start.9 = (bf16[352,1536]{1,0:T(8,128)(2,1)}, bf16[352,1536]{1,0:T(8,128)(2,1)S(1)}, u32[]{:S(2)}) copy-start(bf16[352,1536]{1,0:T(8,128)(2,1)S(1)} %mix.38.piece_ref) | copy-start | bytes 3244036
  756.9 39.0 %collective-permute-start.26 = (bf16[1408,384]{1,0:T(8,128)(2,1)S(1)}, bf16[1408,384]{1,0:T(8,128)(2,1)}, u32[]{:S(2)}, u32[]{:S(2)}) collective-permute-start(bf16[1408,384]{1,0:T(8,128)(2,1)S(1)} %mix.39.piece_ref), channel_id=1, source_target_pairs={{0,2},{2,0},{4,6},{6,4},{1,3},{3,1},{5,7},{7,5}} | collective-permute-start | bytes 3244040 | tf_op jit(solution)/shard_map/ppermute | solution.py:435
  758.6 39.0 %collective-permute-start.35 = (bf16[1408,384]{1,0:T(8,128)(2,1)S(1)}, bf16[1408,384]{1,0:T(8,128)(2,1)S(1)}, u32[]{:S(2)}, u32[]{:S(2)}) collective-permute-start(bf16[1408,384]{1,0:T(8,128)(2,1)S(1)} %mix.37.piece_ref), channel_id=1, source_target_pairs={{0,4},{2,6},{4,0},{6,2},{1,5},{3,7},{5,1},{7,3}} | collective-permute-start | bytes 3244040 | tf_op jit(solution)/shard_map/ppermute | solution.py:436
  760.0 48.5 %collective-permute-start.34 = (bf16[1408,384]{1,0:T(8,128)(2,1)S(1)}, bf16[1408,384]{1,0:T(8,128)(2,1)S(1)}, u32[]{:S(2)}, u32[]{:S(2)}) collective-permute-start(bf16[1408,384]{1,0:T(8,128)(2,1)S(1)} %mix.39.piece_ref), channel_id=1, source_target_pairs={{0,4},{2,6},{4,0},{6,2},{1,5},{3,7},{5,1},{7,3}} | collective-permute-start | bytes 3244040 | tf_op jit(solution)/shard_map/ppermute | solution.py:436
  761.6 70.2 %collective-permute-start.14 = (bf16[352,1536]{1,0:T(8,128)(2,1)S(1)}, bf16[352,1536]{1,0:T(8,128)(2,1)}, u32[]{:S(2)}, u32[]{:S(2)}) collective-permute-start(bf16[352,1536]{1,0:T(8,128)(2,1)S(1)} %mix.36.piece_ref), channel_id=1, source_target_pairs={{0,4},{2,6},{4,0},{6,2},{1,5},{3,7},{5,1},{7,3}} | collective-permute-start | bytes 3244040 | tf_op jit(solution)/shard_map/ppermute | solution.py:436
  775.5 79.5 %collective-permute-start.12 = (bf16[352,1536]{1,0:T(8,128)(2,1)S(1)}, bf16[352,1536]{1,0:T(8,128)(2,1)}, u32[]{:S(2)}, u32[]{:S(2)}) collective-permute-start(bf16[352,1536]{1,0:T(8,128)(2,1)S(1)} %mix.38.piece_ref), channel_id=1, source_target_pairs={{0,4},{2,6},{4,0},{6,2},{1,5},{3,7},{5,1},{7,3}} | collective-permute-start | bytes 3244040 | tf_op jit(solution)/shard_map/ppermute | solution.py:436
  796.0 141.5 %collective-permute-start.32 = (bf16[1408,768]{1,0:T(8,128)(2,1)S(1)}, bf16[1408,768]{1,0:T(8,128)(2,1)}, u32[]{:S(2)}, u32[]{:S(2)}) collective-permute-start(bf16[1408,768]{1,0:T(8,128)(2,1)S(1)} %mix.33.piece_ref), channel_id=1, source_target_pairs={{0,2},{2,0},{4,6},{6,4},{1,3},{3,1},{5,7},{7,5}} | collective-permute-start | bytes 6488072 | tf_op jit(solution)/shard_map/ppermute | solution.py:435
  798.6 139.4 %collective-permute-start.30 = (bf16[1408,768]{1,0:T(8,128)(2,1)S(1)}, bf16[1408,768]{1,0:T(8,128)(2,1)}, u32[]{:S(2)}, u32[]{:S(2)}) collective-permute-start(bf16[1408,768]{1,0:T(8,128)(2,1)S(1)} %mix.35.piece_ref), channel_id=1, source_target_pairs={{0,2},{2,0},{4,6},{6,4},{1,3},{3,1},{5,7},{7,5}} | collective-permute-start | bytes 6488072 | tf_op jit(solution)/shard_map/ppermute | solution.py:435
  809.5 105.9 %collective-permute-start.21 = (bf16[352,1536]{1,0:T(8,128)(2,1)S(1)}, bf16[352,1536]{1,0:T(8,128)(2,1)S(1)}, u32[]{:S(2)}, u32[]{:S(2)}) collective-permute-start(bf16[352,1536]{1,0:T(8,128)(2,1)S(1)} %mix.36.piece_ref), channel_id=1, source_target_pairs={{0,2},{2,0},{4,6},{6,4},{1,3},{3,1},{5,7},{7,5}} | collective-permute-start | bytes 3244040 | tf_op jit(solution)/shard_map/ppermute | solution.py:435
  831.8 107.8 %collective-permute-start.37 = (bf16[1408,768]{1,0:T(8,128)(2,1)S(1)}, bf16[1408,768]{1,0:T(8,128)(2,1)S(1)}, u32[]{:S(2)}, u32[]{:S(2)}) collective-permute-start(bf16[1408,768]{1,0:T(8,128)(2,1)S(1)} %mix.33.piece_ref), channel_id=1, source_target_pairs={{0,4},{2,6},{4,0},{6,2},{1,5},{3,7},{5,1},{7,3}} | collective-permute-start | bytes 6488072 | tf_op jit(solution)/shard_map/ppermute | solution.py:436
  855.0 80.0 %collective-permute-start.20 = (bf16[352,1536]{1,0:T(8,128)(2,1)S(1)}, bf16[352,1536]{1,0:T(8,128)(2,1)S(1)}, u32[]{:S(2)}, u32[]{:S(2)}) collective-permute-start(bf16[352,1536]{1,0:T(8,128)(2,1)S(1)} %mix.38.piece_ref), channel_id=1, source_target_pairs={{0,2},{2,0},{4,6},{6,4},{1,3},{3,1},{5,7},{7,5}} | collective-permute-start | bytes 3244040 | tf_op jit(solution)/shard_map/ppermute | solution.py:435
  916.4 49.9 %collective-permute-start.36 = (bf16[1408,768]{1,0:T(8,128)(2,1)S(1)}, bf16[1408,768]{1,0:T(8,128)(2,1)S(1)}, u32[]{:S(2)}, u32[]{:S(2)}) collective-permute-start(bf16[1408,768]{1,0:T(8,128)(2,1)S(1)} %mix.35.piece_ref), channel_id=1, source_target_pairs={{0,4},{2,6},{4,0},{6,2},{1,5},{3,7},{5,1},{7,3}} | collective-permute-start | bytes 6488072 | tf_op jit(solution)/shard_map/ppermute | solution.py:436
  935.9 144.9 %collective-permute-start.18 = (bf16[352,3072]{1,0:T(8,128)(2,1)S(1)}, bf16[352,3072]{1,0:T(8,128)(2,1)}, u32[]{:S(2)}, u32[]{:S(2)}) collective-permute-start(bf16[352,3072]{1,0:T(8,128)(2,1)S(1)} %mix.32.piece_ref), channel_id=1, source_target_pairs={{0,4},{2,6},{4,0},{6,2},{1,5},{3,7},{5,1},{7,3}} | collective-permute-start | bytes 6488072 | tf_op jit(solution)/shard_map/ppermute | solution.py:436
  937.5 144.2 %collective-permute-start.16 = (bf16[352,3072]{1,0:T(8,128)(2,1)}, bf16[352,3072]{1,0:T(8,128)(2,1)}, u32[]{:S(2)}, u32[]{:S(2)}) collective-permute-start(bf16[352,3072]{1,0:T(8,128)(2,1)} %mix.34.piece_ref), channel_id=1, source_target_pairs={{0,4},{2,6},{4,0},{6,2},{1,5},{3,7},{5,1},{7,3}} | collective-permute-start | bytes 6488072 | tf_op jit(solution)/shard_map/ppermute | solution.py:436
  938.0 145.3 %collective-permute-start.23 = (bf16[352,3072]{1,0:T(8,128)(2,1)S(1)}, bf16[352,3072]{1,0:T(8,128)(2,1)}, u32[]{:S(2)}, u32[]{:S(2)}) collective-permute-start(bf16[352,3072]{1,0:T(8,128)(2,1)S(1)} %mix.32.piece_ref), channel_id=1, source_target_pairs={{0,2},{2,0},{4,6},{6,4},{1,3},{3,1},{5,7},{7,5}} | collective-permute-start | bytes 6488072 | tf_op jit(solution)/shard_map/ppermute | solution.py:435
  941.0 137.3 %collective-permute-start.29 = (bf16[1408,384]{1,0:T(8,128)(2,1)S(1)}, bf16[1408,384]{1,0:T(8,128)(2,1)S(1)}, u32[]{:S(2)}, u32[]{:S(2)}) collective-permute-start(bf16[1408,384]{1,0:T(8,128)(2,1)S(1)} %collective-permute-done.28.piece_ref), channel_id=1, source_target_pairs={{0,4},{2,6},{4,0},{6,2},{1,5},{3,7},{5,1},{7,3}} | collective-permute-start | bytes 3244040 | tf_op jit(solution)/shard_map/ppermute | solution.py:436
  967.7 117.4 %collective-permute-start.22 = (bf16[352,3072]{1,0:T(8,128)(2,1)}, bf16[352,3072]{1,0:T(8,128)(2,1)}, u32[]{:S(2)}, u32[]{:S(2)}) collective-permute-start(bf16[352,3072]{1,0:T(8,128)(2,1)} %mix.34.piece_ref), channel_id=1, source_target_pairs={{0,2},{2,0},{4,6},{6,4},{1,3},{3,1},{5,7},{7,5}} | collective-permute-start | bytes 6488072 | tf_op jit(solution)/shard_map/ppermute | solution.py:435
  1079.3 50.2 %collective-permute-start.33 = (bf16[1408,768]{1,0:T(8,128)(2,1)}, bf16[1408,768]{1,0:T(8,128)(2,1)}, u32[]{:S(2)}, u32[]{:S(2)}) collective-permute-start(bf16[1408,768]{1,0:T(8,128)(2,1)} %collective-permute-done.32.piece_ref), channel_id=1, source_target_pairs={{0,4},{2,6},{4,0},{6,2},{1,5},{3,7},{5,1},{7,3}} | collective-permute-start | bytes 6488072 | tf_op jit(solution)/shard_map/ppermute | solution.py:436
  1080.8 95.0 %collective-permute-start.31 = (bf16[1408,768]{1,0:T(8,128)(2,1)}, bf16[1408,768]{1,0:T(8,128)(2,1)}, u32[]{:S(2)}, u32[]{:S(2)}) collective-permute-start(bf16[1408,768]{1,0:T(8,128)(2,1)} %collective-permute-done.30.piece_ref), channel_id=1, source_target_pairs={{0,4},{2,6},{4,0},{6,2},{1,5},{3,7},{5,1},{7,3}} | collective-permute-start | bytes 6488072 | tf_op jit(solution)/shard_map/ppermute | solution.py:436
  1081.7 236.9 %collective-permute-start.19 = (bf16[352,3072]{1,0:T(8,128)(2,1)}, bf16[352,3072]{1,0:T(8,128)(2,1)}, u32[]{:S(2)}, u32[]{:S(2)}) collective-permute-start(bf16[352,3072]{1,0:T(8,128)(2,1)} %collective-permute-done.18.piece_ref), channel_id=1, source_target_pairs={{0,2},{2,0},{4,6},{6,4},{1,3},{3,1},{5,7},{7,5}} | collective-permute-start | bytes 6488072 | tf_op jit(solution)/shard_map/ppermute | solution.py:435
  1083.3 240.4 %collective-permute-start.17 = (bf16[352,3072]{1,0:T(8,128)(2,1)}, bf16[352,3072]{1,0:T(8,128)(2,1)}, u32[]{:S(2)}, u32[]{:S(2)}) collective-permute-start(bf16[352,3072]{1,0:T(8,128)(2,1)} %collective-permute-done.16.piece_ref), channel_id=1, source_target_pairs={{0,2},{2,0},{4,6},{6,4},{1,3},{3,1},{5,7},{7,5}} | collective-permute-start | bytes 6488072 | tf_op jit(solution)/shard_map/ppermute | solution.py:435
  1085.1 228.7 %collective-permute-start.27 = (bf16[1408,384]{1,0:T(8,128)(2,1)}, bf16[1408,384]{1,0:T(8,128)(2,1)}, u32[]{:S(2)}, u32[]{:S(2)}) collective-permute-start(bf16[1408,384]{1,0:T(8,128)(2,1)} %collective-permute-done.26.piece_ref), channel_id=1, source_target_pairs={{0,4},{2,6},{4,0},{6,2},{1,5},{3,7},{5,1},{7,3}} | collective-permute-start | bytes 3244040 | tf_op jit(solution)/shard_map/ppermute | solution.py:436
  1129.5 199.4 %collective-permute-start.15 = (bf16[352,1536]{1,0:T(8,128)(2,1)}, bf16[352,1536]{1,0:T(8,128)(2,1)}, u32[]{:S(2)}, u32[]{:S(2)}) collective-permute-start(bf16[352,1536]{1,0:T(8,128)(2,1)} %collective-permute-done.14.piece_ref), channel_id=1, source_target_pairs={{0,2},{2,0},{4,6},{6,4},{1,3},{3,1},{5,7},{7,5}} | collective-permute-start | bytes 3244040 | tf_op jit(solution)/shard_map/ppermute | solution.py:435
  1175.8 156.7 %collective-permute-start.13 = (bf16[352,1536]{1,0:T(8,128)(2,1)}, bf16[352,1536]{1,0:T(8,128)(2,1)}, u32[]{:S(2)}, u32[]{:S(2)}) collective-permute-start(bf16[352,1536]{1,0:T(8,128)(2,1)} %collective-permute-done.12.piece_ref), channel_id=1, source_target_pairs={{0,2},{2,0},{4,6},{6,4},{1,3},{3,1},{5,7},{7,5}} | collective-permute-start | bytes 3244040 | tf_op jit(solution)/shard_map/ppermute | solution.py:435
  (31 other events, 108.7 us)
